TPU v7x, 32 devices: a whole 2x2x4 slice. The times are simulated.
32 devices in a mesh: dp: 4 (over y, x), seq: 8 (over z, core).
Axes of the slice: x: 2, y: 2, z: 4, core: 2. Of those that a mesh axis runs over, the one named last changes fastest.
Arguments:
- inputs: bfloat16 [2, 4, 1024, 768], P(None, 'dp', 'seq'), may hold values from -6 to 6
- row_segment: int32 [2, 4, 1024], P(None, 'dp', 'seq'), may hold values from 0 to 7, as said below
- row_flag: int32 [2, 4, 1024], P(None, 'dp', 'seq'), may hold values from 0 to 1, as said below
- row_block: int32 [2, 4, 1024], P(None, 'dp', 'seq'), may hold values from 0 to 31, as said below
- norm1_scale: float32 [768], P('seq'), may hold values from 0.5 to 1.5
- w_qkv: float32 [768, 2304], P('dp', 'seq'), may hold values from -0.21875 to 0.21875
- w_out: float32 [768, 768], P('dp', 'seq'), may hold values from -1.75 to 1.75
- norm2_scale: float32 [768], P('seq'), may hold values from 0.5 to 1.5
- w_fc1: float32 [768, 3072], P('dp', 'seq'), may hold values from -0.21875 to 0.21875
- b_fc1: float32 [3072], P('seq'), may hold values from -3 to 3
- w_fc2: float32 [3072, 768], P('dp', 'seq'), may hold values from -0.109375 to 0.109375
- b_fc2: float32 [768], P('seq'), may hold values from -3 to 3
- cotangent: bfloat16 [2, 4, 1024, 768], P(None, 'dp', 'seq'), may hold values from -6 to 6
Outputs:
- outputs: bfloat16 [2, 4, 1024, 768], P(None, 'dp', 'seq')
- input_grad: bfloat16 [2, 4, 1024, 768], P(None, 'dp', 'seq')
- norm1_scale_grad: float32 [768], P('seq')
- w_qkv_grad: float32 [768, 2304], P('dp', 'seq')
- w_out_grad: float32 [768, 768], P('dp', 'seq')
- norm2_scale_grad: float32 [768], P('seq')
- w_fc1_grad: float32 [768, 3072], P('dp', 'seq')
- b_fc1_grad: float32 [3072], P('seq')
- w_fc2_grad: float32 [3072, 768], P('dp', 'seq')
- b_fc2_grad: float32 [768], P('seq')
Inputs may be any that keep to these rules, and one draw needn't show every extreme that they name: `row_flag`: in every sequence each aligned group of 16 rows carries one flag and one block number, and each pair of a flag and a block 0 to 31 is carried by exactly one group. `row_block`: constant on each aligned group of 16 rows; see row_flag. `row_segment`: A function of the position 16 * row_block + (row mod 16) alone, the same for the noisy and the clean row of a position, never falling as the position grows; every sequence holds exactly 8 documents, numbered from 0.
All inputs are finite; a program needn't handle non-finite values.
Results may differ from a plain program's by a relative error of at most 0.02.
Values may be sent and summed in bfloat16 or wider, within the bound.
No kernel may reach another device: no remote copies, remote signals or barrier semaphores. Data moves between devices by JAX's collectives and lax.ppermute only.
A program may use at most 192 MiB of HBM per device.

v0:
```python
import functools

import jax
import jax.numpy as jnp
import numpy as np
from jax import lax
from jax.experimental import pallas as pl
from jax.experimental.pallas import tpu as pltpu
from jax.sharding import PartitionSpec as P

D = 768
H = 12
HD = 64
FF = 3072
BLK = 16
F32 = jnp.float32
BF = jnp.bfloat16
NEG = -1e30
VMEM_LIMIT = 56 * 1024 * 1024


def cost(flops, nbytes):
    return pl.CostEstimate(flops=int(flops), bytes_accessed=int(nbytes), transcendentals=0)


def params(*semantics):
    return pltpu.CompilerParams(
        dimension_semantics=semantics or None, vmem_limit_bytes=VMEM_LIMIT
    )


def dot(a, b):
    return lax.dot_general(a, b, (((1,), (0,)), ((), ())), preferred_element_type=F32)


def dot_t(a, b):
    return lax.dot_general(a, b, (((1,), (1,)), ((), ())), preferred_element_type=F32)


def whole(shape):
    return pl.BlockSpec(shape, lambda *_: (0,) * len(shape))


def cuts(count, step):
    return [(at, min(step, count - at)) for at in range(0, count, step)]


def lane_mask(width, head):
    lanes = lax.broadcasted_iota(jnp.int32, (1, width), 1)
    return jnp.where(lanes // HD == head, 1.0, 0.0).astype(BF)


def per_head(block, heads):
    return jnp.concatenate([block * lane_mask(block.shape[1], h) for h in range(heads)], axis=0)


def swap_halves(v):
    out = []
    for at in range(0, v.shape[1], 128):
        part = v[:, at : at + 128]
        lanes = lax.broadcasted_iota(jnp.int32, part.shape, 1)
        out.append(
            jnp.where(
                lanes % HD < HD // 2,
                pltpu.roll(part, 128 - HD // 2, 1),
                pltpu.roll(part, HD // 2, 1),
            )
        )
    return jnp.concatenate(out, axis=1)


def widen(table, width):
    return jnp.concatenate([table] * (width // 128), axis=1)


def cos_sin(angle):
    turns = jnp.round(angle * np.float32(2.0 / np.pi))
    left = angle - turns * np.float32(1.5703125)
    left = left - turns * np.float32(4.837512969970703125e-4)
    left = left - turns * np.float32(7.54978995489188e-8)
    sq = left * left
    sine = left + left * sq * (
        np.float32(-1.6666654611e-1)
        + sq * (np.float32(8.3321608736e-3) + sq * np.float32(-1.9515295891e-4))
    )
    cosine = (
        1.0
        - 0.5 * sq
        + sq
        * sq
        * (
            np.float32(4.166664568298827e-2)
            + sq * (np.float32(-1.388731625493765e-3) + sq * np.float32(2.443315711809948e-5))
        )
    )
    quarter = jnp.bitwise_and(turns.astype(jnp.int32), 3)
    odd = jnp.bitwise_and(quarter, 1) == 1
    sin_out = jnp.where(odd, cosine, sine)
    cos_out = jnp.where(odd, sine, cosine)
    sin_out = jnp.where(quarter >= 2, -sin_out, sin_out)
    cos_out = jnp.where((quarter == 1) | (quarter == 2), -cos_out, cos_out)
    return cos_out, sin_out


def normed(v):
    centered = v - jnp.mean(v, axis=1, keepdims=True)
    var = jnp.mean(centered * centered, axis=1, keepdims=True)
    rstd = lax.rsqrt(var + 1e-05)
    return centered * rstd, rstd


def fold8(v, op):
    return op(v.reshape(v.shape[0] // 8, 8, v.shape[1]), axis=0)


def pair_mask(kcol_ref, rows, codes):
    key = kcol_ref[rows, 0:1]
    low, high, same = codes
    return ((key >= low) & (key < high)) | (key == same)


def query_codes(qrow_ref, at, count):
    cols = pl.ds(at, count)
    return qrow_ref[0:1, cols], qrow_ref[1:2, cols], qrow_ref[2:3, cols]


SUB = 64


def chosen(step, entries):
    value = jnp.int32(entries[0])
    for i, e in enumerate(entries[1:], 1):
        value = jnp.where(step == i, jnp.int32(e), value)
    return value


def attend(step, entries, q_ref, k_ref, vt_ref, kcol_ref, qrow_ref, s_scr, p_scr, heads, chunk):
    blocks = k_ref.shape[0] // chunk
    lq = k_ref.shape[1]
    at = pl.multiple_of(chosen(step, entries) * chunk, chunk)
    codes = query_codes(qrow_ref, at, chunk)
    query = per_head(q_ref[pl.ds(at, chunk), :], heads)

    def score(block, best):
        base = pl.multiple_of(block * chunk, chunk)
        s_scr[pl.ds(base, chunk), :] = dot_t(k_ref[pl.ds(base, chunk), :], query)
        best = list(best)
        for sub in range(0, chunk, SUB):
            rows = pl.ds(base + sub, SUB)
            mask = pair_mask(kcol_ref, rows, codes)
            for h in range(heads):
                cols = slice(h * chunk, (h + 1) * chunk)
                value = jnp.where(mask, s_scr[rows, cols], NEG)
                s_scr[rows, cols] = value
                best[h] = jnp.maximum(best[h], fold8(value, jnp.max))
        return tuple(best)

    best = lax.fori_loop(
        0, blocks, score, tuple(jnp.full((8, chunk), NEG, F32) for _ in range(heads))
    )
    best = [jnp.max(b, axis=0, keepdims=True) for b in best]

    def soften(block, sums):
        base = pl.multiple_of(block * chunk, chunk)
        sums = list(sums)
        for sub in range(0, chunk, SUB):
            rows = pl.ds(base + sub, SUB)
            for h in range(heads):
                cols = slice(h * chunk, (h + 1) * chunk)
                value = jnp.exp(s_scr[rows, cols] - best[h])
                sums[h] = sums[h] + fold8(value, jnp.sum)
                p_scr[rows, cols] = value.astype(BF)
        return tuple(sums)

    sums = lax.fori_loop(
        0, blocks, soften, tuple(jnp.zeros((8, chunk), F32) for _ in range(heads))
    )
    sums = [jnp.sum(s, axis=0, keepdims=True) for s in sums]
    tops = []
    for h in range(heads):
        made = dot(vt_ref[...], p_scr[:, h * chunk : (h + 1) * chunk])
        tops.append(made[h * HD : (h + 1) * HD, :] * (1.0 / sums[h]))
    if heads * HD < lq:
        tops.append(jnp.zeros((lq - heads * HD, chunk), F32))
    logs = [best[h] + jnp.log(sums[h]) for h in range(heads)]
    logs.append(jnp.zeros((8 - heads, chunk), F32))
    return jnp.concatenate(tops, axis=0), jnp.concatenate(logs, axis=0)


def block_outputs(entries, lq, hw, chunk):
    shapes = []
    for _ in entries:
        shapes += [
            jax.ShapeDtypeStruct((chunk, hw), BF),
            jax.ShapeDtypeStruct((lq, chunk), F32),
            jax.ShapeDtypeStruct((8, chunk), F32),
        ]
    return shapes


def store_block(step, entries, refs, joined, logs, hw):
    attended = joined.T[:, :hw].astype(BF)
    for i in range(len(entries)):

        @pl.when(step == i)
        def _(i=i):
            refs[3 * i][...] = attended
            refs[3 * i + 1][...] = joined
            refs[3 * i + 2][...] = logs


def by_block(entries, made):
    return {e: tuple(made[3 * i : 3 * i + 3]) for i, e in enumerate(entries)}


def attention_first(arrays, plan, kcol, qrow, freq, wq, gain, heads, chunk, entries):
    total = kcol.shape[0]
    blocks = total // chunk
    lq = wq.shape[1] // 3
    hw = heads * HD
    count = len(arrays)

    def kernel(*refs):
        x_refs = refs[:count]
        kcol_ref, qrow_ref, freq_ref, wq_ref, gain_ref = refs[count : count + 5]
        h1_ref, q_ref, k_ref, v_ref, vt_ref, cs_ref, sn_ref = refs[count + 5 : count + 12]
        block_refs = refs[count + 12 : count + 12 + 3 * len(entries)]
        s_scr, p_scr = refs[count + 12 + 3 * len(entries) :]
        step = pl.program_id(0)

        @pl.when(step == 0)
        def _():
            gain_row = gain_ref[...]
            for which, src, dst, rows in plan:
                for at, size in cuts(rows, 64):
                    xhat, _ = normed(x_refs[which][src + at : src + at + size, :].astype(F32))
                    h1_ref[dst + at : dst + at + size, :] = (xhat * gain_row).astype(BF)
            lanes = lax.broadcasted_iota(jnp.int32, (1, 128), 1)
            sign = jnp.where(lanes % HD < HD // 2, -1.0, 1.0)

            def project(block, carry):
                rows = pl.ds(pl.multiple_of(block * chunk, chunk), chunk)
                cosine, sine = cos_sin(kcol_ref[rows, 1:2] * freq_ref[...])
                sine = sine * sign
                cs_ref[rows, :] = cosine
                sn_ref[rows, :] = sine
                cosine = widen(cosine, lq)
                sine = widen(sine, lq)
                made = dot(h1_ref[rows, :], wq_ref[...])
                q = made[:, :lq]
                q_ref[rows, :] = ((q * cosine + swap_halves(q) * sine).astype(BF) * 0.125).astype(
                    BF
                )
                k = made[:, lq : 2 * lq]
                k_ref[rows, :] = (k * cosine + swap_halves(k) * sine).astype(BF)
                v = made[:, 2 * lq :]
                v_ref[rows, :] = v.astype(BF)
                vt_ref[:, rows] = v.T.astype(BF)
                return carry

            lax.fori_loop(0, blocks, project, 0)

        joined, logs = attend(
            step, entries, q_ref, k_ref, vt_ref, kcol_ref, qrow_ref, s_scr, p_scr, heads, chunk
        )
        store_block(step, entries, block_refs, joined, logs, hw)

    ins = list(arrays) + [kcol, qrow, freq, wq, gain]
    out_shape = [
        jax.ShapeDtypeStruct((total, D), BF),
        jax.ShapeDtypeStruct((total, lq), BF),
        jax.ShapeDtypeStruct((total, lq), BF),
        jax.ShapeDtypeStruct((total, lq), BF),
        jax.ShapeDtypeStruct((lq, total), BF),
        jax.ShapeDtypeStruct((total, 128), F32),
        jax.ShapeDtypeStruct((total, 128), F32),
    ] + block_outputs(entries, lq, hw, chunk)
    made = pl.pallas_call(
        kernel,
        name="attention_first",
        grid=(len(entries),),
        in_specs=[whole(v.shape) for v in ins],
        out_specs=[whole(o.shape) for o in out_shape],
        out_shape=out_shape,
        scratch_shapes=[
            pltpu.VMEM((total, heads * chunk), F32),
            pltpu.VMEM((total, heads * chunk), BF),
        ],
        compiler_params=params("arbitrary"),
        cost_estimate=cost(8e9, 8e6),
    )(*ins)
    return made[:7], by_block(entries, made[7:])


def attention_rest(saved, kcol, qrow, heads, chunk, entries):
    _, q, k, _, vt, _, _ = saved
    total, lq = k.shape
    hw = heads * HD

    def kernel(q_ref, k_ref, vt_ref, kcol_ref, qrow_ref, *refs):
        step = pl.program_id(0)
        s_scr, p_scr = refs[3 * len(entries) :]
        joined, logs = attend(
            step, entries, q_ref, k_ref, vt_ref, kcol_ref, qrow_ref, s_scr, p_scr, heads, chunk
        )
        store_block(step, entries, refs, joined, logs, hw)

    ins = [q, k, vt, kcol, qrow]
    out_shape = block_outputs(entries, lq, hw, chunk)
    made = pl.pallas_call(
        kernel,
        name="attention_rest",
        grid=(len(entries),),
        in_specs=[whole(v.shape) for v in ins],
        out_specs=[whole(o.shape) for o in out_shape],
        out_shape=out_shape,
        scratch_shapes=[
            pltpu.VMEM((total, heads * chunk), F32),
            pltpu.VMEM((total, heads * chunk), BF),
        ],
        compiler_params=params("arbitrary"),
        cost_estimate=cost(5e9, 4e6),
    )(*ins)
    return by_block(entries, made)


def attention_backward(pulls, by, saved, kcol, qrow, wq, heads, chunk, entries, before, last):
    h1, q, k, v, _, cs, sn = saved
    total, lq = k.shape
    blocks = total // chunk
    hw = heads * HD
    n = len(entries)

    def kernel(*refs):
        g_refs, att_refs, lse_refs = refs[:n], refs[n : 2 * n], refs[2 * n : 3 * n]
        q_ref, k_ref, v_ref, cs_ref, sn_ref, kcol_ref, qrow_ref = refs[3 * n : 3 * n + 7]
        refs = refs[3 * n + 7 :]
        if last:
            dq_in, dk_in, dv_in, wq_ref, h1_ref = refs[:5]
            gqkv_ref, n1_ref = refs[5:7]
            gh_refs = refs[7 : 7 + blocks]
            scr = refs[7 + blocks :]
        else:
            dq_out, dk_out, dv_out = refs[:3]
            scr = refs[3:]
        g_scr, row_scr, kt_scr, dk_scr, dv_scr, s_scr, dp_scr, pb_scr, ds_scr, dst_scr = scr
        step = pl.program_id(0)

        @pl.when(step == 0)
        def _():
            for i in range(n):
                g_scr[i, :, :hw] = g_refs[i][...]
                if hw < lq:
                    g_scr[i, :, hw:] = jnp.zeros((chunk, lq - hw), BF)
                product = g_scr[i].astype(F32).T * att_refs[i][...]
                for h in range(heads):
                    row_scr[i, h : h + 1, :] = jnp.sum(
                        product[h * HD : (h + 1) * HD, :], axis=0, keepdims=True
                    )
                row_scr[i, 8:16, :] = lse_refs[i][...]
            if last:
                dk_scr[...] = dk_in[...]
                dv_scr[...] = dv_in[...]
            else:
                dk_scr[...] = jnp.zeros_like(dk_scr)
                dv_scr[...] = jnp.zeros_like(dv_scr)

            def turn(block, carry):
                rows = pl.ds(pl.multiple_of(block * chunk, chunk), chunk)
                flat = k_ref[rows, :].astype(F32).T
                line = lax.broadcasted_iota(jnp.int32, (lq, 1), 0) // HD
                for h in range(heads):
                    kt_scr[block, :, h * chunk : (h + 1) * chunk] = jnp.where(
                        line == h, flat, 0.0
                    ).astype(BF)
                return carry

            lax.fori_loop(0, blocks, turn, 0)

        at = pl.multiple_of(chosen(step, entries) * chunk, chunk)
        own = pl.ds(at, chunk)
        codes = query_codes(qrow_ref, at, chunk)
        query = per_head(q_ref[own, :], heads)
        pull = per_head(g_scr[step], heads)
        delta = [row_scr[step, h : h + 1, :] for h in range(heads)]
        top = [row_scr[step, 8 + h : 9 + h, :] for h in range(heads)]

        def keys(block, dq_t):
            base = pl.multiple_of(block * chunk, chunk)
            rows = pl.ds(base, chunk)
            s_scr[...] = dot_t(k_ref[rows, :], query)
            dp_scr[...] = dot_t(v_ref[rows, :], pull)
            for sub in range(0, chunk, SUB):
                part = slice(sub, sub + SUB)
                mask = pair_mask(kcol_ref, pl.ds(base + sub, SUB), codes)
                for h in range(heads):
                    cols = slice(h * chunk, (h + 1) * chunk)
                    prob = jnp.exp(jnp.where(mask, s_scr[part, cols] - top[h], NEG))
                    slope = (prob * (dp_scr[part, cols] - delta[h])).astype(BF)
                    pb_scr[part, cols] = prob.astype(BF)
                    ds_scr[part, cols] = slope
                    dst_scr[h * chunk + sub : h * chunk + sub + SUB, :] = slope
            dv_scr[rows, :] += dot(pb_scr[...], pull)
            dk_scr[rows, :] += dot(ds_scr[...], query)
            return dq_t + dot(kt_scr[block], dst_scr[...])

        dq_t = lax.fori_loop(0, blocks, keys, jnp.zeros((lq, chunk), F32))

        def unrotate(value, rows):
            return value * widen(cs_ref[rows, :], lq) - swap_halves(value) * widen(
                sn_ref[rows, :], lq
            )

        dq = unrotate(dq_t.T * 0.125, own).astype(BF)
        if not last:
            dq_out[...] = dq

            @pl.when(step == n - 1)
            def _():
                dk_out[...] = dk_scr[...]
                dv_out[...] = dv_scr[...]

        else:
            gqkv_ref[own, :lq] = dq

            @pl.when(step == n - 1)
            def _():
                gqkv_ref[0:chunk, :lq] = dq_in[...]
                n1 = jnp.zeros((8, D), F32)
                for b in range(blocks):
                    rows = slice(b * chunk, (b + 1) * chunk)
                    gqkv_ref[rows, lq : 2 * lq] = unrotate(dk_scr[rows, :], rows).astype(BF)
                    gqkv_ref[rows, 2 * lq :] = dv_scr[rows, :].astype(BF)
                    gh = dot_t(gqkv_ref[rows, :], wq_ref[...])
                    gh_refs[b][...] = gh.astype(gh_refs[b].dtype)
                    n1 = n1 + fold8(gh * h1_ref[rows, :].astype(F32), jnp.sum)
                n1_ref[...] = n1

    ins = [pulls[e] for e in entries] + [by[e][1] for e in entries] + [by[e][2] for e in entries]
    ins += [q, k, v, cs, sn, kcol, qrow]
    if last:
        ins += list(before) + [wq, h1]
        out_shape = [
            jax.ShapeDtypeStruct((total, 3 * lq), BF),
            jax.ShapeDtypeStruct((8, D), F32),
        ]
        for b in range(blocks):
            out_shape.append(jax.ShapeDtypeStruct((chunk, D), F32 if b == 0 else BF))
    else:
        out_shape = [
            jax.ShapeDtypeStruct((chunk, lq), BF),
            jax.ShapeDtypeStruct((total, lq), F32),
            jax.ShapeDtypeStruct((total, lq), F32),
        ]
    return pl.pallas_call(
        kernel,
        name="attention_backward_last" if last else "attention_backward_own",
        grid=(n,),
        in_specs=[whole(a.shape) for a in ins],
        out_specs=[whole(o.shape) for o in out_shape],
        out_shape=out_shape,
        scratch_shapes=[
            pltpu.VMEM((n, chunk, lq), BF),
            pltpu.VMEM((n, 16, chunk), F32),
            pltpu.VMEM((blocks, lq, heads * chunk), BF),
            pltpu.VMEM((total, lq), F32),
            pltpu.VMEM((total, lq), F32),
            pltpu.VMEM((chunk, heads * chunk), F32),
            pltpu.VMEM((chunk, heads * chunk), F32),
            pltpu.VMEM((chunk, heads * chunk), BF),
            pltpu.VMEM((chunk, heads * chunk), BF),
            pltpu.VMEM((heads * chunk, chunk), BF),
        ],
        compiler_params=params("arbitrary"),
        cost_estimate=cost(3e9 * n, 1e7),
    )(*ins)


def dot_first(a, b):
    return lax.dot_general(a, b, (((0,), (0,)), ((), ())), preferred_element_type=F32)


def reorder_columns(place, own, other, order):
    width = own.shape[2]
    out = order.shape[0]

    def kernel(place_ref, own_ref, other_ref, order_ref, out_ref, scr):
        d = place_ref[0]
        scr[...] = jnp.zeros_like(scr)
        for j in range(4):
            scr[192 * j : 192 * j + 192, :width] = own_ref[d ^ j]
            scr[192 * j : 192 * j + 192, 384 : 384 + width] = other_ref[d ^ j]
        out_ref[...] = dot_t(scr[...], order_ref[...]).astype(BF)

    return pl.pallas_call(
        kernel,
        name="reorder_columns",
        grid_spec=pltpu.PrefetchScalarGridSpec(
            num_scalar_prefetch=1,
            grid=(1,),
            in_specs=[whole(own.shape), whole(other.shape), whole(order.shape)],
            out_specs=whole((D, out)),
            scratch_shapes=[pltpu.VMEM((D, 768), BF)],
        ),
        out_shape=jax.ShapeDtypeStruct((D, out), BF),
        compiler_params=params("arbitrary"),
        cost_estimate=cost(1e9, 3e6),
    )(place, own, other, order)


def reorder_out(place, own, other, order):
    def kernel(place_ref, own_ref, other_ref, order_ref, out_ref, scr):
        d = place_ref[0]
        for j in range(4):
            for k in range(4):
                at = 96 * k
                part = slice(96 * j, 96 * j + 96)
                scr[j, :, at : at + 96] = own_ref[k, :, part]
                scr[j, :, 384 + at : 384 + at + 96] = other_ref[k, :, part]
        for j in range(4):
            out_ref[j] = dot_t(scr[d ^ j], order_ref[...]).astype(BF)

    return pl.pallas_call(
        kernel,
        name="reorder_out",
        grid_spec=pltpu.PrefetchScalarGridSpec(
            num_scalar_prefetch=1,
            grid=(1,),
            in_specs=[whole(own.shape), whole(other.shape), whole(order.shape)],
            out_specs=whole((4, 192, D)),
            scratch_shapes=[pltpu.VMEM((4, 192, 768), BF)],
        ),
        out_shape=jax.ShapeDtypeStruct((4, 192, D), BF),
        compiler_params=params("arbitrary"),
        cost_estimate=cost(1e9, 3e6),
    )(place, own, other, order)


def qkv_weight(place, h1, gqkv, order):
    def kernel(place_ref, h_ref, g_ref, order_ref, keep_ref, send_ref):
        d = place_ref[0]
        made = dot_first(h_ref[...], g_ref[...]).astype(BF)
        made = dot(made, order_ref[...]).astype(BF)
        for j in range(4):
            rows = slice(192 * j, 192 * j + 192)
            keep_ref[d ^ j] = made[rows, :288]
            send_ref[d ^ j] = made[rows, 384:672]

    shape = jax.ShapeDtypeStruct((4, 192, 288), BF)
    return pl.pallas_call(
        kernel,
        name="qkv_weight",
        grid_spec=pltpu.PrefetchScalarGridSpec(
            num_scalar_prefetch=1,
            grid=(1,),
            in_specs=[whole(h1.shape), whole(gqkv.shape), whole(order.shape)],
            out_specs=[whole(shape.shape)] * 2,
        ),
        out_shape=[shape, shape],
        compiler_params=params("arbitrary"),
        cost_estimate=cost(2e9, 5e6),
    )(place, h1, gqkv, order)


def out_weight(place, mixed, gproj, order):
    groups = len(mixed)

    def kernel(place_ref, *refs):
        m_refs = refs[:groups]
        g_ref, order_ref, keep_ref, send_ref = refs[groups:]
        d, z = place_ref[0], place_ref[1]
        for k in range(groups):
            made = dot_first(m_refs[k][...], g_ref[...]).astype(BF)
            made = dot(made, order_ref[...]).astype(BF)
            row = d ^ lax.rem(z + (groups - k), groups)
            keep_ref[row] = made[:, :384]
            send_ref[row] = made[:, 384:]

    ins = list(mixed) + [gproj, order]
    shape = jax.ShapeDtypeStruct((4, 192, 384), BF)
    return pl.pallas_call(
        kernel,
        name="out_weight",
        grid_spec=pltpu.PrefetchScalarGridSpec(
            num_scalar_prefetch=1,
            grid=(1,),
            in_specs=[whole(a.shape) for a in ins],
            out_specs=[whole(shape.shape)] * 2,
        ),
        out_shape=[shape, shape],
        compiler_params=params("arbitrary"),
        cost_estimate=cost(1e9, 4e6),
    )(place, *ins)


def output_projection(place, mixed, wout, x, gain):
    groups = len(mixed)
    rows = x.shape[0]

    def kernel(place_ref, *refs):
        m_refs = refs[:groups]
        w_ref, x_ref, gain_ref, res_ref, h2_ref = refs[groups:]
        z = place_ref[1]
        total = x_ref[...].astype(F32)
        for k in range(groups):
            total = total + dot(m_refs[k][...], w_ref[lax.rem(z + (groups - k), groups)])
        res_ref[...] = total
        for at, size in cuts(rows, 64):
            xhat, _ = normed(res_ref[at : at + size, :])
            h2_ref[at : at + size, :] = (xhat * gain_ref[...]).astype(BF)

    ins = list(mixed) + [wout, x, gain]
    return pl.pallas_call(
        kernel,
        name="output_projection",
        grid_spec=pltpu.PrefetchScalarGridSpec(
            num_scalar_prefetch=1,
            grid=(1,),
            in_specs=[whole(a.shape) for a in ins],
            out_specs=[whole((rows, D)), whole((rows, D))],
        ),
        out_shape=[jax.ShapeDtypeStruct((rows, D), F32), jax.ShapeDtypeStruct((rows, D), BF)],
        compiler_params=params("arbitrary"),
        cost_estimate=cost(1e9, 3e6),
    )(place, *ins)


def feed_forward(place, h2_own, h2_other, dy_own, dy_other, weights, bias):
    rows = h2_own.shape[0]
    both = 2 * rows
    width = 384

    def kernel(
        place_ref, ho_ref, hp_ref, go_ref, gp_ref, w1a_ref, w1b_ref, w2a_ref, w2b_ref, b_ref,
        out_own, out_other, gh_own, gh_other, d1a_ref, d1b_ref, d2a_ref, d2b_ref, db_ref,
        h_scr, g_scr, ht_scr, gt_scr, w1_scr, w2_scr, pre_scr, ga_scr, act_scr, slope_scr, out_scr,
        gh_scr, dw_scr,
    ):
        step = pl.program_id(0)
        d = place_ref[0]
        z = place_ref[1]

        @pl.when(step == 0)
        def _():
            h_scr[:rows, :] = ho_ref[...]
            h_scr[rows:, :] = hp_ref[...]
            g_scr[:rows, :] = go_ref[...]
            g_scr[rows:, :] = gp_ref[...]
            for at in range(0, both, 256):
                part = slice(at, at + 256)
                ht_scr[:, part] = h_scr[part, :].astype(F32).T.astype(BF)
                gt_scr[:, part] = g_scr[part, :].astype(F32).T.astype(BF)

        near = lax.rem(step - z + 4, 4)
        hidden = step ^ d
        for odd in range(2):

            @pl.when(d % 2 == odd)
            def _(odd=odd):
                for j in range(4):
                    src = (w1a_ref, w1b_ref)[odd ^ (j % 2)]
                    w1_scr[192 * j : 192 * j + 192, :] = src[(d ^ j) // 2, near]

            @pl.when(hidden // 2 == odd)
            def _(odd=odd):
                for j in range(4):
                    src = (w2a_ref, w2b_ref)[odd]
                    w2_scr[192 * j : 192 * j + 192, :] = src[hidden % 2, lax.rem(j - z + 4, 4)]

        pre_scr[...] = dot(h_scr[...], w1_scr[...])
        ga_scr[...] = dot(g_scr[...], w2_scr[...])
        bias_row = b_ref[0].astype(F32)
        total = jnp.zeros((8, width), F32)
        for at in range(0, both, 32):
            part = slice(at, at + 32)
            u = pre_scr[part, :] + bias_row
            usq = u * u
            c = np.float32(np.sqrt(2.0 / np.pi))
            t = jnp.tanh(c * (u + np.float32(0.044715) * (usq * u)))
            half = 0.5 * (1.0 + t)
            act_scr[part, :] = (u * half).astype(BF)
            rise = half + 0.5 * u * (1.0 - t * t) * (c * (1.0 + np.float32(0.134145) * usq))
            slope = (ga_scr[part, :] * rise).astype(BF)
            slope_scr[part, :] = slope
            total = total + fold8(slope.astype(F32), jnp.sum)
        db_ref[0] = total

        out_now = dot_t(act_scr[...], w2_scr[...])
        gh_now = dot_t(slope_scr[...], w1_scr[...])

        @pl.when(step == 0)
        def _():
            out_scr[...] = out_now
            gh_scr[...] = gh_now

        @pl.when(step > 0)
        def _():
            out_scr[...] += out_now
            gh_scr[...] += gh_now

        dw_scr[0] = dot(ht_scr[...], slope_scr[...]).astype(BF)
        dw_scr[1] = dot(gt_scr[...], act_scr[...]).astype(BF)
        for odd in range(2):

            @pl.when(d % 2 == odd)
            def _(odd=odd):
                for j in range(4):
                    dst = (d1a_ref, d1b_ref)[odd ^ (j % 2)]
                    dst[(d ^ j) // 2, near] = dw_scr[0, 192 * j : 192 * j + 192, :]

            @pl.when(hidden // 2 == odd)
            def _(odd=odd):
                for j in range(4):
                    dst = (d2a_ref, d2b_ref)[odd]
                    dst[hidden % 2, lax.rem(j - z + 4, 4)] = dw_scr[1, 192 * j : 192 * j + 192, :]

        @pl.when(step == 3)
        def _():
            out_own[...] = out_scr[:rows, :]
            out_other[...] = out_scr[rows:, :].astype(BF)
            gh_own[...] = gh_scr[:rows, :]
            gh_other[...] = gh_scr[rows:, :].astype(BF)

    def by_z(i, place_ref):
        return (lax.rem(i - place_ref[1] + 4, 4), 0, 0)

    ins = [h2_own, h2_other, dy_own, dy_other] + list(weights)
    full = jax.ShapeDtypeStruct((2, 4, 192, width), BF)
    out_shape = [
        jax.ShapeDtypeStruct((rows, D), F32),
        jax.ShapeDtypeStruct((rows, D), BF),
        jax.ShapeDtypeStruct((rows, D), F32),
        jax.ShapeDtypeStruct((rows, D), BF),
        full,
        full,
        full,
        full,
        jax.ShapeDtypeStruct((4, 8, width), F32),
    ]
    return pl.pallas_call(
        kernel,
        name="feed_forward",
        grid_spec=pltpu.PrefetchScalarGridSpec(
            num_scalar_prefetch=1,
            grid=(4,),
            in_specs=[whole(a.shape) for a in ins] + [pl.BlockSpec((1, 1, width), by_z)],
            out_specs=[whole(o.shape) for o in out_shape[:-1]]
            + [pl.BlockSpec((1, 8, width), by_z)],
            scratch_shapes=[
                pltpu.VMEM((both, D), BF),
                pltpu.VMEM((both, D), BF),
                pltpu.VMEM((D, both), BF),
                pltpu.VMEM((D, both), BF),
                pltpu.VMEM((D, width), BF),
                pltpu.VMEM((D, width), BF),
                pltpu.VMEM((both, width), F32),
                pltpu.VMEM((both, width), F32),
                pltpu.VMEM((both, width), BF),
                pltpu.VMEM((both, width), BF),
                pltpu.VMEM((both, D), F32),
                pltpu.VMEM((both, D), F32),
                pltpu.VMEM((2, D, width), BF),
            ],
        ),
        out_shape=out_shape,
        compiler_params=params("arbitrary"),
        cost_estimate=cost(7.2e9, 1.5e7),
    )(place, *ins, bias)


def residual_backward(place, gh_own, gh_in, residual, dy, gain, wout):
    rows = dy.shape[0]
    groups, hw = wout.shape[0], wout.shape[1]

    def kernel(place_ref, gh_ref, gi_ref, res_ref, dy_ref, gain_ref, w_ref, *outs):
        gres_ref, gproj_ref, vec_ref = outs[:3]
        gm_refs = outs[3:]
        z = place_ref[1]
        gain_row = gain_ref[...]
        gsum = jnp.zeros((8, D), F32)
        bsum = jnp.zeros((8, D), F32)
        for at, size in cuts(rows, 32):
            part = slice(at, at + size)
            xhat, rstd = normed(res_ref[part, :])
            dy_now = dy_ref[part, :].astype(F32)
            grad = gh_ref[part, :] + gi_ref[part, :].astype(F32)
            along = grad * xhat
            gsum = gsum + fold8(along, jnp.sum)
            bsum = bsum + fold8(dy_now, jnp.sum)
            u = grad * gain_row
            back = (
                u
                - jnp.mean(u, axis=1, keepdims=True)
                - xhat * jnp.mean(along * gain_row, axis=1, keepdims=True)
            )
            value = dy_now + back * rstd
            gres_ref[part, :] = value
            gproj_ref[part, :] = value.astype(BF)
        vec_ref[0:8, :] = gsum
        vec_ref[8:16, :] = bsum
        for k in range(groups):
            gm_refs[k][...] = dot_t(gproj_ref[...], w_ref[lax.rem(z + k, groups)]).astype(BF)

    ins = [gh_own, gh_in, residual, dy, gain, wout]
    out_shape = [
        jax.ShapeDtypeStruct((rows, D), F32),
        jax.ShapeDtypeStruct((rows, D), BF),
        jax.ShapeDtypeStruct((16, D), F32),
    ] + [jax.ShapeDtypeStruct((rows, hw), BF) for _ in range(groups)]
    made = pl.pallas_call(
        kernel,
        name="residual_backward",
        grid_spec=pltpu.PrefetchScalarGridSpec(
            num_scalar_prefetch=1,
            grid=(1,),
            in_specs=[whole(a.shape) for a in ins],
            out_specs=[whole(o.shape) for o in out_shape],
        ),
        out_shape=out_shape,
        compiler_params=params("arbitrary"),
        cost_estimate=cost(1e9, 4e6),
    )(place, *ins)
    return made[0], made[1], made[2], made[3:]


def input_backward(terms, x, gain, gres):
    rows = x.shape[0]
    count = len(terms)

    def kernel(*refs):
        x_ref, gain_ref, gres_ref, out_ref = refs[count:]
        for at, size in cuts(rows, 32):
            part = slice(at, at + size)
            grad = refs[0][part, :].astype(F32)
            for t in range(1, count):
                grad = grad + refs[t][part, :].astype(F32)
            xhat, rstd = normed(x_ref[part, :].astype(F32))
            u = grad * gain_ref[...]
            back = (
                u
                - jnp.mean(u, axis=1, keepdims=True)
                - xhat * jnp.mean(u * xhat, axis=1, keepdims=True)
            )
            out_ref[part, :] = (gres_ref[part, :] + back * rstd).astype(BF)

    ins = list(terms) + [x, gain, gres]
    return pl.pallas_call(
        kernel,
        name="input_backward",
        grid=(1,),
        in_specs=[whole(a.shape) for a in ins],
        out_specs=whole((rows, D)),
        out_shape=jax.ShapeDtypeStruct((rows, D), BF),
        compiler_params=params("arbitrary"),
        cost_estimate=cost(1e8, 3e6),
    )(*ins)


def add_low(a, b):
    return (a.astype(F32) + b.astype(F32)).astype(BF)


def pick(v, index):
    return lax.dynamic_index_in_dim(v, index, 0, keepdims=False)


def after(v, *others):
    return lax.optimization_barrier((v, others))[0]


class Links:
    def __init__(self, n_dp, n_seq):
        self.n_dp, self.n_seq, self.nz = n_dp, n_seq, n_seq // 2

    def core(self, v):
        return lax.ppermute(v, "seq", [(s, s ^ 1) for s in range(self.n_seq)])

    def flip(self, v, bit):
        return lax.ppermute(v, "dp", [(i, i ^ bit) for i in range(self.n_dp)])

    def shift(self, v, k):
        n = self.nz
        return lax.ppermute(
            v, "seq", [(s, 2 * ((s // 2 + k) % n) + s % 2) for s in range(self.n_seq)]
        )


def order_matrix(source, valid):
    rows = lax.broadcasted_iota(jnp.int32, (768, 768), 0)
    return jnp.where((rows == source[None, :]) & valid[None, :], 1.0, 0.0).astype(BF)


def per_device(
    n_dp,
    n_seq,
    inputs,
    row_segment,
    row_flag,
    row_block,
    norm1_scale,
    w_qkv,
    w_out,
    norm2_scale,
    w_fc1,
    b_fc1,
    w_fc2,
    b_fc2,
    cotangent,
):
    links = Links(n_dp, n_seq)
    nz = links.nz
    local = inputs.shape[2]
    chunk = 2 * local
    heads = -(-H // nz)
    hw = heads * HD
    lq = -(-hw // 128) * 128
    fast = n_dp == 4 and nz == 4 and H % nz == 0
    d = lax.axis_index("dp")
    s = lax.axis_index("seq")
    z = s // 2
    c = s % 2
    place = jnp.stack([d, z]).astype(jnp.int32)
    n1_w = D // n_seq
    b1_w = FF // n_seq

    x_loc = inputs[:, 0]
    x_keep = pick(x_loc, c)
    labels = jnp.stack([row_segment[:, 0], row_flag[:, 0], row_block[:, 0]], axis=1)
    labels = labels.astype(BF).reshape(2, 3 * local)
    vector = jnp.concatenate([norm1_scale, norm2_scale, b_fc2, b_fc1]).astype(BF)
    vector = jnp.pad(vector, (0, D - vector.shape[0]))
    lab_keep, lab_send = pick(labels, c), pick(labels, 1 - c)
    extra = jnp.stack([jnp.pad(lab_send, (0, D - 3 * local)), vector])
    message = jnp.concatenate([pick(x_loc, 1 - c), jnp.pad(extra, ((0, 14), (0, 0)))], axis=0)
    swapped = links.core(message)
    extra = jnp.stack(
        [
            jnp.concatenate([lab_keep, swapped[local, : 3 * local]]),
            vector,
            swapped[local + 1],
        ]
    )
    x_ext = jnp.concatenate(
        [x_keep, swapped[:local], jnp.pad(extra, ((0, 13), (0, 0)))], axis=0
    )

    def to_both(w):
        return jnp.where(c == 0, w[0], w[1]), jnp.where(c == 0, w[1], w[0])

    cot = cotangent[:, 0]
    if fast:
        two = w_fc2.astype(BF).T.reshape(96, 2, 384)
        two_keep, two_send = to_both((two[:, 0], two[:, 1]))
        both = jnp.concatenate([cot.reshape(chunk, D), jnp.pad(two_send, ((0, 0), (0, 384)))])
    else:
        both = cot.reshape(chunk, D)
    both_in = links.core(both)
    cot_in = both_in[:chunk].reshape(2, local, D)
    dy_own = jnp.concatenate([pick(cot, c), pick(cot_in, c)], axis=0)
    dy_other = jnp.concatenate([pick(cot_in, 1 - c), pick(cot, 1 - c)], axis=0)

    if nz == 4:
        x_before = links.shift(x_ext, 1)
        x_after = links.shift(x_ext, -1)
        x_low = links.shift(x_before[:144], 1)
        x_high = links.shift(x_after[144:], -1)
        gathered = [[x_ext], [x_after], [x_low, x_high], [x_before]]
        settled = (x_low, x_high)
    else:
        gathered = [[x_ext]] + [[links.shift(x_ext, -k)] for k in range(1, nz)]
        settled = (x_ext,)
    arrays, plan, extras = [], [], []
    for k, pieces in enumerate(gathered):
        at = 0
        for piece in pieces:
            rows = min(piece.shape[0], chunk - at)
            plan.append((len(arrays), 0, k * chunk + at, rows))
            at += rows
            arrays.append(piece)
        extras.append(pieces[-1][-16:])
    extras = jnp.stack(extras)
    labels_all = extras[:, 0].astype(F32).reshape(nz, 2, 3, local)
    segment = labels_all[:, :, 0].reshape(-1)
    flag = labels_all[:, :, 1].reshape(-1)
    block = labels_all[:, :, 2].reshape(-1)
    total = segment.shape[0]
    start = segment * 4096.0
    key_code = start + jnp.where(flag > 0.5, block, block + 2048.0)
    low = start
    high = start + block + flag
    same = jnp.where(flag > 0.5, -1.0, key_code)
    position = block * BLK + (jnp.arange(total, dtype=jnp.int32) % BLK).astype(F32)
    qrow = jnp.pad(jnp.stack([low, high, same]), ((0, 5), (0, 0)))
    kcol = jnp.pad(jnp.stack([key_code, position], axis=1), ((0, 0), (0, 6)))
    freq = np.tile(
        np.float32(10000.0) ** (np.float32(-2.0) * np.arange(32, dtype=np.float32) / HD), 4
    )
    freq = jnp.asarray(freq.astype(np.float32)[None, :])
    vectors = extras[:, 1:3]
    bias_rel = vectors[:, 0, 3 * n1_w : 3 * n1_w + b1_w]
    vectors = jnp.roll(jnp.where(c == 0, vectors, vectors[:, ::-1]), z, axis=0)
    gain_one = vectors[:, :, :n1_w].reshape(1, D).astype(F32)
    gain_two = vectors[:, :, n1_w : 2 * n1_w].reshape(1, D).astype(F32)
    bias_two = vectors[:, :, 2 * n1_w : 3 * n1_w].reshape(1, D).astype(F32)

    if fast:
        cols = jnp.arange(768, dtype=jnp.int32)
        half, at = cols // 384, cols % 384
        qkv_order = order_matrix(
            256 * (at // 96) + 96 * (c ^ half) + at % 96, at < 288
        )
        out_order = order_matrix(
            192 * ((z + at // 96) % 4) + 96 * (c ^ half) + at % 96, at < 384
        )
        wq_parts = w_qkv.astype(BF)
        parts = []
        for i in range(3):
            parts.append(
                lax.ppermute(
                    wq_parts[:, 96 * i : 96 * i + 96],
                    "seq",
                    [(q, (3 * q + i) % 8) for q in range(8)],
                )
            )
        parts = jnp.stack(parts)
        wq_own = jnp.concatenate(
            [pick(parts, (2 * t + s) % 3) for t in range(3)] + [w_out.astype(BF)], axis=1
        )
        wq_own = jnp.stack([wq_own, links.flip(wq_own, 1)])
        wq_own = jnp.stack([wq_own, links.flip(wq_own, 2)]).reshape(4, 192, 384)
        wq_in = links.core(wq_own)
        wq = reorder_columns(place, wq_own, wq_in, qkv_order)
        wo_own = jnp.concatenate([wq_own[j, :, 288:] for j in range(4)], axis=1)

        two = jnp.concatenate(to_both((two_keep, both_in[chunk:, :384])), axis=0)
        w12 = jnp.stack([w_fc1.astype(BF), two])
        w_before = links.shift(w12, 1)
        w_after = links.shift(w12, -1)
        w1_two = links.shift(w_before[0], 1)
        w2_two = links.shift(w_after[1], -1)
        w1 = jnp.stack([w12[0], w_after[0], w1_two, w_before[0]])
        w2 = jnp.stack([w12[1], w_after[1], w2_two, w_before[1]])
        kcol = after(kcol, w1, w2)
        w1_in = links.flip(w1, 2)
        w2_in = links.flip(w2, 1)
        bias_one = bias_rel.reshape(4, 1, 384)
        ff_place = place
    else:

        def everywhere(w):
            w = lax.all_gather(w.astype(BF), "seq", axis=1, tiled=True)
            return lax.all_gather(w, "dp", axis=0, tiled=True)

        wq = everywhere(w_qkv).reshape(D, 3, D)
        wq = jnp.pad(wq, ((0, 0), (0, 0), (0, nz * hw - D)))
        wq = lax.dynamic_slice_in_dim(wq, z * hw, hw, 2)
        wq = jnp.pad(wq, ((0, 0), (0, 0), (0, lq - hw))).reshape(D, 3 * lq)
        wout = jnp.pad(everywhere(w_out), ((0, nz * hw - D), (0, 0))).reshape(nz, hw, D)
        w1 = lax.dynamic_slice_in_dim(everywhere(w_fc1), c * (FF // 2), FF // 2, 1)
        w1 = w1.reshape(2, 2, 192, 4, 384).transpose(3, 1, 0, 2, 4)
        w2 = lax.dynamic_slice_in_dim(everywhere(w_fc2), c * (FF // 2), FF // 2, 0)
        w2 = w2.reshape(2, 2, 384, 4, 192).transpose(3, 1, 0, 4, 2)
        w1, w2 = w1.transpose(1, 2, 0, 3, 4), w2.transpose(2, 1, 0, 3, 4)
        weights = (w1[0], w1[1], w2[0], w2[1])
        bias_all = vectors[:, :, 3 * n1_w : 3 * n1_w + b1_w].reshape(FF)
        bias_one = lax.dynamic_slice_in_dim(bias_all, c * (FF // 2), FF // 2, 0).reshape(4, 1, 384)
        ff_place = jnp.zeros((2,), jnp.int32)

    far = sorted(range(1, nz), key=lambda k: -min(k, nz - k))
    first = far[: nz // 2]
    rest = far[nz // 2 :] + [0]
    saved, by = attention_first(
        arrays, plan, kcol, qrow, freq, wq, gain_one, heads, chunk, first
    )
    mixed = {k: links.shift(by[k][0], k) for k in first}
    rest_in = saved
    if fast:
        w1_in, w2_in, wo_own, _ = lax.optimization_barrier((w1_in, w2_in, wo_own, by[first[0]]))
        w1a = jnp.stack([w1, w1_in])
        w2a = jnp.stack([w2, w2_in])
        w1b = links.flip(w1a, 1)
        w2b = links.flip(w2a, 2)
        weights = (w1a, w1b, w2a, w2b)
        wo_own = jnp.stack([wo_own] + [links.shift(wo_own, -k) for k in range(1, 4)])
        rest_in = after(tuple(saved), w1a, w2a)
    by_rest = attention_rest(rest_in, kcol, qrow, heads, chunk, rest)
    by = {**by, **by_rest}
    for k in rest:
        mixed[k] = links.shift(by[k][0], k) if k else by[k][0]
    mixed = [mixed[k] for k in range(nz)]
    if fast:
        wo_own = after(wo_own, by[0][0])
        wout = reorder_out(place, wo_own, links.core(wo_own), out_order)
    x_own = x_ext[:chunk]
    residual, h2 = output_projection(place, mixed, wout, x_own, gain_two)
    h2_in = links.core(h2)
    (out_own, out_other, gh_own, gh_other, dw1a, dw1b, dw2a, dw2b, db1) = feed_forward(
        ff_place, h2, h2_in, dy_own, dy_other, weights, bias_one
    )
    gh_in = links.core(gh_other)
    if fast:
        dw1_in = links.flip(dw1b, 1)
        dw2_in = links.flip(dw2b, 2)
    gres, gproj, sums, gmixed = residual_backward(
        place, gh_own, gh_in, residual, dy_own, gain_two, wout
    )
    pulled = [gmixed[0]] + [links.shift(gmixed[k], k) for k in range(1, nz)]
    pulled = [pulled[(nz - k) % nz] for k in range(nz)]
    part = attention_backward(
        pulled, by, saved, kcol, qrow, wq, heads, chunk, [0], None, False
    )
    grad_gain_two = jnp.sum(sums[:8], axis=0)
    grad_bias_two = jnp.sum(sums[8:], axis=0)
    grad_bias_one = jnp.sum(db1, axis=1)
    if fast:
        wo_keep, wo_send = out_weight(place, mixed, gproj, out_order)
        wo_came = links.core(wo_send)
    out_other = after(out_other, part)
    out_in = links.core(out_other)
    out_rows = (residual + out_own + out_in.astype(F32) + bias_two).astype(BF)
    rows_in = links.core(out_rows[local:])
    if fast:
        dwo = add_low(wo_keep, wo_came)
        part, _ = lax.optimization_barrier((part, (dwo, out_rows, grad_bias_one, grad_bias_two)))
        dwo = sum(
            [dwo[..., :96].astype(F32)]
            + [
                links.shift(dwo[..., 96 * k : 96 * k + 96], k).astype(F32)
                for k in range(1, 4)
            ]
        )
    made = attention_backward(
        pulled, by, saved, kcol, qrow, wq, heads, chunk, list(range(1, nz)), part, True
    )
    gqkv, n1_sum, gh1 = made[0], made[1], made[2:]
    if nz == 4:
        low_in = links.shift(gh1[2][:local], 1)
        high_in = links.shift(gh1[2][local:], -1)
        up = jnp.concatenate([add_low(gh1[1][:local], low_in), gh1[1][local:]], axis=0)
        down = jnp.concatenate([gh1[3][:local], add_low(gh1[3][local:], high_in)], axis=0)
        terms = [gh1[0], links.shift(up, 1), links.shift(down, -1)]
    else:
        terms = [gh1[0]] + [links.shift(gh1[k], k) for k in range(1, nz)]
    grad_rows = input_backward(terms, x_own, gain_one, gres)
    grad_in = links.core(grad_rows[local:])

    def by_micro(own, other):
        return jnp.where(c == 0, jnp.stack([own, other]), jnp.stack([other, own]))[:, None]

    outputs = by_micro(out_rows[:local], rows_in)
    input_grad = by_micro(grad_rows[:local], grad_in)

    grad_gain_one = jnp.sum(n1_sum, axis=0) / gain_one[0]

    if fast:
        wq_keep, wq_send = qkv_weight(place, saved[0], after(gqkv, low_in, high_in), qkv_order)
        joint = jnp.concatenate(
            [add_low(wq_keep, links.core(wq_send)), dwo.astype(BF)], axis=2
        )
        joint = joint.reshape(2, 2, 192, 384)
        joint = add_low(joint[0], links.flip(joint[1], 2))
        joint = joint[0].astype(F32) + links.flip(joint[1], 1).astype(F32)
        g_out = joint[:, 288:]
        third = jnp.stack([joint[:, 96 * t : 96 * t + 96] for t in range(3)])
        g_qkv = jnp.concatenate(
            [
                lax.ppermute(
                    pick(third, lax.rem(2 * (i - s + 9), 3)),
                    "seq",
                    [((3 * q + i) % 8, q) for q in range(8)],
                )
                for i in range(3)
            ],
            axis=1,
        )
        dw1_in, dw2_in, _ = lax.optimization_barrier((dw1_in, dw2_in, gqkv))
        dw1_in = links.flip(add_low(dw1a[1], dw1_in[1]), 2), dw1_in[0]
        dw2_in = links.flip(add_low(dw2a[1], dw2_in[1]), 1), dw2_in[0]
        dw1 = dw1a[0].astype(F32) + dw1_in[0].astype(F32) + dw1_in[1].astype(F32)
        dw2 = dw2a[0].astype(F32) + dw2_in[0].astype(F32) + dw2_in[1].astype(F32)
        low_in = links.shift(dw1[2].astype(BF), 1)
        high_in = links.shift(dw2[2].astype(BF), -1)
        up = jnp.stack([dw1[1] + low_in.astype(F32), dw2[1]]).astype(BF)
        down = jnp.stack([dw1[3], dw2[3] + high_in.astype(F32)]).astype(BF)
        up_in = links.shift(up, 1).astype(F32)
        down_in = links.shift(down, -1).astype(F32)
        dw = jnp.stack([dw1[0], dw2[0]]) + up_in + down_in
        g_fc1 = dw[0]
        keep, send = to_both((dw[1, :96], dw[1, 96:]))
        came = links.core(send)
        g_fc2 = jnp.concatenate(to_both((keep, came)), axis=1).T
        three = jnp.stack([grad_gain_one, grad_gain_two, grad_bias_two]).reshape(3, 4, 2, 96)
        three = jnp.roll(three, -z, axis=1)
        keep, send = to_both((three[:, :, 0], three[:, :, 1]))
        three = (keep + links.core(send)).transpose(1, 0, 2).reshape(4, 288)
        vec = jnp.concatenate([three, grad_bias_one, jnp.zeros((4, 352), F32)], axis=1)
        vec = vec.reshape(4, 8, 128)
        vec = sum([vec[0]] + [links.shift(vec[k], k) for k in range(1, 4)])
        for bit in (1, 2):
            vec = vec + links.flip(vec, bit)
        vec = vec.reshape(1024)
        vecs = (vec[:96], vec[96:192], vec[288:672], vec[192:288])
    else:

        def owned(w):
            w = lax.psum_scatter(w.astype(BF), "seq", scatter_dimension=1, tiled=True)
            return lax.psum_scatter(w, "dp", scatter_dimension=0, tiled=True).astype(F32)

        dwq = jnp.einsum("rd,rj->dj", saved[0], gqkv, preferred_element_type=F32)
        spread = jnp.zeros((D, 3, nz * hw), F32)
        spread = lax.dynamic_update_slice_in_dim(
            spread, dwq.reshape(D, 3, lq)[..., :hw], z * hw, 2
        )
        g_qkv = owned(spread[..., :D].reshape(D, 3 * D))
        mixed_all = jnp.concatenate(mixed, axis=1)
        dwo = jnp.einsum("ri,ro->io", mixed_all, gproj, preferred_element_type=F32)
        dwo = dwo.reshape(nz, hw, D)
        dwo = jnp.roll(dwo[::-1], z + 1, axis=0).reshape(nz * hw, D)[:D]
        g_out = owned(dwo)
        half = jnp.stack([dw1a, dw1b]).transpose(1, 0, 3, 2, 4).reshape(D, FF // 2)
        full = lax.dynamic_update_slice_in_dim(
            jnp.zeros((D, FF), BF), half, c * (FF // 2), 1
        )
        g_fc1 = owned(full)
        half = jnp.stack([dw2a, dw2b]).transpose(0, 1, 4, 2, 3).reshape(FF // 2, D)
        full = lax.dynamic_update_slice_in_dim(
            jnp.zeros((FF, D), BF), half, c * (FF // 2), 0
        )
        g_fc2 = owned(full)
        bias_full = lax.dynamic_update_slice_in_dim(
            jnp.zeros((FF,), F32), grad_bias_one.reshape(-1), c * (FF // 2), 0
        )
        vecs = tuple(
            lax.psum(lax.psum_scatter(v, "seq", scatter_dimension=0, tiled=True), "dp")
            for v in (grad_gain_one, grad_gain_two, bias_full, grad_bias_two)
        )

    return (
        outputs,
        input_grad,
        vecs[0],
        g_qkv,
        g_out,
        vecs[1],
        g_fc1,
        vecs[2],
        g_fc2,
        vecs[3],
    )


def solution(mesh):
    rows = P(None, "dp", "seq", None)
    labels = P(None, "dp", "seq")
    matrix = P("dp", "seq")
    vector = P("seq")
    return jax.shard_map(
        functools.partial(per_device, mesh.shape["dp"], mesh.shape["seq"]),
        mesh=mesh,
        in_specs=(
            rows, labels, labels, labels, vector, matrix, matrix, vector, matrix, vector, matrix,
            vector, rows,
        ),
        out_specs=(
            rows, rows, vector, matrix, matrix, vector, matrix, vector, matrix, vector,
        ),
        check_vma=False,
    )
```

profile of v0, /device:TPU:0, one launch (start us, length us, event | category | flops | bytes accessed | tf_op | source)
XLA Modules:
  0.0 323.3 jit_solution(16836484564843722849)
XLA Ops:
  2.4 3.9 %collective-permute-start.11 = (bf16[192,96]{1,0:T(8,128)(2,1)S(1)}, bf16[192,96]{1,0:T(8,128)(2,1)S(1)}, u32[]{:S(2)}, u32[]{:S(2)}) collective-permute-start(bf16[192,96]{1,0:T(8,128)(2,1)S(1)} %get-tuple-element.199), channel_id=1, source_target_pairs={{0,1},{1,4},{2,7},{3,2},{4,5},{5,0},{6,3},{7,6},{8,9},{9,12},{10,1... | collective-permute-start | bytes 110600 | tf_op jit(solution)/shard_map/ppermute | solution.py:1019
  6.3 5.0 %collective-permute-start.12 = (bf16[192,96]{1,0:T(8,128)(2,1)S(1)}, bf16[192,96]{1,0:T(8,128)(2,1)S(1)}, u32[]{:S(2)}, u32[]{:S(2)}) collective-permute-start(bf16[192,96]{1,0:T(8,128)(2,1)S(1)} %get-tuple-element.198), channel_id=1, source_target_pairs={{0,2},{1,5},{2,0},{3,3},{4,6},{5,1},{6,4},{7,7},{8,10},{9,13},{10,... | collective-permute-start | bytes 110600 | tf_op jit(solution)/shard_map/ppermute | solution.py:1019
  23.7 4.0 %collective-permute-done.13 = bf16[192,384]{1,0:T(8,128)(2,1)S(1)} collective-permute-done((bf16[192,384]{1,0:T(8,128)(2,1)S(1)}, bf16[192,384]{1,0:T(8,128)(2,1)S(1)}, u32[]{:S(2)}, u32[]{:S(2)}) %collective-permute-start.13) | collective-permute-done | bytes 147488 | tf_op jit(solution)/shard_map/ppermute | solution.py:879
  31.6 4.8 %collective-permute-done.14 = bf16[2,192,384]{2,1,0:T(8,128)(2,1)S(1)} collective-permute-done((bf16[2,192,384]{2,1,0:T(8,128)(2,1)S(1)}, bf16[2,192,384]{2,1,0:T(8,128)(2,1)S(1)}, u32[]{:S(2)}, u32[]{:S(2)}) %collective-permute-start.14) | collective-permute-done | bytes 294944 | tf_op jit(solution)/shard_map/ppermute | solution.py:879
  39.3 10.8 %collective-permute-done.1.refs_1_ = bf16[272,768]{1,0:T(8,128)(2,1)S(1)} collective-permute-done((bf16[272,768]{1,0:T(8,128)(2,1)S(1)}, bf16[272,768]{1,0:T(8,128)(2,1)S(1)}, u32[]{:S(2)}, u32[]{:S(2)}) %collective-permute-start.1) | collective-permute-done | bytes 417824 | tf_op jit(solution)/shard_map/ppermute | solution.py:883
  53.0 18.0 %collective-permute-done.4.refs_3_ = bf16[128,768]{1,0:T(8,128)(2,1)S(1)} collective-permute-done((bf16[128,768]{1,0:T(8,128)(2,1)S(1)}, bf16[128,768]{1,0:T(8,128)(2,1)S(1)}, u32[]{:S(2)}, u32[]{:S(2)}) %collective-permute-start.4) | collective-permute-done | bytes 196640 | tf_op jit(solution)/shard_map/ppermute | solution.py:883
  84.4 4.5 %reorder_columns.1.refs_8_.refs_19_ = bf16[768,768]{1,0:T(8,128)(2,1)} custom-call(s32[2]{0:T(128)} %pad_add_fusion.place_ref, bf16[4,192,384]{2,1,0:T(8,128)(2,1)} %bitcast.189, bf16[4,192,384]{2,1,0:T(8,128)(2,1)} %collective-permute-done.15.other_ref, bf16[768,768]{1,0:T(8,128)(2,1)} %select_convert_fusion.1.order_ref), custom_call_target="tpu_custom_call" | custom-call | flops 1000000000 | bytes 3000000 | tf_op jit(solution)/shard_map/reorder_columns/pallas_call | solution.py:495
  88.9 14.3 %attention_first.1 = (bf16[1024,768]{1,0:T(8,128)(2,1)}, bf16[1024,256]{1,0:T(8,128)(2,1)}, bf16[1024,256]{1,0:T(8,128)(2,1)}, bf16[1024,256]{1,0:T(8,128)(2,1)}...) custom-call(bf16[272,768]{1,0:T(8,128)(2,1)} %copy-done.10, ...), custom_call_target="tpu_custom_call" | custom-call | flops 8000000000 | bytes 8000000 | tf_op jit(solution)/shard_map/attention_first/pallas_call | solution.py:278
  107.0 8.1 %attention_rest.1 = (bf16[256,192]{1,0:T(8,128)(2,1)}, f32[256,256]{1,0:T(8,128)}, f32[8,256]{1,0:T(8,128)}, bf16[256,192]{1,0:T(8,128)(2,1)}, f32[256,256]{1,0:T(8,128)}, /*index=5*/f32[8,256]{1,0:T(8,128)}) custom-call(bf16[1024,256]{1,0:T(8,128)(2,1)} %get-tuple-element.88.q_ref.refs_3_.refs_9_, ...), custom_call_target="tpu_custom_call" | custom-call | flops 5000000000 | bytes 4000000 | tf_op jit(solution)/shard_map/attention_rest/pallas_call | solution.py:310
  119.7 2.9 collective-permute-start.19
  123.8 2.7 collective-permute-start.20
  128.0 5.7 %reorder_out.1.refs_4_.w_ref = bf16[4,192,768]{2,1,0:T(8,128)(2,1)} custom-call(s32[2]{0:T(128)} %pad_add_fusion.place_ref, bf16[4,192,384]{2,1,0:T(8,128)(2,1)} %copy-done.9, bf16[4,192,384]{2,1,0:T(8,128)(2,1)} %copy-done.25, bf16[768,768]{1,0:T(8,128)(2,1)} %select_convert_fusion.order_ref.refs_5_), custom_call_target="tpu_custom_call" | custom-call | flops 1000000000 | bytes 3000000 | tf_op jit(solution)/shard_map/reorder_out/pallas_call | solution.py:523
  135.1 3.8 %output_projection.1 = (f32[256,768]{1,0:T(8,128)}, bf16[256,768]{1,0:T(8,128)(2,1)}) custom-call(s32[2]{0:T(128)} %pad_add_fusion.place_ref, bf16[256,192]{1,0:T(8,128)(2,1)} %get-tuple-element.91.refs_0_, bf16[256,192]{1,0:T(8,128)(2,1)} %copy-done.30, bf16[256,192]{1,0:T(8,128)(2,1)} %copy-done.29, bf16[256,192]{1,0:T(8,128)(2,1)} %copy-done.31, ...), custom_call_target="tpu_custom_call" | custom-call | flops 1000000000 | bytes 3000000 | tf_op jit(solution)/shard_map/output_projection/pallas_call | solution.py:613
  141.2 2.6 collective-permute-done.27.w2b_ref
  145.3 20.9 %feed_forward.1 = (f32[256,768]{1,0:T(8,128)}, bf16[256,768]{1,0:T(8,128)(2,1)}, f32[256,768]{1,0:T(8,128)}, bf16[256,768]{1,0:T(8,128)(2,1)}, bf16[2,4,192,384]...) custom-call(s32[2]{0:T(128)} %pad_add_fusion.place_ref, ...), custom_call_target="tpu_custom_call" | custom-call | flops 7200000000 | bytes 15000000 | tf_op jit(solution)/shard_map/feed_forward/pallas_call | solution.py:740
  168.9 4.6 %residual_backward.1 = (f32[256,768]{1,0:T(8,128)}, bf16[256,768]{1,0:T(8,128)(2,1)}, f32[16,768]{1,0:T(8,128)}, bf16[256,192]{1,0:T(8,128)(2,1)}, bf16[256,192]...) custom-call(s32[2]{0:T(128)} %pad_add_fusion.place_ref, f32[256,768]{1,0:T(8,128)} %get-tuple-element.100.gh_ref, ...), custom_call_target="tpu_custom_call" | custom-call | flops 1000000000 | bytes 4000000 | tf_op jit(solution)/shard_map/residual_backward/pallas_call | solution.py:810
  173.5 7.6 %attention_backward_own.1 = (bf16[256,256]{1,0:T(8,128)(2,1)}, f32[1024,256]{1,0:T(8,128)}, f32[1024,256]{1,0:T(8,128)}) custom-call(bf16[256,192]{1,0:T(8,128)(2,1)} %get-tuple-element.102.refs_0_, f32[256,256]{1,0:T(8,128)} %get-tuple-element.103.refs_1_, f32[8,256]{1,0:T(8,128)} %get-tuple-element.104.refs_2_, ...), custom_call_target="tpu_custom_call" | custom-call | flops 3000000000 | bytes 10000000 | tf_op jit(solution)/shard_map/attention_backward_own/pallas_call | solution.py:455
  181.2 4.9 %out_weight.1 = (bf16[4,192,384]{2,1,0:T(8,128)(2,1)}, bf16[4,192,384]{2,1,0:T(8,128)(2,1)}) custom-call(s32[2]{0:T(128)} %pad_add_fusion.place_ref, bf16[256,192]{1,0:T(8,128)(2,1)} %get-tuple-element.91.refs_0_, bf16[256,192]{1,0:T(8,128)(2,1)} %copy-done.30, bf16[256,192]{1,0:T(8,128)(2,1)} %copy-done.29, bf16[256,192]{1,0:T(8,128)(2,1)} %copy-done.31, ...), custom_call_target="tpu_custom_call" | custom-call | flops 1000000000 | bytes 4000000 | tf_op jit(solution)/shard_map/out_weight/pallas_call | solution.py:581
  189.1 3.5 %collective-permute-start.31 = (bf16[256,192]{1,0:T(8,128)(2,1)}, bf16[256,192]{1,0:T(8,128)(2,1)}, u32[]{:S(2)}, u32[]{:S(2)}) collective-permute-start(bf16[256,192]{1,0:T(8,128)(2,1)} %get-tuple-element.109), channel_id=1, source_target_pairs={{0,6},{1,7},{2,0},{3,1},{4,2},{5,3},{6,4},{7,5},{8,14},{9,15},{10,... | collective-permute-start | bytes 294920 | tf_op jit(solution)/shard_map/ppermute | solution.py:883
  197.5 6.8 %collective-permute-done.32.refs_1_ = bf16[256,192]{1,0:T(8,128)(2,1)S(1)} collective-permute-done((bf16[256,192]{1,0:T(8,128)(2,1)}, bf16[256,192]{1,0:T(8,128)(2,1)S(1)}, u32[]{:S(2)}, u32[]{:S(2)}) %collective-permute-start.32) | collective-permute-done | bytes 98336 | tf_op jit(solution)/shard_map/ppermute | solution.py:883
  205.0 18.5 %attention_backward_last.1 = (bf16[1024,768]{1,0:T(8,128)(2,1)}, f32[8,768]{1,0:T(8,128)}, f32[256,768]{1,0:T(8,128)}, bf16[256,768]{1,0:T(8,128)(2,1)}, bf16[25...) custom-call(bf16[256,192]{1,0:T(8,128)(2,1)} %collective-permute-done.31.refs_0_, bf16[256,192]{1,0:T(8,128)(2,1)} %copy-done.35, ...), custom_call_target="tpu_custom_call" | custom-call | flops 8999999488 | bytes 10000000 | tf_op jit(solution)/shard_map/attention_backward_last/pallas_call | solution.py:455
  230.0 2.8 collective-permute-start.43
  247.3 5.9 %collective-permute-done.48 = bf16[4,192,96]{2,1,0:T(8,128)(2,1)S(1)} collective-permute-done((bf16[4,192,96]{2,1,0:T(8,128)(2,1)S(1)}, bf16[4,192,96]{2,1,0:T(8,128)(2,1)S(1)}, u32[]{:S(2)}, u32[]{:S(2)}) %collective-permute-start.48) | collective-permute-done | bytes 147488 | tf_op jit(solution)/shard_map/ppermute | solution.py:883
  253.2 3.4 %collective-permute-start.37 = (bf16[128,768]{1,0:T(8,128)(2,1)S(1)}, bf16[128,768]{1,0:T(8,128)(2,1)S(1)}, u32[]{:S(2)}, u32[]{:S(2)}) collective-permute-start(bf16[128,768]{1,0:T(8,128)(2,1)S(1)} %get-tuple-element.169), channel_id=1, source_target_pairs={{0,6},{1,7},{2,0},{3,1},{4,2},{5,3},{6,4},{7,5},{8,14},{9,15},{10,... | collective-permute-start | bytes 589832 | tf_op jit(solution)/shard_map/ppermute | solution.py:883
  262.3 2.6 collective-permute-start.38
  266.5 6.4 %qkv_weight.1 = (bf16[4,192,288]{2,1,0:T(8,128)(2,1)}, bf16[4,192,288]{2,1,0:T(8,128)(2,1)}) custom-call(s32[2]{0:T(128)} %pad_add_fusion.place_ref, bf16[1024,768]{1,0:T(8,128)(2,1)} %get-tuple-element.76.refs_20_.h_ref, bf16[1024,768]{1,0:T(8,128)(2,1)} %get-tuple-element.131.g_ref, bf16[768,768]{1,0:T(8,128)(2,1)} %select_convert_fusion.1.order_ref), custom_call_target="tpu_custom_call" | custom-call | flops 2000000000 | bytes 5000000 | tf_op jit(solution)/shard_map/qkv_weight/pallas_call | solution.py:550
  276.0 7.8 %collective-permute-done.36.refs_1_ = bf16[256,768]{1,0:T(8,128)(2,1)S(1)} collective-permute-done((bf16[256,768]{1,0:T(8,128)(2,1)}, bf16[256,768]{1,0:T(8,128)(2,1)S(1)}, u32[]{:S(2)}, u32[]{:S(2)}) %collective-permute-start.36) | collective-permute-done | bytes 393248 | tf_op jit(solution)/shard_map/ppermute | solution.py:883
  284.6 3.1 input_backward.1
  296.4 4.3 %collective-permute-done.59 = bf16[192,384]{1,0:T(8,128)(2,1)S(1)} collective-permute-done((bf16[192,384]{1,0:T(8,128)(2,1)S(1)}, bf16[192,384]{1,0:T(8,128)(2,1)S(1)}, u32[]{:S(2)}, u32[]{:S(2)}) %collective-permute-start.59) | collective-permute-done | bytes 147488 | tf_op jit(solution)/shard_map/ppermute | solution.py:883
  303.0 3.2 collective-permute-start.62
  310.1 5.2 %collective-permute-start.54 = (f32[192,96]{1,0:T(8,128)S(1)}, f32[192,96]{1,0:T(8,128)S(1)}, u32[]{:S(2)}, u32[]{:S(2)}) collective-permute-start(f32[192,96]{1,0:T(8,128)S(1)} %get-tuple-element.184), channel_id=1, source_target_pairs={{2,0},{5,1},{0,2},{3,3},{6,4},{1,5},{4,6},{7,7},{10,8},{13,9},{8,1... | collective-permute-start | bytes 221192 | tf_op jit(solution)/shard_map/ppermute | solution.py:1167
  316.2 3.6 %collective-permute-done.54 = f32[192,96]{1,0:T(8,128)S(1)} collective-permute-done((f32[192,96]{1,0:T(8,128)S(1)}, f32[192,96]{1,0:T(8,128)S(1)}, u32[]{:S(2)}, u32[]{:S(2)}) %collective-permute-start.54) | collective-permute-done | bytes 73760 | tf_op jit(solution)/shard_map/ppermute | solution.py:1167
  (338 shorter events, 115.2 us)
Async XLA Ops:
  1.7 19.4 %collective-permute-start.10 = (bf16[192,96]{1,0:T(8,128)(2,1)S(1)}, bf16[192,96]{1,0:T(8,128)(2,1)S(1)}, u32[]{:S(2)}, u32[]{:S(2)}) collective-permute-start(bf16[192,96]{1,0:T(8,128)(2,1)S(1)} %get-tuple-element.197), channel_id=1, source_target_pairs={{0,0},{1,3},{2,6},{3,1},{4,4},{5,7},{6,2},{7,5},{8,8},{9,11},{10,1... | collective-permute-start | bytes 110600 | tf_op jit(solution)/shard_map/ppermute | solution.py:1019
  2.4 18.7 %collective-permute-start.11 = (bf16[192,96]{1,0:T(8,128)(2,1)S(1)}, bf16[192,96]{1,0:T(8,128)(2,1)S(1)}, u32[]{:S(2)}, u32[]{:S(2)}) collective-permute-start(bf16[192,96]{1,0:T(8,128)(2,1)S(1)} %get-tuple-element.199), channel_id=1, source_target_pairs={{0,1},{1,4},{2,7},{3,2},{4,5},{5,0},{6,3},{7,6},{8,9},{9,12},{10,1... | collective-permute-start | bytes 110600 | tf_op jit(solution)/shard_map/ppermute | solution.py:1019
  6.3 14.8 %collective-permute-start.12 = (bf16[192,96]{1,0:T(8,128)(2,1)S(1)}, bf16[192,96]{1,0:T(8,128)(2,1)S(1)}, u32[]{:S(2)}, u32[]{:S(2)}) collective-permute-start(bf16[192,96]{1,0:T(8,128)(2,1)S(1)} %get-tuple-element.198), channel_id=1, source_target_pairs={{0,2},{1,5},{2,0},{3,3},{4,6},{5,1},{6,4},{7,7},{8,10},{9,13},{10,... | collective-permute-start | bytes 110600 | tf_op jit(solution)/shard_map/ppermute | solution.py:1019
  17.5 11.8 %collective-permute-start = (bf16[144,768]{1,0:T(8,128)(2,1)S(1)}, bf16[144,768]{1,0:T(8,128)(2,1)S(1)}, u32[]{:S(2)}, u32[]{:S(2)}) collective-permute-start(bf16[144,768]{1,0:T(8,128)(2,1)S(1)} %pad_maximum_fusion.19), channel_id=1, source_target_pairs={{0,1},{1,0},{2,3},{3,2},{4,5},{5,4},{6,7},{7,6},{8,9},{9,8},{10,11... | collective-permute-start | bytes 663560 | tf_op jit(solution)/shard_map/ppermute | solution.py:876
  19.3 17.5 %collective-permute-start.5 = (bf16[352,768]{1,0:T(8,128)(2,1)}, bf16[352,768]{1,0:T(8,128)(2,1)S(1)}, u32[]{:S(2)}, u32[]{:S(2)}) collective-permute-start(bf16[352,768]{1,0:T(8,128)(2,1)} %fusion.6), channel_id=1, source_target_pairs={{0,1},{1,0},{2,3},{3,2},{4,5},{5,4},{6,7},{7,6},{8,9},{9,8},{10,11... | collective-permute-start | bytes 1622024 | tf_op jit(solution)/shard_map/ppermute | solution.py:876
  29.5 20.6 %collective-permute-start.1 = (bf16[272,768]{1,0:T(8,128)(2,1)S(1)}, bf16[272,768]{1,0:T(8,128)(2,1)S(1)}, u32[]{:S(2)}, u32[]{:S(2)}) collective-permute-start(bf16[272,768]{1,0:T(8,128)(2,1)S(1)} %pad_maximum_fusion.6.refs_0_), channel_id=1, source_target_pairs={{0,6},{1,7},{2,0},{3,1},{4,2},{5,3},{6,4},{7,5},{8,14},{9,15},{10,... | collective-permute-start | bytes 1253384 | tf_op jit(solution)/shard_map/ppermute | solution.py:883
  30.5 20.3 %collective-permute-start.2 = (bf16[272,768]{1,0:T(8,128)(2,1)S(1)}, bf16[272,768]{1,0:T(8,128)(2,1)S(1)}, u32[]{:S(2)}, u32[]{:S(2)}) collective-permute-start(bf16[272,768]{1,0:T(8,128)(2,1)S(1)} %pad_maximum_fusion.6.refs_0_), channel_id=1, source_target_pairs={{0,2},{1,3},{2,4},{3,5},{4,6},{5,7},{6,0},{7,1},{8,10},{9,11},{10,... | collective-permute-start | bytes 1253384 | tf_op jit(solution)/shard_map/ppermute | solution.py:883
  36.4 48.0 %collective-permute-start.15 = (bf16[4,192,384]{2,1,0:T(8,128)(2,1)S(1)}, bf16[4,192,384]{2,1,0:T(8,128)(2,1)}, u32[]{:S(2)}, u32[]{:S(2)}) collective-permute-start(bf16[4,192,384]{2,1,0:T(8,128)(2,1)S(1)} %bitcast.187), channel_id=1, source_target_pairs={{0,1},{1,0},{2,3},{3,2},{4,5},{5,4},{6,7},{7,6},{8,9},{9,8},{10,11... | collective-permute-start | bytes 1769480 | tf_op jit(solution)/shard_map/ppermute | solution.py:876
  37.3 34.7 %collective-permute-start.6 = (bf16[2,192,384]{2,1,0:T(8,128)(2,1)S(1)}, bf16[2,192,384]{2,1,0:T(8,128)(2,1)}, u32[]{:S(2)}, u32[]{:S(2)}) collective-permute-start(bf16[2,192,384]{2,1,0:T(8,128)(2,1)S(1)} %pad_maximum_fusion.13), channel_id=1, source_target_pairs={{0,6},{1,7},{2,0},{3,1},{4,2},{5,3},{6,4},{7,5},{8,14},{9,15},{10,... | collective-permute-start | bytes 884744 | tf_op jit(solution)/shard_map/ppermute | solution.py:883
  38.2 35.6 %collective-permute-start.7 = (bf16[2,192,384]{2,1,0:T(8,128)(2,1)S(1)}, bf16[2,192,384]{2,1,0:T(8,128)(2,1)}, u32[]{:S(2)}, u32[]{:S(2)}) collective-permute-start(bf16[2,192,384]{2,1,0:T(8,128)(2,1)S(1)} %pad_maximum_fusion.13), channel_id=1, source_target_pairs={{0,2},{1,3},{2,4},{3,5},{4,6},{5,7},{6,0},{7,1},{8,10},{9,11},{10,... | collective-permute-start | bytes 884744 | tf_op jit(solution)/shard_map/ppermute | solution.py:883
  50.1 20.8 %collective-permute-start.4 = (bf16[128,768]{1,0:T(8,128)(2,1)S(1)}, bf16[128,768]{1,0:T(8,128)(2,1)S(1)}, u32[]{:S(2)}, u32[]{:S(2)}) collective-permute-start(bf16[128,768]{1,0:T(8,128)(2,1)S(1)} %slice.359), channel_id=1, source_target_pairs={{0,6},{1,7},{2,0},{3,1},{4,2},{5,3},{6,4},{7,5},{8,14},{9,15},{10,... | collective-permute-start | bytes 589832 | tf_op jit(solution)/shard_map/ppermute | solution.py:883
  51.6 37.3 %collective-permute-start.3 = (bf16[144,768]{1,0:T(8,128)(2,1)}, bf16[144,768]{1,0:T(8,128)(2,1)}, u32[]{:S(2)}, u32[]{:S(2)}) collective-permute-start(bf16[144,768]{1,0:T(8,128)(2,1)} %slice.358), channel_id=1, source_target_pairs={{0,2},{1,3},{2,4},{3,5},{4,6},{5,7},{6,0},{7,1},{8,10},{9,11},{10,... | collective-permute-start | bytes 663560 | tf_op jit(solution)/shard_map/ppermute | solution.py:883
  81.1 22.1 %collective-permute-start.17 = (bf16[4,192,384]{2,1,0:T(8,128)(2,1)S(1)}, bf16[4,192,384]{2,1,0:T(8,128)(2,1)S(1)}, u32[]{:S(2)}, u32[]{:S(2)}) collective-permute-start(bf16[4,192,384]{2,1,0:T(8,128)(2,1)S(1)} %get-tuple-element.160), channel_id=1, source_target_pairs={{0,8},{8,0},{16,24},{24,16},{1,9},{9,1},{17,25},{25,17},{2,10},{10... | collective-permute-start | bytes 1769480 | tf_op jit(solution)/shard_map/ppermute | solution.py:879
  83.8 19.4 %collective-permute-start.16 = (bf16[4,192,384]{2,1,0:T(8,128)(2,1)S(1)}, bf16[4,192,384]{2,1,0:T(8,128)(2,1)S(1)}, u32[]{:S(2)}, u32[]{:S(2)}) collective-permute-start(bf16[4,192,384]{2,1,0:T(8,128)(2,1)S(1)} %get-tuple-element.162), channel_id=1, source_target_pairs={{0,16},{8,24},{16,0},{24,8},{1,17},{9,25},{17,1},{25,9},{2,18},{10... | collective-permute-start | bytes 1769480 | tf_op jit(solution)/shard_map/ppermute | solution.py:879
  103.2 11.9 %collective-permute-start.21 = (bf16[192,384]{1,0:T(8,128)(2,1)S(1)}, bf16[192,384]{1,0:T(8,128)(2,1)S(1)}, u32[]{:S(2)}, u32[]{:S(2)}) collective-permute-start(bf16[192,384]{1,0:T(8,128)(2,1)S(1)} %pad_maximum_fusion.22), channel_id=1, source_target_pairs={{0,6},{1,7},{2,0},{3,1},{4,2},{5,3},{6,4},{7,5},{8,14},{9,15},{10,... | collective-permute-start | bytes 442376 | tf_op jit(solution)/shard_map/ppermute | solution.py:883
  115.3 28.5 %collective-permute-start.27 = (bf16[2,4,192,384]{3,2,1,0:T(8,128)(2,1)S(1)}, bf16[2,4,192,384]{3,2,1,0:T(8,128)(2,1)}, u32[]{:S(2)}, u32[]{:S(2)}) collective-permute-start(bf16[2,4,192,384]{3,2,1,0:T(8,128)(2,1)S(1)} %pad_maximum_fusion.1.w2a_ref), channel_id=1, source_target_pairs={{0,16},{8,24},{16,0},{24,8},{1,17},{9,25},{17,1},{25,9},{2,18},{10... | collective-permute-start | bytes 3538952 | tf_op jit(solution)/shard_map/ppermute | solution.py:879
  116.9 28.3 %collective-permute-start.26 = (bf16[2,4,192,384]{3,2,1,0:T(8,128)(2,1)}, bf16[2,4,192,384]{3,2,1,0:T(8,128)(2,1)}, u32[]{:S(2)}, u32[]{:S(2)}) collective-permute-start(bf16[2,4,192,384]{3,2,1,0:T(8,128)(2,1)} %pad_maximum_fusion.w1a_ref), channel_id=1, source_target_pairs={{0,8},{8,0},{16,24},{24,16},{1,9},{9,1},{17,25},{25,17},{2,10},{10... | collective-permute-start | bytes 3538952 | tf_op jit(solution)/shard_map/ppermute | solution.py:879
  119.7 13.9 %collective-permute-start.19 = (bf16[256,192]{1,0:T(8,128)(2,1)S(1)}, bf16[256,192]{1,0:T(8,128)(2,1)S(1)}, u32[]{:S(2)}, u32[]{:S(2)}) collective-permute-start(bf16[256,192]{1,0:T(8,128)(2,1)S(1)} %copy-done.32), channel_id=1, source_target_pairs={{0,4},{1,5},{2,6},{3,7},{4,0},{5,1},{6,2},{7,3},{8,12},{9,13},{10,... | collective-permute-start | bytes 294920 | tf_op jit(solution)/shard_map/ppermute | solution.py:883
  187.3 71.4 %collective-permute-start.55 = (bf16[2,4,192,384]{3,2,1,0:T(8,128)(2,1)}, bf16[2,4,192,384]{3,2,1,0:T(8,128)(2,1)S(1)}, u32[]{:S(2)}, u32[]{:S(2)}) collective-permute-start(bf16[2,4,192,384]{3,2,1,0:T(8,128)(2,1)} %get-tuple-element.135), channel_id=1, source_target_pairs={{0,8},{8,0},{16,24},{24,16},{1,9},{9,1},{17,25},{25,17},{2,10},{10... | collective-permute-start | bytes 3538952 | tf_op jit(solution)/shard_map/ppermute | solution.py:879
  188.6 70.1 %collective-permute-start.56 = (bf16[2,4,192,384]{3,2,1,0:T(8,128)(2,1)}, bf16[2,4,192,384]{3,2,1,0:T(8,128)(2,1)S(1)}, u32[]{:S(2)}, u32[]{:S(2)}) collective-permute-start(bf16[2,4,192,384]{3,2,1,0:T(8,128)(2,1)} %get-tuple-element.136), channel_id=1, source_target_pairs={{0,16},{8,24},{16,0},{24,8},{1,17},{9,25},{17,1},{25,9},{2,18},{10... | collective-permute-start | bytes 3538952 | tf_op jit(solution)/shard_map/ppermute | solution.py:879
  234.7 12.1 %collective-permute-start.47 = (bf16[4,192,96]{2,1,0:T(8,128)(2,1)S(1)}, bf16[4,192,96]{2,1,0:T(8,128)(2,1)S(1)}, u32[]{:S(2)}, u32[]{:S(2)}) collective-permute-start(bf16[4,192,96]{2,1,0:T(8,128)(2,1)S(1)} %get-tuple-element.156), channel_id=1, source_target_pairs={{0,2},{1,3},{2,4},{3,5},{4,6},{5,7},{6,0},{7,1},{8,10},{9,11},{10,... | collective-permute-start | bytes 442376 | tf_op jit(solution)/shard_map/ppermute | solution.py:883
  237.8 15.4 %collective-permute-start.48 = (bf16[4,192,96]{2,1,0:T(8,128)(2,1)S(1)}, bf16[4,192,96]{2,1,0:T(8,128)(2,1)S(1)}, u32[]{:S(2)}, u32[]{:S(2)}) collective-permute-start(bf16[4,192,96]{2,1,0:T(8,128)(2,1)S(1)} %get-tuple-element.158), channel_id=1, source_target_pairs={{0,4},{1,5},{2,6},{3,7},{4,0},{5,1},{6,2},{7,3},{8,12},{9,13},{10,... | collective-permute-start | bytes 442376 | tf_op jit(solution)/shard_map/ppermute | solution.py:883
  243.1 15.5 %collective-permute-start.49 = (bf16[4,192,96]{2,1,0:T(8,128)(2,1)S(1)}, bf16[4,192,96]{2,1,0:T(8,128)(2,1)S(1)}, u32[]{:S(2)}, u32[]{:S(2)}) collective-permute-start(bf16[4,192,96]{2,1,0:T(8,128)(2,1)S(1)} %get-tuple-element.157), channel_id=1, source_target_pairs={{0,6},{1,7},{2,0},{3,1},{4,2},{5,3},{6,4},{7,5},{8,14},{9,15},{10,... | collective-permute-start | bytes 442376 | tf_op jit(solution)/shard_map/ppermute | solution.py:883
  246.8 13.6 %collective-permute-start.35 = (bf16[128,768]{1,0:T(8,128)(2,1)S(1)}, bf16[128,768]{1,0:T(8,128)(2,1)S(1)}, u32[]{:S(2)}, u32[]{:S(2)}) collective-permute-start(bf16[128,768]{1,0:T(8,128)(2,1)S(1)} %get-tuple-element.170), channel_id=1, source_target_pairs={{0,2},{1,3},{2,4},{3,5},{4,6},{5,7},{6,0},{7,1},{8,10},{9,11},{10,... | collective-permute-start | bytes 589832 | tf_op jit(solution)/shard_map/ppermute | solution.py:883
  258.8 33.0 %collective-permute-start.57 = (bf16[4,192,384]{2,1,0:T(8,128)(2,1)S(1)}, bf16[4,192,384]{2,1,0:T(8,128)(2,1)S(1)}, u32[]{:S(2)}, u32[]{:S(2)}) collective-permute-start(bf16[4,192,384]{2,1,0:T(8,128)(2,1)S(1)} %fusion.3), channel_id=1, source_target_pairs={{0,16},{8,24},{16,0},{24,8},{1,17},{9,25},{17,1},{25,9},{2,18},{10... | collective-permute-start | bytes 1769480 | tf_op jit(solution)/shard_map/ppermute | solution.py:879
  262.3 13.8 %collective-permute-start.38 = (bf16[256,768]{1,0:T(8,128)(2,1)}, bf16[256,768]{1,0:T(8,128)(2,1)}, u32[]{:S(2)}, u32[]{:S(2)}) collective-permute-start(bf16[256,768]{1,0:T(8,128)(2,1)} %pad_maximum_fusion.11), channel_id=1, source_target_pairs={{0,6},{1,7},{2,0},{3,1},{4,2},{5,3},{6,4},{7,5},{8,14},{9,15},{10,... | collective-permute-start | bytes 1179656 | tf_op jit(solution)/shard_map/ppermute | solution.py:883
  265.8 18.1 %collective-permute-start.36 = (bf16[256,768]{1,0:T(8,128)(2,1)}, bf16[256,768]{1,0:T(8,128)(2,1)S(1)}, u32[]{:S(2)}, u32[]{:S(2)}) collective-permute-start(bf16[256,768]{1,0:T(8,128)(2,1)} %pad_maximum_fusion.10), channel_id=1, source_target_pairs={{0,2},{1,3},{2,4},{3,5},{4,6},{5,7},{6,0},{7,1},{8,10},{9,11},{10,... | collective-permute-start | bytes 1179656 | tf_op jit(solution)/shard_map/ppermute | solution.py:883
  272.8 16.0 %collective-permute-start.46 = (bf16[4,192,288]{2,1,0:T(8,128)(2,1)}, bf16[4,192,288]{2,1,0:T(8,128)(2,1)}, u32[]{:S(2)}, u32[]{:S(2)}) collective-permute-start(bf16[4,192,288]{2,1,0:T(8,128)(2,1)} %get-tuple-element.133), channel_id=1, source_target_pairs={{0,1},{1,0},{2,3},{3,2},{4,5},{5,4},{6,7},{7,6},{8,9},{9,8},{10,11... | collective-permute-start | bytes 1327112 | tf_op jit(solution)/shard_map/ppermute | solution.py:876
  273.0 20.8 %collective-permute-start.58 = (bf16[4,192,384]{2,1,0:T(8,128)(2,1)S(1)}, bf16[4,192,384]{2,1,0:T(8,128)(2,1)S(1)}, u32[]{:S(2)}, u32[]{:S(2)}) collective-permute-start(bf16[4,192,384]{2,1,0:T(8,128)(2,1)S(1)} %fusion.4), channel_id=1, source_target_pairs={{0,8},{8,0},{16,24},{24,16},{1,9},{9,1},{17,25},{25,17},{2,10},{10... | collective-permute-start | bytes 1769480 | tf_op jit(solution)/shard_map/ppermute | solution.py:879
  288.8 21.4 %collective-permute-start.39 = (bf16[128,768]{1,0:T(8,128)(2,1)S(1)}, bf16[128,768]{1,0:T(8,128)(2,1)S(1)}, u32[]{:S(2)}, u32[]{:S(2)}) collective-permute-start(bf16[128,768]{1,0:T(8,128)(2,1)S(1)} %get-tuple-element.168), channel_id=1, source_target_pairs={{0,1},{1,0},{2,3},{3,2},{4,5},{5,4},{6,7},{7,6},{8,9},{9,8},{10,11... | collective-permute-start | bytes 589832 | tf_op jit(solution)/shard_map/ppermute | solution.py:876
  300.8 19.8 %collective-permute-start.60 = (bf16[2,192,384]{2,1,0:T(8,128)(2,1)S(1)}, bf16[2,192,384]{2,1,0:T(8,128)(2,1)S(1)}, u32[]{:S(2)}, u32[]{:S(2)}) collective-permute-start(bf16[2,192,384]{2,1,0:T(8,128)(2,1)S(1)} %pad_maximum_fusion.17), channel_id=1, source_target_pairs={{0,2},{1,3},{2,4},{3,5},{4,6},{5,7},{6,0},{7,1},{8,10},{9,11},{10,... | collective-permute-start | bytes 884744 | tf_op jit(solution)/shard_map/ppermute | solution.py:883
  303.0 17.7 %collective-permute-start.62 = (bf16[2,192,384]{2,1,0:T(8,128)(2,1)S(1)}, bf16[2,192,384]{2,1,0:T(8,128)(2,1)S(1)}, u32[]{:S(2)}, u32[]{:S(2)}) collective-permute-start(bf16[2,192,384]{2,1,0:T(8,128)(2,1)S(1)} %pad_maximum_fusion.18), channel_id=1, source_target_pairs={{0,6},{1,7},{2,0},{3,1},{4,2},{5,3},{6,4},{7,5},{8,14},{9,15},{10,... | collective-permute-start | bytes 884744 | tf_op jit(solution)/shard_map/ppermute | solution.py:883
  (70 other events, 542.5 us)
where the time goes:
time: 324 us; the launch traced here: 323 us
  Pallas kernels  102 us (31%)
  starting transfers between devices  84.8 us (26%)
  waiting for transfers between devices  82.5 us (25%)
  other arithmetic  30.9 us (10%)
  local copies, waits for them, and re-layouts  21 us (6%)
    ppermute x31, waiting for transfers between devices, shift(): lax.ppermute(v, 'seq', [(s, 2 * ((s // 2 + k) % n) + s % 2) for s in rang...  61 us
    ppermute x31, starting transfers between devices, shift(): lax.ppermute(v, 'seq', [(s, 2 * ((s // 2 + k) % n) + s % 2) for s in rang...  47.8 us
    pallas_call x2, Pallas kernels, attention_backward(): pl.pallas_call(kernel, name='attention_backward_last' if last else 'atten...  26.1 us
    pallas_call x1, Pallas kernels, feed_forward(): pl.pallas_call(kernel, name='feed_forward', grid_spec=pltpu.PrefetchScala...  20.9 us
    ppermute x14, starting transfers between devices, flip(): return lax.ppermute(v, 'dp', [(i, i ^ bit) for i in range(self.n_dp)])  17.4 us
    ppermute x14, waiting for transfers between devices, flip(): return lax.ppermute(v, 'dp', [(i, i ^ bit) for i in range(self.n_dp)])  15.2 us
    pallas_call x1, Pallas kernels, attention_first(): pl.pallas_call(kernel, name='attention_first', grid=(len(entries),), in_s...  14.3 us
    ppermute x3, starting transfers between devices, per_device(): lax.ppermute(wq_parts[:, 96 * i:96 * i + 96], 'seq', [(q, (3 * q + i) % 8...  9.52 us
  transfers between devices with their start and end apart: 64, of which 24 were waited for; matrix products, arithmetic and copies ran while one was open for 14% of the time, Pallas kernels for 21%

commit v1 on v0

--- a/solution.py
+++ b/solution.py
@@ -20,7 +20,7 @@
 
 
 def cost(flops, nbytes):
-    return pl.CostEstimate(flops=int(flops), bytes_accessed=int(nbytes), transcendentals=0)
+    return pl.CostEstimate(flops=int(flops * 1e-3), bytes_accessed=int(nbytes * 1e-3), transcendentals=0)
 
 
 def params(*semantics):
@@ -114,7 +114,7 @@
 
 
 def pair_mask(kcol_ref, rows, codes):
-    key = kcol_ref[rows, 0:1]
+    key = kcol_ref[rows, 3:4]
     low, high, same = codes
     return ((key >= low) & (key < high)) | (key == same)
 
@@ -213,24 +213,163 @@
     return {e: tuple(made[3 * i : 3 * i + 3]) for i, e in enumerate(entries)}
 
 
-def attention_first(arrays, plan, kcol, qrow, freq, wq, gain, heads, chunk, entries):
-    total = kcol.shape[0]
-    blocks = total // chunk
-    lq = wq.shape[1] // 3
+def fill_rows(scr, row, which, labels, vectors, at):
+    local = labels[0].shape[1]
+    for i, ref in enumerate(labels):
+        value = jnp.where(which == 0, ref[0:1, :], ref[1:2, :]).astype(F32)
+        scr[row : row + 1, at + local * i : at + local * (i + 1)] = value
+    for i, ref in enumerate(vectors):
+        scr[row + 1 : row + 2, 128 * i : 128 * i + ref.shape[1]] = ref[...]
+
+
+def message_rows(place, x, labels, vectors):
+    local = x.shape[1]
+
+    def kernel(place_ref, x_ref, *refs):
+        label_refs, vector_refs, out_ref, scr = refs[:3], refs[3:7], refs[7], refs[8]
+        other = 1 - place_ref[2]
+        out_ref[:local, :] = x_ref[other]
+        scr[...] = jnp.zeros_like(scr)
+        fill_rows(scr, 0, other, label_refs, vector_refs, 0)
+        out_ref[local:, :] = scr[...].astype(BF)
+
+    ins = [x] + list(labels) + list(vectors)
+    return pl.pallas_call(
+        kernel,
+        name="message_rows",
+        grid_spec=pltpu.PrefetchScalarGridSpec(
+            num_scalar_prefetch=1,
+            grid=(1,),
+            in_specs=[whole(a.shape) for a in ins],
+            out_specs=whole((local + 16, D)),
+            scratch_shapes=[pltpu.VMEM((16, D), F32)],
+        ),
+        out_shape=jax.ShapeDtypeStruct((local + 16, D), BF),
+        compiler_params=params("arbitrary"),
+        cost_estimate=cost(1e6, 1e6),
+    )(place, *ins)
+
+
+def own_rows(place, x, labels, vectors, came):
+    local = x.shape[1]
+
+    def kernel(place_ref, x_ref, *refs):
+        label_refs, vector_refs, came_ref, out_ref, scr = refs[:3], refs[3:7], *refs[7:]
+        own = place_ref[2]
+        out_ref[:local, :] = x_ref[own]
+        out_ref[local : 2 * local, :] = came_ref[:local, :]
+        scr[...] = jnp.zeros_like(scr)
+        fill_rows(scr, 0, own, label_refs, vector_refs, 0)
+        extra = came_ref[local:, :].astype(F32)
+        scr[0:1, 3 * local : 6 * local] = extra[0:1, : 3 * local]
+        scr[2:3, :] = extra[1:2, :]
+        out_ref[2 * local :, :] = scr[...].astype(BF)
+
+    ins = [x] + list(labels) + list(vectors) + [came]
+    return pl.pallas_call(
+        kernel,
+        name="own_rows",
+        grid_spec=pltpu.PrefetchScalarGridSpec(
+            num_scalar_prefetch=1,
+            grid=(1,),
+            in_specs=[whole(a.shape) for a in ins],
+            out_specs=whole((2 * local + 16, D)),
+            scratch_shapes=[pltpu.VMEM((16, D), F32)],
+        ),
+        out_shape=jax.ShapeDtypeStruct((2 * local + 16, D), BF),
+        compiler_params=params("arbitrary"),
+        cost_estimate=cost(1e6, 1e6),
+    )(place, *ins)
+
+
+def attention_first(place, arrays, plan, extras, freq, wq, order, heads, chunk, entries, widths):
+    blocks = len(extras)
+    total = blocks * chunk
+    local = chunk // 2
     hw = heads * HD
+    lq = -(-hw // 128) * 128
     count = len(arrays)
-
-    def kernel(*refs):
+    parts = len(wq)
+    n_w, b_w = widths
+    fixed = 11
+
+    def kernel(place_ref, *refs):
         x_refs = refs[:count]
-        kcol_ref, qrow_ref, freq_ref, wq_ref, gain_ref = refs[count : count + 5]
-        h1_ref, q_ref, k_ref, v_ref, vt_ref, cs_ref, sn_ref = refs[count + 5 : count + 12]
-        block_refs = refs[count + 12 : count + 12 + 3 * len(entries)]
-        s_scr, p_scr = refs[count + 12 + 3 * len(entries) :]
+        freq_ref, order_ref = refs[count : count + 2]
+        wq_refs = refs[count + 2 : count + 2 + parts]
+        outs = refs[count + 2 + parts :]
+        h1_ref, q_ref, k_ref, v_ref, vt_ref, cs_ref, sn_ref, kcol_ref, qrow_ref, gain_ref, wq_ref = (
+            outs[:fixed]
+        )
+        bias_ref = outs[fixed]
+        block_refs = outs[fixed + 1 : fixed + 1 + 3 * len(entries)]
+        s_scr, p_scr, g_scr = outs[fixed + 1 + 3 * len(entries) :]
         step = pl.program_id(0)
+        d, c = place_ref[0], place_ref[2]
 
         @pl.when(step == 0)
         def _():
-            gain_row = gain_ref[...]
+            g_scr[...] = jnp.zeros_like(g_scr)
+            bias_ref[...] = jnp.zeros_like(bias_ref)
+            turn = lax.broadcasted_iota(jnp.int32, (1, chunk), 1) % BLK
+            for k, (which, at) in enumerate(extras):
+                rows = x_refs[which][at : at + 16, :].astype(F32)
+
+                def label(i, rows=rows):
+                    return jnp.concatenate(
+                        [
+                            rows[0:1, i * local : (i + 1) * local],
+                            rows[0:1, (3 + i) * local : (4 + i) * local],
+                        ],
+                        axis=1,
+                    )
+
+                segment, flag, block = label(0), label(1), label(2)
+                start = segment * 4096.0
+                clean = flag > 0.5
+                key = start + jnp.where(clean, block, block + 2048.0)
+                place_now = block * BLK + turn.astype(F32)
+                coded = jnp.concatenate(
+                    [
+                        start,
+                        start + block + flag,
+                        jnp.where(clean, -1.0, key),
+                        key,
+                        place_now,
+                        jnp.zeros((3, chunk), F32),
+                    ],
+                    axis=0,
+                )
+                qrow_ref[:, k * chunk : (k + 1) * chunk] = coded
+                kcol_ref[k * chunk : (k + 1) * chunk, :] = coded.T
+                for half in range(2):
+                    vector = rows[1 + half : 2 + half, :]
+                    lane = 384 * half + n_w * k
+                    for i in range(3):
+                        g_scr[i : i + 1, lane : lane + n_w] = vector[:, 128 * i : 128 * i + n_w]
+                if parts == 2:
+                    bias_ref[k : k + 1, :b_w] = rows[1:2, 384 : 384 + b_w]
+            gain_ref[...] = dot_t(g_scr[...].astype(BF), order_ref[...])
+            if parts == 2:
+                for half in range(2):
+
+                    @pl.when(c == half)
+                    def _(half=half):
+                        for j in range(4):
+                            rows = slice(192 * j, 192 * j + 192)
+                            for t in range(3):
+                                for i in range(2):
+                                    at = lq * t + 96 * (i ^ half)
+                                    wq_ref[rows, at : at + 96] = wq_refs[i][
+                                        d ^ j, :, 96 * t : 96 * t + 96
+                                    ]
+
+                for t in range(3):
+                    if hw < lq:
+                        wq_ref[:, lq * t + hw : lq * (t + 1)] = jnp.zeros((D, lq - hw), BF)
+            else:
+                wq_ref[...] = wq_refs[0][...]
+            gain_row = gain_ref[0:1, :]
             for which, src, dst, rows in plan:
                 for at, size in cuts(rows, 64):
                     xhat, _ = normed(x_refs[which][src + at : src + at + size, :].astype(F32))
@@ -240,7 +379,7 @@
 
             def project(block, carry):
                 rows = pl.ds(pl.multiple_of(block * chunk, chunk), chunk)
-                cosine, sine = cos_sin(kcol_ref[rows, 1:2] * freq_ref[...])
+                cosine, sine = cos_sin(kcol_ref[rows, 4:5] * freq_ref[...])
                 sine = sine * sign
                 cs_ref[rows, :] = cosine
                 sn_ref[rows, :] = sine
@@ -265,7 +404,7 @@
         )
         store_block(step, entries, block_refs, joined, logs, hw)
 
-    ins = list(arrays) + [kcol, qrow, freq, wq, gain]
+    ins = list(arrays) + [freq, order] + list(wq)
     out_shape = [
         jax.ShapeDtypeStruct((total, D), BF),
         jax.ShapeDtypeStruct((total, lq), BF),
@@ -274,26 +413,35 @@
         jax.ShapeDtypeStruct((lq, total), BF),
         jax.ShapeDtypeStruct((total, 128), F32),
         jax.ShapeDtypeStruct((total, 128), F32),
+        jax.ShapeDtypeStruct((total, 8), F32),
+        jax.ShapeDtypeStruct((8, total), F32),
+        jax.ShapeDtypeStruct((16, D), F32),
+        jax.ShapeDtypeStruct((D, 3 * lq), BF),
+        jax.ShapeDtypeStruct((-(-blocks // 8) * 8, 384), F32),
     ] + block_outputs(entries, lq, hw, chunk)
     made = pl.pallas_call(
         kernel,
         name="attention_first",
-        grid=(len(entries),),
-        in_specs=[whole(v.shape) for v in ins],
-        out_specs=[whole(o.shape) for o in out_shape],
+        grid_spec=pltpu.PrefetchScalarGridSpec(
+            num_scalar_prefetch=1,
+            grid=(len(entries),),
+            in_specs=[whole(v.shape) for v in ins],
+            out_specs=[whole(o.shape) for o in out_shape],
+            scratch_shapes=[
+                pltpu.VMEM((total, heads * chunk), F32),
+                pltpu.VMEM((total, heads * chunk), BF),
+                pltpu.VMEM((16, D), F32),
+            ],
+        ),
         out_shape=out_shape,
-        scratch_shapes=[
-            pltpu.VMEM((total, heads * chunk), F32),
-            pltpu.VMEM((total, heads * chunk), BF),
-        ],
         compiler_params=params("arbitrary"),
         cost_estimate=cost(8e9, 8e6),
-    )(*ins)
-    return made[:7], by_block(entries, made[7:])
-
-
-def attention_rest(saved, kcol, qrow, heads, chunk, entries):
-    _, q, k, _, vt, _, _ = saved
+    )(place, *ins)
+    return made[:12], by_block(entries, made[12:])
+
+
+def attention_rest(saved, heads, chunk, entries):
+    q, k, vt, kcol, qrow = saved
     total, lq = k.shape
     hw = heads * HD
 
@@ -324,22 +472,25 @@
     return by_block(entries, made)
 
 
-def attention_backward(pulls, by, saved, kcol, qrow, wq, heads, chunk, entries, before, last):
-    h1, q, k, v, _, cs, sn = saved
+def attention_backward(pulls, by, saved, heads, chunk, entries, before, finish):
+    h1, q, k, v, _, cs, sn, kcol, qrow, gains, wq = saved[:11]
+    last = finish is not None
     total, lq = k.shape
     blocks = total // chunk
     hw = heads * HD
     n = len(entries)
+    halves = blocks == 4
+    pieces = blocks + 1 if halves else blocks
 
     def kernel(*refs):
         g_refs, att_refs, lse_refs = refs[:n], refs[n : 2 * n], refs[2 * n : 3 * n]
         q_ref, k_ref, v_ref, cs_ref, sn_ref, kcol_ref, qrow_ref = refs[3 * n : 3 * n + 7]
         refs = refs[3 * n + 7 :]
         if last:
-            dq_in, dk_in, dv_in, wq_ref, h1_ref = refs[:5]
-            gqkv_ref, n1_ref = refs[5:7]
-            gh_refs = refs[7 : 7 + blocks]
-            scr = refs[7 + blocks :]
+            dq_in, dk_in, dv_in, wq_ref, h1_ref, gains_ref, sums_ref, order_ref = refs[:8]
+            gqkv_ref, keep_ref, send_ref = refs[8:11]
+            gh_refs = refs[11 : 11 + pieces]
+            scr = refs[11 + pieces :]
         else:
             dq_out, dk_out, dv_out = refs[:3]
             scr = refs[3:]
@@ -432,20 +583,37 @@
                     gqkv_ref[rows, lq : 2 * lq] = unrotate(dk_scr[rows, :], rows).astype(BF)
                     gqkv_ref[rows, 2 * lq :] = dv_scr[rows, :].astype(BF)
                     gh = dot_t(gqkv_ref[rows, :], wq_ref[...])
-                    gh_refs[b][...] = gh.astype(gh_refs[b].dtype)
+                    if halves and b == 2:
+                        gh_refs[2][...] = gh[: chunk // 2, :].astype(BF)
+                        gh_refs[4][...] = gh[chunk // 2 :, :].astype(BF)
+                    else:
+                        gh_refs[b][...] = gh.astype(gh_refs[b].dtype)
                     n1 = n1 + fold8(gh * h1_ref[rows, :].astype(F32), jnp.sum)
-                n1_ref[...] = n1
+                lines = [
+                    jnp.sum(n1, axis=0, keepdims=True) / gains_ref[0:1, :],
+                    jnp.sum(sums_ref[0:8, :], axis=0, keepdims=True),
+                    jnp.sum(sums_ref[8:16, :], axis=0, keepdims=True),
+                    jnp.zeros((13, D), F32),
+                ]
+                lines = jnp.concatenate(lines, axis=0)
+                high = lines.astype(BF)
+                rest = (lines - high.astype(F32)).astype(BF)
+                lines = dot(high, order_ref[...]) + dot(rest, order_ref[...])
+                keep_ref[...] = lines[:, :384]
+                send_ref[...] = lines[:, 384:]
 
     ins = [pulls[e] for e in entries] + [by[e][1] for e in entries] + [by[e][2] for e in entries]
     ins += [q, k, v, cs, sn, kcol, qrow]
     if last:
-        ins += list(before) + [wq, h1]
+        ins += list(before) + [wq, h1, gains] + list(finish)
         out_shape = [
             jax.ShapeDtypeStruct((total, 3 * lq), BF),
-            jax.ShapeDtypeStruct((8, D), F32),
+            jax.ShapeDtypeStruct((16, 384), F32),
+            jax.ShapeDtypeStruct((16, 384), F32),
         ]
-        for b in range(blocks):
-            out_shape.append(jax.ShapeDtypeStruct((chunk, D), F32 if b == 0 else BF))
+        for b in range(pieces):
+            rows = chunk // 2 if halves and b in (2, 4) else chunk
+            out_shape.append(jax.ShapeDtypeStruct((rows, D), F32 if b == 0 else BF))
     else:
         out_shape = [
             jax.ShapeDtypeStruct((chunk, lq), BF),
@@ -480,34 +648,6 @@
     return lax.dot_general(a, b, (((0,), (0,)), ((), ())), preferred_element_type=F32)
 
 
-def reorder_columns(place, own, other, order):
-    width = own.shape[2]
-    out = order.shape[0]
-
-    def kernel(place_ref, own_ref, other_ref, order_ref, out_ref, scr):
-        d = place_ref[0]
-        scr[...] = jnp.zeros_like(scr)
-        for j in range(4):
-            scr[192 * j : 192 * j + 192, :width] = own_ref[d ^ j]
-            scr[192 * j : 192 * j + 192, 384 : 384 + width] = other_ref[d ^ j]
-        out_ref[...] = dot_t(scr[...], order_ref[...]).astype(BF)
-
-    return pl.pallas_call(
-        kernel,
-        name="reorder_columns",
-        grid_spec=pltpu.PrefetchScalarGridSpec(
-            num_scalar_prefetch=1,
-            grid=(1,),
-            in_specs=[whole(own.shape), whole(other.shape), whole(order.shape)],
-            out_specs=whole((D, out)),
-            scratch_shapes=[pltpu.VMEM((D, 768), BF)],
-        ),
-        out_shape=jax.ShapeDtypeStruct((D, out), BF),
-        compiler_params=params("arbitrary"),
-        cost_estimate=cost(1e9, 3e6),
-    )(place, own, other, order)
-
-
 def reorder_out(place, own, other, order):
     def kernel(place_ref, own_ref, other_ref, order_ref, out_ref, scr):
         d = place_ref[0]
@@ -536,10 +676,10 @@
     )(place, own, other, order)
 
 
-def qkv_weight(place, h1, gqkv, order):
+def qkv_weight(place, h1_t, gqkv, order):
     def kernel(place_ref, h_ref, g_ref, order_ref, keep_ref, send_ref):
         d = place_ref[0]
-        made = dot_first(h_ref[...], g_ref[...]).astype(BF)
+        made = dot(h_ref[...], g_ref[...]).astype(BF)
         made = dot(made, order_ref[...]).astype(BF)
         for j in range(4):
             rows = slice(192 * j, 192 * j + 192)
@@ -553,13 +693,13 @@
         grid_spec=pltpu.PrefetchScalarGridSpec(
             num_scalar_prefetch=1,
             grid=(1,),
-            in_specs=[whole(h1.shape), whole(gqkv.shape), whole(order.shape)],
+            in_specs=[whole(h1_t.shape), whole(gqkv.shape), whole(order.shape)],
             out_specs=[whole(shape.shape)] * 2,
         ),
         out_shape=[shape, shape],
         compiler_params=params("arbitrary"),
         cost_estimate=cost(2e9, 5e6),
-    )(place, h1, gqkv, order)
+    )(place, h1_t, gqkv, order)
 
 
 def out_weight(place, mixed, gproj, order):
@@ -595,19 +735,19 @@
 
 def output_projection(place, mixed, wout, x, gain):
     groups = len(mixed)
-    rows = x.shape[0]
+    rows = mixed[0].shape[0]
 
     def kernel(place_ref, *refs):
         m_refs = refs[:groups]
         w_ref, x_ref, gain_ref, res_ref, h2_ref = refs[groups:]
         z = place_ref[1]
-        total = x_ref[...].astype(F32)
+        total = x_ref[:rows, :].astype(F32)
         for k in range(groups):
             total = total + dot(m_refs[k][...], w_ref[lax.rem(z + (groups - k), groups)])
         res_ref[...] = total
         for at, size in cuts(rows, 64):
             xhat, _ = normed(res_ref[at : at + size, :])
-            h2_ref[at : at + size, :] = (xhat * gain_ref[...]).astype(BF)
+            h2_ref[at : at + size, :] = (xhat * gain_ref[1:2, :]).astype(BF)
 
     ins = list(mixed) + [wout, x, gain]
     return pl.pallas_call(
@@ -625,7 +765,7 @@
     )(place, *ins)
 
 
-def feed_forward(place, h2_own, h2_other, dy_own, dy_other, weights, bias):
+def feed_forward(place, h2_own, h2_other, cot, cot_in, weights, bias):
     rows = h2_own.shape[0]
     both = 2 * rows
     width = 384
@@ -639,13 +779,17 @@
         step = pl.program_id(0)
         d = place_ref[0]
         z = place_ref[1]
+        c = place_ref[2]
 
         @pl.when(step == 0)
         def _():
             h_scr[:rows, :] = ho_ref[...]
             h_scr[rows:, :] = hp_ref[...]
-            g_scr[:rows, :] = go_ref[...]
-            g_scr[rows:, :] = gp_ref[...]
+            local = rows // 2
+            g_scr[:local, :] = go_ref[c]
+            g_scr[local:rows, :] = gp_ref[c]
+            g_scr[rows : rows + local, :] = gp_ref[1 - c]
+            g_scr[rows + local :, :] = go_ref[1 - c]
             for at in range(0, both, 256):
                 part = slice(at, at + 256)
                 ht_scr[:, part] = h_scr[part, :].astype(F32).T.astype(BF)
@@ -669,7 +813,7 @@
 
         pre_scr[...] = dot(h_scr[...], w1_scr[...])
         ga_scr[...] = dot(g_scr[...], w2_scr[...])
-        bias_row = b_ref[0].astype(F32)
+        bias_row = b_ref[pl.ds(near, 1), :]
         total = jnp.zeros((8, width), F32)
         for at in range(0, both, 32):
             part = slice(at, at + 32)
@@ -683,7 +827,7 @@
             slope = (ga_scr[part, :] * rise).astype(BF)
             slope_scr[part, :] = slope
             total = total + fold8(slope.astype(F32), jnp.sum)
-        db_ref[0] = total
+        db_ref[0] = jnp.sum(total, axis=0, keepdims=True)
 
         out_now = dot_t(act_scr[...], w2_scr[...])
         gh_now = dot_t(slope_scr[...], w1_scr[...])
@@ -724,7 +868,7 @@
     def by_z(i, place_ref):
         return (lax.rem(i - place_ref[1] + 4, 4), 0, 0)
 
-    ins = [h2_own, h2_other, dy_own, dy_other] + list(weights)
+    ins = [h2_own, h2_other, cot, cot_in] + list(weights) + [bias]
     full = jax.ShapeDtypeStruct((2, 4, 192, width), BF)
     out_shape = [
         jax.ShapeDtypeStruct((rows, D), F32),
@@ -735,7 +879,7 @@
         full,
         full,
         full,
-        jax.ShapeDtypeStruct((4, 8, width), F32),
+        jax.ShapeDtypeStruct((4, 1, width), F32),
     ]
     return pl.pallas_call(
         kernel,
@@ -743,9 +887,9 @@
         grid_spec=pltpu.PrefetchScalarGridSpec(
             num_scalar_prefetch=1,
             grid=(4,),
-            in_specs=[whole(a.shape) for a in ins] + [pl.BlockSpec((1, 1, width), by_z)],
+            in_specs=[whole(a.shape) for a in ins],
             out_specs=[whole(o.shape) for o in out_shape[:-1]]
-            + [pl.BlockSpec((1, 8, width), by_z)],
+            + [pl.BlockSpec((1, 1, width), by_z)],
             scratch_shapes=[
                 pltpu.VMEM((both, D), BF),
                 pltpu.VMEM((both, D), BF),
@@ -765,24 +909,24 @@
         out_shape=out_shape,
         compiler_params=params("arbitrary"),
         cost_estimate=cost(7.2e9, 1.5e7),
-    )(place, *ins, bias)
-
-
-def residual_backward(place, gh_own, gh_in, residual, dy, gain, wout):
-    rows = dy.shape[0]
+    )(place, *ins)
+
+
+def residual_backward(place, gh_own, gh_in, residual, cot, cot_in, gain, wout):
+    rows, local = residual.shape[0], cot.shape[1]
     groups, hw = wout.shape[0], wout.shape[1]
 
-    def kernel(place_ref, gh_ref, gi_ref, res_ref, dy_ref, gain_ref, w_ref, *outs):
+    def kernel(place_ref, gh_ref, gi_ref, res_ref, ca_ref, cb_ref, gain_ref, w_ref, *outs):
         gres_ref, gproj_ref, vec_ref = outs[:3]
         gm_refs = outs[3:]
-        z = place_ref[1]
-        gain_row = gain_ref[...]
+        z, c = place_ref[1], place_ref[2]
+        gain_row = gain_ref[1:2, :]
         gsum = jnp.zeros((8, D), F32)
         bsum = jnp.zeros((8, D), F32)
         for at, size in cuts(rows, 32):
             part = slice(at, at + size)
             xhat, rstd = normed(res_ref[part, :])
-            dy_now = dy_ref[part, :].astype(F32)
+            dy_now = (ca_ref, cb_ref)[at // local][c, at % local : at % local + size, :].astype(F32)
             grad = gh_ref[part, :] + gi_ref[part, :].astype(F32)
             along = grad * xhat
             gsum = gsum + fold8(along, jnp.sum)
@@ -801,7 +945,7 @@
         for k in range(groups):
             gm_refs[k][...] = dot_t(gproj_ref[...], w_ref[lax.rem(z + k, groups)]).astype(BF)
 
-    ins = [gh_own, gh_in, residual, dy, gain, wout]
+    ins = [gh_own, gh_in, residual, cot, cot_in, gain, wout]
     out_shape = [
         jax.ShapeDtypeStruct((rows, D), F32),
         jax.ShapeDtypeStruct((rows, D), BF),
@@ -824,7 +968,7 @@
 
 
 def input_backward(terms, x, gain, gres):
-    rows = x.shape[0]
+    rows = gres.shape[0]
     count = len(terms)
 
     def kernel(*refs):
@@ -835,7 +979,7 @@
             for t in range(1, count):
                 grad = grad + refs[t][part, :].astype(F32)
             xhat, rstd = normed(x_ref[part, :].astype(F32))
-            u = grad * gain_ref[...]
+            u = grad * gain_ref[0:1, :]
             back = (
                 u
                 - jnp.mean(u, axis=1, keepdims=True)
@@ -919,56 +1063,30 @@
     s = lax.axis_index("seq")
     z = s // 2
     c = s % 2
-    place = jnp.stack([d, z]).astype(jnp.int32)
-    n1_w = D // n_seq
-    b1_w = FF // n_seq
-
-    x_loc = inputs[:, 0]
-    x_keep = pick(x_loc, c)
-    labels = jnp.stack([row_segment[:, 0], row_flag[:, 0], row_block[:, 0]], axis=1)
-    labels = labels.astype(BF).reshape(2, 3 * local)
-    vector = jnp.concatenate([norm1_scale, norm2_scale, b_fc2, b_fc1]).astype(BF)
-    vector = jnp.pad(vector, (0, D - vector.shape[0]))
-    lab_keep, lab_send = pick(labels, c), pick(labels, 1 - c)
-    extra = jnp.stack([jnp.pad(lab_send, (0, D - 3 * local)), vector])
-    message = jnp.concatenate([pick(x_loc, 1 - c), jnp.pad(extra, ((0, 14), (0, 0)))], axis=0)
-    swapped = links.core(message)
-    extra = jnp.stack(
-        [
-            jnp.concatenate([lab_keep, swapped[local, : 3 * local]]),
-            vector,
-            swapped[local + 1],
-        ]
-    )
-    x_ext = jnp.concatenate(
-        [x_keep, swapped[:local], jnp.pad(extra, ((0, 13), (0, 0)))], axis=0
+    place = jnp.stack([d, z, c]).astype(jnp.int32)
+    n_w, b_w = D // n_seq, FF // n_seq
+    cols = jnp.arange(768, dtype=jnp.int32)
+    side, at = cols // 384, cols % 384
+    out_order = order_matrix(
+        n_w * (2 * ((z + at // n_w) % nz) + (c ^ side)) + at % n_w, at < 384
     )
 
     def to_both(w):
         return jnp.where(c == 0, w[0], w[1]), jnp.where(c == 0, w[1], w[0])
 
-    cot = cotangent[:, 0]
-    if fast:
-        two = w_fc2.astype(BF).T.reshape(96, 2, 384)
-        two_keep, two_send = to_both((two[:, 0], two[:, 1]))
-        both = jnp.concatenate([cot.reshape(chunk, D), jnp.pad(two_send, ((0, 0), (0, 384)))])
-    else:
-        both = cot.reshape(chunk, D)
-    both_in = links.core(both)
-    cot_in = both_in[:chunk].reshape(2, local, D)
-    dy_own = jnp.concatenate([pick(cot, c), pick(cot_in, c)], axis=0)
-    dy_other = jnp.concatenate([pick(cot_in, 1 - c), pick(cot, 1 - c)], axis=0)
-
+    x_loc = inputs[:, 0]
+    labels = (row_segment[:, 0], row_flag[:, 0], row_block[:, 0])
+    vectors = tuple(v.reshape(1, -1) for v in (norm1_scale, norm2_scale, b_fc2, b_fc1))
+    came = links.core(message_rows(place, x_loc, labels, vectors))
+    x_ext = own_rows(place, x_loc, labels, vectors, came)
     if nz == 4:
         x_before = links.shift(x_ext, 1)
         x_after = links.shift(x_ext, -1)
         x_low = links.shift(x_before[:144], 1)
         x_high = links.shift(x_after[144:], -1)
         gathered = [[x_ext], [x_after], [x_low, x_high], [x_before]]
-        settled = (x_low, x_high)
     else:
         gathered = [[x_ext]] + [[links.shift(x_ext, -k)] for k in range(1, nz)]
-        settled = (x_ext,)
     arrays, plan, extras = [], [], []
     for k, pieces in enumerate(gathered):
         at = 0
@@ -977,42 +1095,29 @@
             plan.append((len(arrays), 0, k * chunk + at, rows))
             at += rows
             arrays.append(piece)
-        extras.append(pieces[-1][-16:])
-    extras = jnp.stack(extras)
-    labels_all = extras[:, 0].astype(F32).reshape(nz, 2, 3, local)
-    segment = labels_all[:, :, 0].reshape(-1)
-    flag = labels_all[:, :, 1].reshape(-1)
-    block = labels_all[:, :, 2].reshape(-1)
-    total = segment.shape[0]
-    start = segment * 4096.0
-    key_code = start + jnp.where(flag > 0.5, block, block + 2048.0)
-    low = start
-    high = start + block + flag
-    same = jnp.where(flag > 0.5, -1.0, key_code)
-    position = block * BLK + (jnp.arange(total, dtype=jnp.int32) % BLK).astype(F32)
-    qrow = jnp.pad(jnp.stack([low, high, same]), ((0, 5), (0, 0)))
-    kcol = jnp.pad(jnp.stack([key_code, position], axis=1), ((0, 0), (0, 6)))
+        extras.append((len(arrays) - 1, pieces[-1].shape[0] - 16))
     freq = np.tile(
         np.float32(10000.0) ** (np.float32(-2.0) * np.arange(32, dtype=np.float32) / HD), 4
     )
     freq = jnp.asarray(freq.astype(np.float32)[None, :])
-    vectors = extras[:, 1:3]
-    bias_rel = vectors[:, 0, 3 * n1_w : 3 * n1_w + b1_w]
-    vectors = jnp.roll(jnp.where(c == 0, vectors, vectors[:, ::-1]), z, axis=0)
-    gain_one = vectors[:, :, :n1_w].reshape(1, D).astype(F32)
-    gain_two = vectors[:, :, n1_w : 2 * n1_w].reshape(1, D).astype(F32)
-    bias_two = vectors[:, :, 2 * n1_w : 3 * n1_w].reshape(1, D).astype(F32)
+    cot = cotangent[:, 0]
 
     if fast:
-        cols = jnp.arange(768, dtype=jnp.int32)
-        half, at = cols // 384, cols % 384
+        two = w_fc2.astype(BF).T.reshape(96, 2, 384)
+        two_keep, two_send = to_both((two[:, 0], two[:, 1]))
+        two = jnp.concatenate(to_both((two_keep, links.core(two_send))), axis=0)
+        w12 = jnp.stack([w_fc1.astype(BF), two])
+        w_before = links.shift(w12, 1)
+        w_after = links.shift(w12, -1)
+        w1_two = links.shift(w_before[0], 1)
+        w2_two = links.shift(w_after[1], -1)
+        w1 = jnp.stack([w12[0], w_after[0], w1_two, w_before[0]])
+        w2 = jnp.stack([w12[1], w_after[1], w2_two, w_before[1]])
+
         qkv_order = order_matrix(
-            256 * (at // 96) + 96 * (c ^ half) + at % 96, at < 288
-        )
-        out_order = order_matrix(
-            192 * ((z + at // 96) % 4) + 96 * (c ^ half) + at % 96, at < 384
-        )
-        wq_parts = w_qkv.astype(BF)
+            256 * (cols % 384 // 96) + 96 * (c ^ side) + cols % 96, cols % 384 < 288
+        )
+        wq_parts = after(w_qkv.astype(BF), x_ext)
         parts = []
         for i in range(3):
             parts.append(
@@ -1028,22 +1133,14 @@
         )
         wq_own = jnp.stack([wq_own, links.flip(wq_own, 1)])
         wq_own = jnp.stack([wq_own, links.flip(wq_own, 2)]).reshape(4, 192, 384)
-        wq_in = links.core(wq_own)
-        wq = reorder_columns(place, wq_own, wq_in, qkv_order)
+        wq = (wq_own, links.core(wq_own))
         wo_own = jnp.concatenate([wq_own[j, :, 288:] for j in range(4)], axis=1)
 
-        two = jnp.concatenate(to_both((two_keep, both_in[chunk:, :384])), axis=0)
-        w12 = jnp.stack([w_fc1.astype(BF), two])
-        w_before = links.shift(w12, 1)
-        w_after = links.shift(w12, -1)
-        w1_two = links.shift(w_before[0], 1)
-        w2_two = links.shift(w_after[1], -1)
-        w1 = jnp.stack([w12[0], w_after[0], w1_two, w_before[0]])
-        w2 = jnp.stack([w12[1], w_after[1], w2_two, w_before[1]])
-        kcol = after(kcol, w1, w2)
+        x_ext_late, _ = lax.optimization_barrier((arrays[0], (w1, w2, wo_own)))
+        arrays[0] = x_ext_late
         w1_in = links.flip(w1, 2)
         w2_in = links.flip(w2, 1)
-        bias_one = bias_rel.reshape(4, 1, 384)
+        wo_all = [wo_own] + [links.shift(wo_own, -k) for k in range(1, 4)]
         ff_place = place
     else:
 
@@ -1054,7 +1151,7 @@
         wq = everywhere(w_qkv).reshape(D, 3, D)
         wq = jnp.pad(wq, ((0, 0), (0, 0), (0, nz * hw - D)))
         wq = lax.dynamic_slice_in_dim(wq, z * hw, hw, 2)
-        wq = jnp.pad(wq, ((0, 0), (0, 0), (0, lq - hw))).reshape(D, 3 * lq)
+        wq = (jnp.pad(wq, ((0, 0), (0, 0), (0, lq - hw))).reshape(D, 3 * lq),)
         wout = jnp.pad(everywhere(w_out), ((0, nz * hw - D), (0, 0))).reshape(nz, hw, D)
         w1 = lax.dynamic_slice_in_dim(everywhere(w_fc1), c * (FF // 2), FF // 2, 1)
         w1 = w1.reshape(2, 2, 192, 4, 384).transpose(3, 1, 0, 2, 4)
@@ -1062,86 +1159,83 @@
         w2 = w2.reshape(2, 2, 384, 4, 192).transpose(3, 1, 0, 4, 2)
         w1, w2 = w1.transpose(1, 2, 0, 3, 4), w2.transpose(2, 1, 0, 3, 4)
         weights = (w1[0], w1[1], w2[0], w2[1])
-        bias_all = vectors[:, :, 3 * n1_w : 3 * n1_w + b1_w].reshape(FF)
-        bias_one = lax.dynamic_slice_in_dim(bias_all, c * (FF // 2), FF // 2, 0).reshape(4, 1, 384)
-        ff_place = jnp.zeros((2,), jnp.int32)
+        bias_all = lax.all_gather(b_fc1.astype(BF), "seq", axis=0, tiled=True).astype(F32)
+        bias = lax.dynamic_slice_in_dim(bias_all, c * (FF // 2), FF // 2, 0).reshape(4, 384)
+        bias = jnp.pad(bias, ((0, 4), (0, 0)))
+        ff_place = jnp.stack([0 * d, 0 * z, c]).astype(jnp.int32)
+    cot_in = links.core(after(cot, x_ext))
 
     far = sorted(range(1, nz), key=lambda k: -min(k, nz - k))
     first = far[: nz // 2]
     rest = far[nz // 2 :] + [0]
     saved, by = attention_first(
-        arrays, plan, kcol, qrow, freq, wq, gain_one, heads, chunk, first
+        place, arrays, plan, extras, freq, wq, out_order, heads, chunk, first, (n_w, b_w)
     )
-    mixed = {k: links.shift(by[k][0], k) for k in first}
-    rest_in = saved
+    h1, gains = saved[0], saved[9]
+    rest_in = tuple(saved[i] for i in (1, 2, 4, 7, 8))
     if fast:
-        w1_in, w2_in, wo_own, _ = lax.optimization_barrier((w1_in, w2_in, wo_own, by[first[0]]))
+        bias = saved[11]
+        w1_in, w2_in, wo_all, _ = lax.optimization_barrier((w1_in, w2_in, wo_all, h1))
         w1a = jnp.stack([w1, w1_in])
         w2a = jnp.stack([w2, w2_in])
+        wo_all = jnp.stack(wo_all)
+        wo_in = links.core(wo_all)
         w1b = links.flip(w1a, 1)
         w2b = links.flip(w2a, 2)
         weights = (w1a, w1b, w2a, w2b)
-        wo_own = jnp.stack([wo_own] + [links.shift(wo_own, -k) for k in range(1, 4)])
-        rest_in = after(tuple(saved), w1a, w2a)
-    by_rest = attention_rest(rest_in, kcol, qrow, heads, chunk, rest)
-    by = {**by, **by_rest}
+        rest_in = after(rest_in, w1a, w2a, wo_all)
+    mixed = {k: links.shift(by[k][0], k) for k in first}
+    by = {**by, **attention_rest(rest_in, heads, chunk, rest)}
     for k in rest:
         mixed[k] = links.shift(by[k][0], k) if k else by[k][0]
     mixed = [mixed[k] for k in range(nz)]
+    h1_t = after(h1, by[0][0]).T
     if fast:
-        wo_own = after(wo_own, by[0][0])
-        wout = reorder_out(place, wo_own, links.core(wo_own), out_order)
-    x_own = x_ext[:chunk]
-    residual, h2 = output_projection(place, mixed, wout, x_own, gain_two)
+        wout = reorder_out(place, after(wo_all, by[0][0]), wo_in, out_order)
+    residual, h2 = output_projection(place, mixed, wout, after(x_ext, h1_t), gains)
     h2_in = links.core(h2)
     (out_own, out_other, gh_own, gh_other, dw1a, dw1b, dw2a, dw2b, db1) = feed_forward(
-        ff_place, h2, h2_in, dy_own, dy_other, weights, bias_one
+        ff_place, h2, h2_in, cot, cot_in, weights, bias
     )
     gh_in = links.core(gh_other)
+    out_in = links.core(out_other)
+    gres, gproj, sums, gmixed = residual_backward(
+        place, gh_own, gh_in, residual, cot, cot_in, gains, wout
+    )
     if fast:
         dw1_in = links.flip(dw1b, 1)
         dw2_in = links.flip(dw2b, 2)
-    gres, gproj, sums, gmixed = residual_backward(
-        place, gh_own, gh_in, residual, dy_own, gain_two, wout
-    )
     pulled = [gmixed[0]] + [links.shift(gmixed[k], k) for k in range(1, nz)]
     pulled = [pulled[(nz - k) % nz] for k in range(nz)]
-    part = attention_backward(
-        pulled, by, saved, kcol, qrow, wq, heads, chunk, [0], None, False
-    )
-    grad_gain_two = jnp.sum(sums[:8], axis=0)
-    grad_bias_two = jnp.sum(sums[8:], axis=0)
-    grad_bias_one = jnp.sum(db1, axis=1)
+    part = attention_backward(pulled, by, saved, heads, chunk, [0], None, None)
+    out_rows = (residual + out_own + out_in.astype(F32) + gains[2:3]).astype(BF)
+    rows_in = links.core(out_rows[local:])
     if fast:
         wo_keep, wo_send = out_weight(place, mixed, gproj, out_order)
         wo_came = links.core(wo_send)
-    out_other = after(out_other, part)
-    out_in = links.core(out_other)
-    out_rows = (residual + out_own + out_in.astype(F32) + bias_two).astype(BF)
-    rows_in = links.core(out_rows[local:])
+        dwo = [
+            add_low(wo_keep[..., 96 * k : 96 * k + 96], wo_came[..., 96 * k : 96 * k + 96])
+            for k in range(4)
+        ]
+        part, _ = lax.optimization_barrier((part, (dwo, out_rows)))
+        dwo = [dwo[0]] + [links.shift(dwo[k], k) for k in range(1, 4)]
+    made = attention_backward(
+        pulled, by, saved, heads, chunk, list(range(1, nz)), part, (sums, out_order)
+    )
     if fast:
-        dwo = add_low(wo_keep, wo_came)
-        part, _ = lax.optimization_barrier((part, (dwo, out_rows, grad_bias_one, grad_bias_two)))
-        dwo = sum(
-            [dwo[..., :96].astype(F32)]
-            + [
-                links.shift(dwo[..., 96 * k : 96 * k + 96], k).astype(F32)
-                for k in range(1, 4)
-            ]
-        )
-    made = attention_backward(
-        pulled, by, saved, kcol, qrow, wq, heads, chunk, list(range(1, nz)), part, True
-    )
-    gqkv, n1_sum, gh1 = made[0], made[1], made[2:]
+        made, dwo, dw1_in, dw2_in, rows_in = lax.optimization_barrier(
+            (made, dwo, dw1_in, dw2_in, rows_in)
+        )
+    gqkv, vec_keep, vec_send, gh1 = made[0], made[1], made[2], made[3:]
     if nz == 4:
-        low_in = links.shift(gh1[2][:local], 1)
-        high_in = links.shift(gh1[2][local:], -1)
+        low_in = links.shift(gh1[2], 1)
+        high_in = links.shift(gh1[4], -1)
         up = jnp.concatenate([add_low(gh1[1][:local], low_in), gh1[1][local:]], axis=0)
         down = jnp.concatenate([gh1[3][:local], add_low(gh1[3][local:], high_in)], axis=0)
         terms = [gh1[0], links.shift(up, 1), links.shift(down, -1)]
     else:
         terms = [gh1[0]] + [links.shift(gh1[k], k) for k in range(1, nz)]
-    grad_rows = input_backward(terms, x_own, gain_one, gres)
+    grad_rows = input_backward(terms, x_ext, gains, gres)
     grad_in = links.core(grad_rows[local:])
 
     def by_micro(own, other):
@@ -1149,17 +1243,33 @@
 
     outputs = by_micro(out_rows[:local], rows_in)
     input_grad = by_micro(grad_rows[:local], grad_in)
-
-    grad_gain_one = jnp.sum(n1_sum, axis=0) / gain_one[0]
+    vec = vec_keep + links.core(vec_send)
 
     if fast:
-        wq_keep, wq_send = qkv_weight(place, saved[0], after(gqkv, low_in, high_in), qkv_order)
+        dw1_in = links.flip(add_low(dw1a[1], dw1_in[1]), 2), dw1_in[0]
+        dw2_in = links.flip(add_low(dw2a[1], dw2_in[1]), 1), dw2_in[0]
+        wq_keep, wq_send = qkv_weight(place, h1_t, after(gqkv, low_in, high_in), qkv_order)
+        dwo = sum(t.astype(F32) for t in dwo)
         joint = jnp.concatenate(
             [add_low(wq_keep, links.core(wq_send)), dwo.astype(BF)], axis=2
         )
-        joint = joint.reshape(2, 2, 192, 384)
-        joint = add_low(joint[0], links.flip(joint[1], 2))
-        joint = joint[0].astype(F32) + links.flip(joint[1], 1).astype(F32)
+        joint = joint.reshape(2, 384, 384)
+        vec = jnp.concatenate([vec[:3], db1[:, 0], jnp.zeros((9, 384), F32)], axis=0)
+        came = links.flip(jnp.concatenate([joint[1], vec.astype(BF)], axis=0), 2)
+        joint = add_low(joint[0], came[:384]).reshape(2, 192, 384)
+        vec = vec + came[384:].astype(F32)
+        came = links.flip(jnp.concatenate([joint[1], vec.astype(BF)], axis=0), 1)
+        joint = joint[0].astype(F32) + came[:192].astype(F32)
+        vec = vec + came[192:].astype(F32)
+        vec = [
+            jnp.concatenate(
+                [jnp.pad(vec[:3, 96 * k : 96 * k + 96], ((0, 0), (0, 288))), vec[3 + k : 4 + k]],
+                axis=0,
+            )
+            for k in range(4)
+        ]
+        vec = sum([vec[0]] + [links.shift(vec[k], k) for k in range(1, 4)])
+        vecs = (vec[0, :96], vec[1, :96], vec[3], vec[2, :96])
         g_out = joint[:, 288:]
         third = jnp.stack([joint[:, 96 * t : 96 * t + 96] for t in range(3)])
         g_qkv = jnp.concatenate(
@@ -1173,9 +1283,6 @@
             ],
             axis=1,
         )
-        dw1_in, dw2_in, _ = lax.optimization_barrier((dw1_in, dw2_in, gqkv))
-        dw1_in = links.flip(add_low(dw1a[1], dw1_in[1]), 2), dw1_in[0]
-        dw2_in = links.flip(add_low(dw2a[1], dw2_in[1]), 1), dw2_in[0]
         dw1 = dw1a[0].astype(F32) + dw1_in[0].astype(F32) + dw1_in[1].astype(F32)
         dw2 = dw2a[0].astype(F32) + dw2_in[0].astype(F32) + dw2_in[1].astype(F32)
         low_in = links.shift(dw1[2].astype(BF), 1)
@@ -1187,26 +1294,14 @@
         dw = jnp.stack([dw1[0], dw2[0]]) + up_in + down_in
         g_fc1 = dw[0]
         keep, send = to_both((dw[1, :96], dw[1, 96:]))
-        came = links.core(send)
-        g_fc2 = jnp.concatenate(to_both((keep, came)), axis=1).T
-        three = jnp.stack([grad_gain_one, grad_gain_two, grad_bias_two]).reshape(3, 4, 2, 96)
-        three = jnp.roll(three, -z, axis=1)
-        keep, send = to_both((three[:, :, 0], three[:, :, 1]))
-        three = (keep + links.core(send)).transpose(1, 0, 2).reshape(4, 288)
-        vec = jnp.concatenate([three, grad_bias_one, jnp.zeros((4, 352), F32)], axis=1)
-        vec = vec.reshape(4, 8, 128)
-        vec = sum([vec[0]] + [links.shift(vec[k], k) for k in range(1, 4)])
-        for bit in (1, 2):
-            vec = vec + links.flip(vec, bit)
-        vec = vec.reshape(1024)
-        vecs = (vec[:96], vec[96:192], vec[288:672], vec[192:288])
+        g_fc2 = jnp.concatenate(to_both((keep, links.core(send))), axis=1).T
     else:
 
         def owned(w):
             w = lax.psum_scatter(w.astype(BF), "seq", scatter_dimension=1, tiled=True)
             return lax.psum_scatter(w, "dp", scatter_dimension=0, tiled=True).astype(F32)
 
-        dwq = jnp.einsum("rd,rj->dj", saved[0], gqkv, preferred_element_type=F32)
+        dwq = jnp.einsum("rd,rj->dj", h1, gqkv, preferred_element_type=F32)
         spread = jnp.zeros((D, 3, nz * hw), F32)
         spread = lax.dynamic_update_slice_in_dim(
             spread, dwq.reshape(D, 3, lq)[..., :hw], z * hw, 2
@@ -1228,12 +1323,15 @@
         )
         g_fc2 = owned(full)
         bias_full = lax.dynamic_update_slice_in_dim(
-            jnp.zeros((FF,), F32), grad_bias_one.reshape(-1), c * (FF // 2), 0
-        )
-        vecs = tuple(
-            lax.psum(lax.psum_scatter(v, "seq", scatter_dimension=0, tiled=True), "dp")
-            for v in (grad_gain_one, grad_gain_two, bias_full, grad_bias_two)
-        )
+            jnp.zeros((FF,), F32), db1.reshape(-1), c * (FF // 2), 0
+        )
+        bias_full = lax.psum(
+            lax.psum_scatter(bias_full, "seq", scatter_dimension=0, tiled=True), "dp"
+        )
+        vec = vec[:3].reshape(3, nz, n_w)
+        vec = sum([vec[:, 0]] + [links.shift(vec[:, k], k) for k in range(1, nz)])
+        vec = lax.psum(vec, "dp")
+        vecs = (vec[0], vec[1], bias_full, vec[2])
 
     return (
         outputs,

time: 324 us -> 297 us (0.917)
  other arithmetic: 30.9 us -> 17.4 us
  starting transfers between devices: 84.8 us -> 76.1 us
  local copies, waits for them, and re-layouts: 21 us -> 13.2 us
  Pallas kernels: 102 us -> 107 us
    ppermute x14 -> x12, waiting for transfers between devices: 15.2 us -> 4.08 us  [flip(): return lax.ppermute(v, 'dp', [(i, i ^ bit) for i in range(self.n_dp)])]
    ppermute x31, waiting for transfers between devices: 61 us -> 69.8 us  [shift(): lax.ppermute(v, 'seq', [(s, 2 * ((s // 2 + k) % n) + s % 2) for s in rang...]
    another operation x16 -> x4, other arithmetic: 7.27 us -> 2.25 us
    concatenate x11 -> x5, other arithmetic: 4.19 us -> 0.07 us  [the longest x1 0.03 us: per_device(): came = links.flip(jnp.concatenate([joint[1], vec.astype(BF)], axis=0), 2)]
    ppermute x14 -> x12, starting transfers between devices: 17.4 us -> 13.8 us  [flip(): return lax.ppermute(v, 'dp', [(i, i ^ bit) for i in range(self.n_dp)])]
    slice x2, local copies, waits for them, and re-layouts: 3.41 us -> 0.08 us  [per_device(): w2 = jnp.stack([w12[1], w_after[1], w2_two, w_before[1]])]
    pallas_call x2 -> x3, Pallas kernels: 18.8 us -> 21.8 us  [the longest x1 16.6 us: attention_first(): pl.pallas_call(kernel, name='attention_first', grid_spec=pltpu.PrefetchSc...]
  transfers between devices with their start and end apart: 64 -> 63, of which waited for: 24 -> 19; matrix products, arithmetic and copies ran while one was open for 14% -> 8% of each run, Pallas kernels for 21% -> 27%
where the time goes in v1:
time: 297 us; the launch traced here: 296 us
  Pallas kernels  107 us (36%)
  waiting for transfers between devices  81.1 us (27%)
  starting transfers between devices  76.1 us (26%)
  other arithmetic  17.4 us (6%)
  local copies, waits for them, and re-layouts  13.2 us (4%)
    ppermute x31, waiting for transfers between devices, shift(): lax.ppermute(v, 'seq', [(s, 2 * ((s // 2 + k) % n) + s % 2) for s in rang...  69.8 us
    ppermute x31, starting transfers between devices, shift(): lax.ppermute(v, 'seq', [(s, 2 * ((s // 2 + k) % n) + s % 2) for s in rang...  46.2 us
    pallas_call x2, Pallas kernels, attention_backward(): pl.pallas_call(kernel, name='attention_backward_last' if last else 'atten...  27.1 us
    pallas_call x1, Pallas kernels, feed_forward(): pl.pallas_call(kernel, name='feed_forward', grid_spec=pltpu.PrefetchScala...  20.9 us
    pallas_call x1, Pallas kernels, attention_first(): pl.pallas_call(kernel, name='attention_first', grid_spec=pltpu.PrefetchSc...  16.6 us
    ppermute x12, starting transfers between devices, flip(): return lax.ppermute(v, 'dp', [(i, i ^ bit) for i in range(self.n_dp)])  13.8 us
    ppermute x3, starting transfers between devices, per_device(): lax.ppermute(wq_parts[:, 96 * i:96 * i + 96], 'seq', [(q, (3 * q + i) % 8...  9.42 us
    pallas_call x1, Pallas kernels, attention_rest(): pl.pallas_call(kernel, name='attention_rest', grid=(len(entries),), in_sp...  8.36 us
  transfers between devices with their start and end apart: 63, of which 19 were waited for; matrix products, arithmetic and copies ran while one was open for 8% of the time, Pallas kernels for 27%

profile of v1, /device:TPU:0, one launch (start us, length us, event | category | flops | bytes accessed | tf_op | source)
XLA Modules:
  0.0 296.3 jit_solution(4981209984891113214)
XLA Ops:
  12.6 4.1 %collective-permute-start.7 = (bf16[192,96]{1,0:T(8,128)(2,1)S(1)}, bf16[192,96]{1,0:T(8,128)(2,1)S(1)}, u32[]{:S(2)}, u32[]{:S(2)}) collective-permute-start(bf16[192,96]{1,0:T(8,128)(2,1)S(1)} %get-tuple-element.246), channel_id=1, source_target_pairs={{0,1},{1,4},{2,7},{3,2},{4,5},{5,0},{6,3},{7,6},{8,9},{9,12},{10,1... | collective-permute-start | bytes 110600 | tf_op jit(solution)/shard_map/ppermute | solution.py:1124
  16.7 4.5 %collective-permute-start.8 = (bf16[192,96]{1,0:T(8,128)(2,1)S(1)}, bf16[192,96]{1,0:T(8,128)(2,1)S(1)}, u32[]{:S(2)}, u32[]{:S(2)}) collective-permute-start(bf16[192,96]{1,0:T(8,128)(2,1)S(1)} %get-tuple-element.245), channel_id=1, source_target_pairs={{0,2},{1,5},{2,0},{3,3},{4,6},{5,1},{6,4},{7,7},{8,10},{9,13},{10,... | collective-permute-start | bytes 110600 | tf_op jit(solution)/shard_map/ppermute | solution.py:1124
  28.2 3.3 %collective-permute-start.11 = (bf16[272,768]{1,0:T(8,128)(2,1)S(1)}, bf16[272,768]{1,0:T(8,128)(2,1)S(1)}, u32[]{:S(2)}, u32[]{:S(2)}) collective-permute-start(bf16[272,768]{1,0:T(8,128)(2,1)S(1)} %copy-done), channel_id=1, source_target_pairs={{0,6},{1,7},{2,0},{3,1},{4,2},{5,3},{6,4},{7,5},{8,14},{9,15},{10,... | collective-permute-start | bytes 1253384 | tf_op jit(solution)/shard_map/ppermute | solution.py:1027
  33.3 12.0 %collective-permute-done.2 = bf16[2,192,384]{2,1,0:T(8,128)(2,1)S(1)} collective-permute-done((bf16[2,192,384]{2,1,0:T(8,128)(2,1)S(1)}, bf16[2,192,384]{2,1,0:T(8,128)(2,1)S(1)}, u32[]{:S(2)}, u32[]{:S(2)}) %collective-permute-start.2) | collective-permute-done | bytes 294944 | tf_op jit(solution)/shard_map/ppermute | solution.py:1027
  47.7 10.6 %collective-permute-done.5 = bf16[192,384]{1,0:T(8,128)(2,1)S(1)} collective-permute-done((bf16[192,384]{1,0:T(8,128)(2,1)S(1)}, bf16[192,384]{1,0:T(8,128)(2,1)S(1)}, u32[]{:S(2)}, u32[]{:S(2)}) %collective-permute-start.5) | collective-permute-done | bytes 147488 | tf_op jit(solution)/shard_map/ppermute | solution.py:1027
  63.5 3.0 collective-permute-start.14
  66.8 7.3 %collective-permute-done.14.refs_3_ = bf16[128,768]{1,0:T(8,128)(2,1)S(1)} collective-permute-done((bf16[128,768]{1,0:T(8,128)(2,1)S(1)}, bf16[128,768]{1,0:T(8,128)(2,1)S(1)}, u32[]{:S(2)}, u32[]{:S(2)}) %collective-permute-start.14) | collective-permute-done | bytes 196640 | tf_op jit(solution)/shard_map/ppermute | solution.py:1027
  79.1 16.6 %attention_first.1 = (bf16[1024,768]{1,0:T(8,128)(2,1)}, bf16[1024,256]{1,0:T(8,128)(2,1)}, bf16[1024,256]{1,0:T(8,128)(2,1)}, bf16[1024,256]{1,0:T(8,128)(2,1)}...) custom-call(s32[3]{0:T(128)} %pad_add_fusion.place_ref, ...), custom_call_target="tpu_custom_call" | custom-call | flops 8000000 | bytes 8000 | tf_op jit(solution)/shard_map/attention_first/pallas_call | solution.py:422
  99.3 8.4 %attention_rest.1 = (bf16[256,192]{1,0:T(8,128)(2,1)}, f32[256,256]{1,0:T(8,128)}, f32[8,256]{1,0:T(8,128)}, bf16[256,192]{1,0:T(8,128)(2,1)}, f32[256,256]{1,0:T(8,128)}, /*index=5*/f32[8,256]{1,0:T(8,128)}) custom-call(bf16[1024,256]{1,0:T(8,128)(2,1)} %get-tuple-element.117.q_ref.refs_3_.refs_9_, ...), custom_call_target="tpu_custom_call" | custom-call | flops 5000000 | bytes 4000 | tf_op jit(solution)/shard_map/attention_rest/pallas_call | solution.py:458
  107.6 3.2 %collective-permute-start.23 = (bf16[256,192]{1,0:T(8,128)(2,1)}, bf16[256,192]{1,0:T(8,128)(2,1)S(1)}, u32[]{:S(2)}, u32[]{:S(2)}) collective-permute-start(bf16[256,192]{1,0:T(8,128)(2,1)} %get-tuple-element.125), channel_id=1, source_target_pairs={{0,6},{1,7},{2,0},{3,1},{4,2},{5,3},{6,4},{7,5},{8,14},{9,15},{10,... | collective-permute-start | bytes 294920 | tf_op jit(solution)/shard_map/ppermute | solution.py:1027
  114.1 5.8 %reorder_out.1.refs_4_.w_ref = bf16[4,192,768]{2,1,0:T(8,128)(2,1)} custom-call(s32[3]{0:T(128)} %pad_add_fusion.place_ref, bf16[4,192,384]{2,1,0:T(8,128)(2,1)} %copy-done.5, bf16[4,192,384]{2,1,0:T(8,128)(2,1)} %copy-done.16, bf16[768,768]{1,0:T(8,128)(2,1)} %select_convert_fusion.1.refs_6_.order_ref.refs_5_.refs_23_), custom_call_target="tpu_custom_call" | custom-call | flops 1000000 | bytes 3000 | tf_op jit(solution)/shard_map/reorder_out/pallas_call | solution.py:663
  119.9 3.9 %collective-permute-done.22.refs_2_ = bf16[256,192]{1,0:T(8,128)(2,1)} collective-permute-done((bf16[256,192]{1,0:T(8,128)(2,1)}, bf16[256,192]{1,0:T(8,128)(2,1)}, u32[]{:S(2)}, u32[]{:S(2)}) %collective-permute-start.22) | collective-permute-done | bytes 98336 | tf_op jit(solution)/shard_map/ppermute | solution.py:1027
  123.8 3.9 %output_projection.1 = (f32[256,768]{1,0:T(8,128)}, bf16[256,768]{1,0:T(8,128)(2,1)}) custom-call(s32[3]{0:T(128)} %pad_add_fusion.place_ref, bf16[256,192]{1,0:T(8,128)(2,1)} %get-tuple-element.122.refs_0_, bf16[256,192]{1,0:T(8,128)(2,1)} %collective-permute-done.21.refs_1_, bf16[256,192]{1,0:T(8,128)(2,1)} %collective-permute-done.22.refs_2_, ...), custom_call_target="tpu_custom_call" | custom-call | flops 1000000 | bytes 3000 | tf_op jit(solution)/shard_map/output_projection/pallas_call | solution.py:753
  130.4 20.9 %feed_forward.1 = (f32[256,768]{1,0:T(8,128)}, bf16[256,768]{1,0:T(8,128)(2,1)}, f32[256,768]{1,0:T(8,128)}, bf16[256,768]{1,0:T(8,128)(2,1)}, bf16[2,4,192,384]...) custom-call(s32[3]{0:T(128)} %pad_add_fusion.place_ref, ...), custom_call_target="tpu_custom_call" | custom-call | flops 7200000 | bytes 15000 | tf_op jit(solution)/shard_map/feed_forward/pallas_call | solution.py:884
  155.3 4.7 %residual_backward.1 = (f32[256,768]{1,0:T(8,128)}, bf16[256,768]{1,0:T(8,128)(2,1)}, f32[16,768]{1,0:T(8,128)}, bf16[256,192]{1,0:T(8,128)(2,1)}, bf16[256,192]...) custom-call(s32[3]{0:T(128)} %pad_add_fusion.place_ref, f32[256,768]{1,0:T(8,128)} %get-tuple-element.136.gh_ref, ...), custom_call_target="tpu_custom_call" | custom-call | flops 1000000 | bytes 4000 | tf_op jit(solution)/shard_map/residual_backward/pallas_call | solution.py:954
  160.0 4.9 %out_weight.1 = (bf16[4,192,384]{2,1,0:T(8,128)(2,1)}, bf16[4,192,384]{2,1,0:T(8,128)(2,1)}) custom-call(s32[3]{0:T(128)} %pad_add_fusion.place_ref, bf16[256,192]{1,0:T(8,128)(2,1)} %get-tuple-element.122.refs_0_, bf16[256,192]{1,0:T(8,128)(2,1)} %collective-permute-done.21.refs_1_, bf16[256,192]{1,0:T(8,128)(2,1)} %collective-permute-done.22.refs_2_, ...), custom_call_target="tpu_custom_call" | custom-call | flops 1000000 | bytes 4000 | tf_op jit(solution)/shard_map/out_weight/pallas_call | solution.py:721
  167.9 4.3 %collective-permute-done.31.refs_0_ = bf16[256,192]{1,0:T(8,128)(2,1)S(1)} collective-permute-done((bf16[256,192]{1,0:T(8,128)(2,1)S(1)}, bf16[256,192]{1,0:T(8,128)(2,1)S(1)}, u32[]{:S(2)}, u32[]{:S(2)}) %collective-permute-start.31) | collective-permute-done | bytes 98336 | tf_op jit(solution)/shard_map/ppermute | solution.py:1027
  172.8 7.0 %collective-permute-done.32.refs_1_ = bf16[256,192]{1,0:T(8,128)(2,1)S(1)} collective-permute-done((bf16[256,192]{1,0:T(8,128)(2,1)S(1)}, bf16[256,192]{1,0:T(8,128)(2,1)S(1)}, u32[]{:S(2)}, u32[]{:S(2)}) %collective-permute-start.32) | collective-permute-done | bytes 98336 | tf_op jit(solution)/shard_map/ppermute | solution.py:1027
  179.9 2.7 collective-permute-start.36
  185.5 7.6 %attention_backward_own.1 = (bf16[256,256]{1,0:T(8,128)(2,1)}, f32[1024,256]{1,0:T(8,128)}, f32[1024,256]{1,0:T(8,128)}) custom-call(bf16[256,192]{1,0:T(8,128)(2,1)} %get-tuple-element.150.refs_0_, f32[256,256]{1,0:T(8,128)} %get-tuple-element.151.refs_1_, f32[8,256]{1,0:T(8,128)} %get-tuple-element.152.refs_2_, ...), custom_call_target="tpu_custom_call" | custom-call | flops 3000000 | bytes 10000 | tf_op jit(solution)/shard_map/attention_backward_own/pallas_call | solution.py:623
  193.1 19.6 %attention_backward_last.1 = (bf16[1024,768]{1,0:T(8,128)(2,1)}, f32[16,384]{1,0:T(8,128)}, f32[16,384]{1,0:T(8,128)}, f32[256,768]{1,0:T(8,128)}, bf16[256,768]...) custom-call(bf16[256,192]{1,0:T(8,128)(2,1)} %copy-done.32, ...), custom_call_target="tpu_custom_call" | custom-call | flops 9000000 | bytes 10000 | tf_op jit(solution)/shard_map/attention_backward_last/pallas_call | solution.py:623
  216.6 3.1 %collective-permute-start.43 = (bf16[128,768]{1,0:T(8,128)(2,1)S(1)}, bf16[128,768]{1,0:T(8,128)(2,1)}, u32[]{:S(2)}, u32[]{:S(2)}) collective-permute-start(bf16[128,768]{1,0:T(8,128)(2,1)S(1)} %copy-done.40), channel_id=1, source_target_pairs={{0,6},{1,7},{2,0},{3,1},{4,2},{5,3},{6,4},{7,5},{8,14},{9,15},{10,... | collective-permute-start | bytes 589832 | tf_op jit(solution)/shard_map/ppermute | solution.py:1027
  225.8 6.4 %qkv_weight.1 = (bf16[4,192,288]{2,1,0:T(8,128)(2,1)}, bf16[4,192,288]{2,1,0:T(8,128)(2,1)}) custom-call(s32[3]{0:T(128)} %pad_add_fusion.place_ref, bf16[768,1024]{1,0:T(8,128)(2,1)} %bitcast.147, bf16[1024,768]{1,0:T(8,128)(2,1)} %get-tuple-element.185.g_ref, bf16[768,768]{1,0:T(8,128)(2,1)} %select_convert_fusion.order_ref), custom_call_target="tpu_custom_call" | custom-call | flops 2000000 | bytes 5000 | tf_op jit(solution)/shard_map/qkv_weight/pallas_call | solution.py:690
  233.2 2.7 collective-permute-start.44
  238.8 2.9 collective-permute-start.60
  241.7 3.8 %collective-permute-done.44.refs_2_ = bf16[256,768]{1,0:T(8,128)(2,1)} collective-permute-done((bf16[256,768]{1,0:T(8,128)(2,1)S(1)}, bf16[256,768]{1,0:T(8,128)(2,1)}, u32[]{:S(2)}, u32[]{:S(2)}) %collective-permute-start.44) | collective-permute-done | bytes 393248 | tf_op jit(solution)/shard_map/ppermute | solution.py:1027
  245.5 10.1 %collective-permute-done.42.refs_1_ = bf16[256,768]{1,0:T(8,128)(2,1)} collective-permute-done((bf16[256,768]{1,0:T(8,128)(2,1)S(1)}, bf16[256,768]{1,0:T(8,128)(2,1)}, u32[]{:S(2)}, u32[]{:S(2)}) %collective-permute-start.42) | collective-permute-done | bytes 393248 | tf_op jit(solution)/shard_map/ppermute | solution.py:1027
  255.7 3.1 %input_backward.1 = bf16[256,768]{1,0:T(8,128)(2,1)} custom-call(f32[256,768]{1,0:T(8,128)} %get-tuple-element.175.refs_0_, bf16[256,768]{1,0:T(8,128)(2,1)} %collective-permute-done.42.refs_1_, bf16[256,768]{1,0:T(8,128)(2,1)} %collective-permute-done.44.refs_2_, bf16[272,768]{1,0:T(8,128)(2,1)} %own_rows.1.refs_0_.refs_5_.refs_3_, ...), custom_call_target="tpu_custom_call" | custom-call | flops 100000 | bytes 3000 | tf_op jit(solution)/shard_map/input_backward/pallas_call | solution.py:991
  262.9 2.7 collective-permute-start.61
  266.4 4.0 %collective-permute-done.48 = bf16[400,384]{1,0:T(8,128)(2,1)S(1)} collective-permute-done((bf16[400,384]{1,0:T(8,128)(2,1)S(1)}, bf16[400,384]{1,0:T(8,128)(2,1)S(1)}, u32[]{:S(2)}, u32[]{:S(2)}) %collective-permute-start.48) | collective-permute-done | bytes 307232 | tf_op jit(solution)/shard_map/ppermute | solution.py:1023
  273.3 4.7 %collective-permute-done.61 = bf16[2,192,384]{2,1,0:T(8,128)(2,1)S(1)} collective-permute-done((bf16[2,192,384]{2,1,0:T(8,128)(2,1)S(1)}, bf16[2,192,384]{2,1,0:T(8,128)(2,1)S(1)}, u32[]{:S(2)}, u32[]{:S(2)}) %collective-permute-start.61) | collective-permute-done | bytes 294944 | tf_op jit(solution)/shard_map/ppermute | solution.py:1027
  291.8 3.6 %collective-permute-done.55 = f32[192,96]{1,0:T(8,128)S(1)} collective-permute-done((f32[192,96]{1,0:T(8,128)S(1)}, f32[192,96]{1,0:T(8,128)S(1)}, u32[]{:S(2)}, u32[]{:S(2)}) %collective-permute-start.55) | collective-permute-done | bytes 73760 | tf_op jit(solution)/shard_map/ppermute | solution.py:1277
  (294 shorter events, 89.4 us)
Async XLA Ops:
  21.3 24.0 %collective-permute-start.2 = (bf16[2,192,384]{2,1,0:T(8,128)(2,1)S(1)}, bf16[2,192,384]{2,1,0:T(8,128)(2,1)S(1)}, u32[]{:S(2)}, u32[]{:S(2)}) collective-permute-start(bf16[2,192,384]{2,1,0:T(8,128)(2,1)S(1)} %pad_maximum_fusion.10), channel_id=1, source_target_pairs={{0,6},{1,7},{2,0},{3,1},{4,2},{5,3},{6,4},{7,5},{8,14},{9,15},{10,... | collective-permute-start | bytes 884744 | tf_op jit(solution)/shard_map/ppermute | solution.py:1027
  25.1 20.3 %collective-permute-start.3 = (bf16[2,192,384]{2,1,0:T(8,128)(2,1)S(1)}, bf16[2,192,384]{2,1,0:T(8,128)(2,1)S(1)}, u32[]{:S(2)}, u32[]{:S(2)}) collective-permute-start(bf16[2,192,384]{2,1,0:T(8,128)(2,1)S(1)} %pad_maximum_fusion.10), channel_id=1, source_target_pairs={{0,2},{1,3},{2,4},{3,5},{4,6},{5,7},{6,0},{7,1},{8,10},{9,11},{10,... | collective-permute-start | bytes 884744 | tf_op jit(solution)/shard_map/ppermute | solution.py:1027
  27.6 34.9 %collective-permute-start.12 = (bf16[272,768]{1,0:T(8,128)(2,1)S(1)}, bf16[272,768]{1,0:T(8,128)(2,1)S(1)}, u32[]{:S(2)}, u32[]{:S(2)}) collective-permute-start(bf16[272,768]{1,0:T(8,128)(2,1)S(1)} %copy-done), channel_id=1, source_target_pairs={{0,2},{1,3},{2,4},{3,5},{4,6},{5,7},{6,0},{7,1},{8,10},{9,11},{10,... | collective-permute-start | bytes 1253384 | tf_op jit(solution)/shard_map/ppermute | solution.py:1027
  28.2 35.4 %collective-permute-start.11 = (bf16[272,768]{1,0:T(8,128)(2,1)S(1)}, bf16[272,768]{1,0:T(8,128)(2,1)S(1)}, u32[]{:S(2)}, u32[]{:S(2)}) collective-permute-start(bf16[272,768]{1,0:T(8,128)(2,1)S(1)} %copy-done), channel_id=1, source_target_pairs={{0,6},{1,7},{2,0},{3,1},{4,2},{5,3},{6,4},{7,5},{8,14},{9,15},{10,... | collective-permute-start | bytes 1253384 | tf_op jit(solution)/shard_map/ppermute | solution.py:1027
  31.7 15.9 %collective-permute-start.10 = (bf16[2,192,384]{2,1,0:T(8,128)(2,1)S(1)}, bf16[2,192,384]{2,1,0:T(8,128)(2,1)S(1)}, u32[]{:S(2)}, u32[]{:S(2)}) collective-permute-start(bf16[2,192,384]{2,1,0:T(8,128)(2,1)S(1)} %get-tuple-element.234), channel_id=1, source_target_pairs={{0,16},{8,24},{16,0},{24,8},{1,17},{9,25},{17,1},{25,9},{2,18},{10... | collective-permute-start | bytes 884744 | tf_op jit(solution)/shard_map/ppermute | solution.py:1023
  45.3 12.9 %collective-permute-start.5 = (bf16[192,384]{1,0:T(8,128)(2,1)S(1)}, bf16[192,384]{1,0:T(8,128)(2,1)S(1)}, u32[]{:S(2)}, u32[]{:S(2)}) collective-permute-start(bf16[192,384]{1,0:T(8,128)(2,1)S(1)} %get-tuple-element.236), channel_id=1, source_target_pairs={{0,6},{1,7},{2,0},{3,1},{4,2},{5,3},{6,4},{7,5},{8,14},{9,15},{10,... | collective-permute-start | bytes 442376 | tf_op jit(solution)/shard_map/ppermute | solution.py:1027
  45.5 15.3 %collective-permute-start.4 = (bf16[192,384]{1,0:T(8,128)(2,1)S(1)}, bf16[192,384]{1,0:T(8,128)(2,1)S(1)}, u32[]{:S(2)}, u32[]{:S(2)}) collective-permute-start(bf16[192,384]{1,0:T(8,128)(2,1)S(1)} %get-tuple-element.239), channel_id=1, source_target_pairs={{0,2},{1,3},{2,4},{3,5},{4,6},{5,7},{6,0},{7,1},{8,10},{9,11},{10,... | collective-permute-start | bytes 442376 | tf_op jit(solution)/shard_map/ppermute | solution.py:1027
  47.6 29.2 %collective-permute-start.15 = (bf16[4,192,384]{2,1,0:T(8,128)(2,1)S(1)}, bf16[4,192,384]{2,1,0:T(8,128)(2,1)S(1)}, u32[]{:S(2)}, u32[]{:S(2)}) collective-permute-start(bf16[4,192,384]{2,1,0:T(8,128)(2,1)S(1)} %bitcast.148), channel_id=1, source_target_pairs={{0,1},{1,0},{2,3},{3,2},{4,5},{5,4},{6,7},{7,6},{8,9},{9,8},{10,11... | collective-permute-start | bytes 1769480 | tf_op jit(solution)/shard_map/ppermute | solution.py:1020
  58.4 37.3 %collective-permute-start.17 = (bf16[4,192,384]{2,1,0:T(8,128)(2,1)S(1)}, bf16[4,192,384]{2,1,0:T(8,128)(2,1)S(1)}, u32[]{:S(2)}, u32[]{:S(2)}) collective-permute-start(bf16[4,192,384]{2,1,0:T(8,128)(2,1)S(1)} %get-tuple-element.215), channel_id=1, source_target_pairs={{0,8},{8,0},{16,24},{24,16},{1,9},{9,1},{17,25},{25,17},{2,10},{10... | collective-permute-start | bytes 1769480 | tf_op jit(solution)/shard_map/ppermute | solution.py:1023
  60.9 34.7 %collective-permute-start.16 = (bf16[4,192,384]{2,1,0:T(8,128)(2,1)S(1)}, bf16[4,192,384]{2,1,0:T(8,128)(2,1)S(1)}, u32[]{:S(2)}, u32[]{:S(2)}) collective-permute-start(bf16[4,192,384]{2,1,0:T(8,128)(2,1)S(1)} %get-tuple-element.217), channel_id=1, source_target_pairs={{0,16},{8,24},{16,0},{24,8},{1,17},{9,25},{17,1},{25,9},{2,18},{10... | collective-permute-start | bytes 1769480 | tf_op jit(solution)/shard_map/ppermute | solution.py:1023
  62.6 13.0 %collective-permute-start.13 = (bf16[144,768]{1,0:T(8,128)(2,1)S(1)}, bf16[144,768]{1,0:T(8,128)(2,1)S(1)}, u32[]{:S(2)}, u32[]{:S(2)}) collective-permute-start(bf16[144,768]{1,0:T(8,128)(2,1)S(1)} %slice.324), channel_id=1, source_target_pairs={{0,2},{1,3},{2,4},{3,5},{4,6},{5,7},{6,0},{7,1},{8,10},{9,11},{10,... | collective-permute-start | bytes 663560 | tf_op jit(solution)/shard_map/ppermute | solution.py:1027
  74.1 21.6 %collective-permute-start.18 = (bf16[192,384]{1,0:T(8,128)(2,1)S(1)}, bf16[192,384]{1,0:T(8,128)(2,1)S(1)}, u32[]{:S(2)}, u32[]{:S(2)}) collective-permute-start(bf16[192,384]{1,0:T(8,128)(2,1)S(1)} %pad_maximum_fusion.19), channel_id=1, source_target_pairs={{0,6},{1,7},{2,0},{3,1},{4,2},{5,3},{6,4},{7,5},{8,14},{9,15},{10,... | collective-permute-start | bytes 442376 | tf_op jit(solution)/shard_map/ppermute | solution.py:1027
  75.6 20.1 %collective-permute-start.19 = (bf16[192,384]{1,0:T(8,128)(2,1)S(1)}, bf16[192,384]{1,0:T(8,128)(2,1)S(1)}, u32[]{:S(2)}, u32[]{:S(2)}) collective-permute-start(bf16[192,384]{1,0:T(8,128)(2,1)S(1)} %pad_maximum_fusion.19), channel_id=1, source_target_pairs={{0,4},{1,5},{2,6},{3,7},{4,0},{5,1},{6,2},{7,3},{8,12},{9,13},{10,... | collective-permute-start | bytes 442376 | tf_op jit(solution)/shard_map/ppermute | solution.py:1027
  76.9 18.8 %collective-permute-start.20 = (bf16[192,384]{1,0:T(8,128)(2,1)S(1)}, bf16[192,384]{1,0:T(8,128)(2,1)S(1)}, u32[]{:S(2)}, u32[]{:S(2)}) collective-permute-start(bf16[192,384]{1,0:T(8,128)(2,1)S(1)} %pad_maximum_fusion.19), channel_id=1, source_target_pairs={{0,2},{1,3},{2,4},{3,5},{4,6},{5,7},{6,0},{7,1},{8,10},{9,11},{10,... | collective-permute-start | bytes 442376 | tf_op jit(solution)/shard_map/ppermute | solution.py:1027
  95.8 33.8 %collective-permute-start.28 = (bf16[2,4,192,384]{3,2,1,0:T(8,128)(2,1)S(1)}, bf16[2,4,192,384]{3,2,1,0:T(8,128)(2,1)}, u32[]{:S(2)}, u32[]{:S(2)}) collective-permute-start(bf16[2,4,192,384]{3,2,1,0:T(8,128)(2,1)S(1)} %pad_maximum_fusion.1.w2a_ref), channel_id=1, source_target_pairs={{0,16},{8,24},{16,0},{24,8},{1,17},{9,25},{17,1},{25,9},{2,18},{10... | collective-permute-start | bytes 3538952 | tf_op jit(solution)/shard_map/ppermute | solution.py:1023
  97.6 32.0 %collective-permute-start.27 = (bf16[2,4,192,384]{3,2,1,0:T(8,128)(2,1)}, bf16[2,4,192,384]{3,2,1,0:T(8,128)(2,1)}, u32[]{:S(2)}, u32[]{:S(2)}) collective-permute-start(bf16[2,4,192,384]{3,2,1,0:T(8,128)(2,1)} %pad_maximum_fusion.w1a_ref), channel_id=1, source_target_pairs={{0,8},{8,0},{16,24},{24,16},{1,9},{9,1},{17,25},{25,17},{2,10},{10... | collective-permute-start | bytes 3538952 | tf_op jit(solution)/shard_map/ppermute | solution.py:1023
  107.6 12.2 %collective-permute-start.23 = (bf16[256,192]{1,0:T(8,128)(2,1)}, bf16[256,192]{1,0:T(8,128)(2,1)S(1)}, u32[]{:S(2)}, u32[]{:S(2)}) collective-permute-start(bf16[256,192]{1,0:T(8,128)(2,1)} %get-tuple-element.125), channel_id=1, source_target_pairs={{0,6},{1,7},{2,0},{3,1},{4,2},{5,3},{6,4},{7,5},{8,14},{9,15},{10,... | collective-permute-start | bytes 294920 | tf_op jit(solution)/shard_map/ppermute | solution.py:1027
  151.4 16.2 %collective-permute-start.29 = (bf16[256,768]{1,0:T(8,128)(2,1)}, bf16[256,768]{1,0:T(8,128)(2,1)S(1)}, u32[]{:S(2)}, u32[]{:S(2)}) collective-permute-start(bf16[256,768]{1,0:T(8,128)(2,1)} %get-tuple-element.135), channel_id=1, source_target_pairs={{0,1},{1,0},{2,3},{3,2},{4,5},{5,4},{6,7},{7,6},{8,9},{9,8},{10,11... | collective-permute-start | bytes 1179656 | tf_op jit(solution)/shard_map/ppermute | solution.py:1020
  151.8 60.9 %collective-permute-start.38 = (bf16[2,4,192,384]{3,2,1,0:T(8,128)(2,1)}, bf16[2,4,192,384]{3,2,1,0:T(8,128)(2,1)S(1)}, u32[]{:S(2)}, u32[]{:S(2)}) collective-permute-start(bf16[2,4,192,384]{3,2,1,0:T(8,128)(2,1)} %get-tuple-element.172), channel_id=1, source_target_pairs={{0,8},{8,0},{16,24},{24,16},{1,9},{9,1},{17,25},{25,17},{2,10},{10... | collective-permute-start | bytes 3538952 | tf_op jit(solution)/shard_map/ppermute | solution.py:1023
  152.5 60.3 %collective-permute-start.39 = (bf16[2,4,192,384]{3,2,1,0:T(8,128)(2,1)}, bf16[2,4,192,384]{3,2,1,0:T(8,128)(2,1)S(1)}, u32[]{:S(2)}, u32[]{:S(2)}) collective-permute-start(bf16[2,4,192,384]{3,2,1,0:T(8,128)(2,1)} %get-tuple-element.173), channel_id=1, source_target_pairs={{0,16},{8,24},{16,0},{24,8},{1,17},{9,25},{17,1},{25,9},{2,18},{10... | collective-permute-start | bytes 3538952 | tf_op jit(solution)/shard_map/ppermute | solution.py:1023
  179.8 32.9 %collective-permute-start.35 = (bf16[4,192,96]{2,1,0:T(8,128)(2,1)S(1)}, bf16[4,192,96]{2,1,0:T(8,128)(2,1)S(1)}, u32[]{:S(2)}, u32[]{:S(2)}) collective-permute-start(bf16[4,192,96]{2,1,0:T(8,128)(2,1)S(1)} %get-tuple-element.204), channel_id=1, source_target_pairs={{0,2},{1,3},{2,4},{3,5},{4,6},{5,7},{6,0},{7,1},{8,10},{9,11},{10,... | collective-permute-start | bytes 442376 | tf_op jit(solution)/shard_map/ppermute | solution.py:1027
  179.9 32.9 %collective-permute-start.36 = (bf16[4,192,96]{2,1,0:T(8,128)(2,1)S(1)}, bf16[4,192,96]{2,1,0:T(8,128)(2,1)S(1)}, u32[]{:S(2)}, u32[]{:S(2)}) collective-permute-start(bf16[4,192,96]{2,1,0:T(8,128)(2,1)S(1)} %get-tuple-element.203), channel_id=1, source_target_pairs={{0,4},{1,5},{2,6},{3,7},{4,0},{5,1},{6,2},{7,3},{8,12},{9,13},{10,... | collective-permute-start | bytes 442376 | tf_op jit(solution)/shard_map/ppermute | solution.py:1027
  182.6 30.2 %collective-permute-start.37 = (bf16[4,192,96]{2,1,0:T(8,128)(2,1)S(1)}, bf16[4,192,96]{2,1,0:T(8,128)(2,1)S(1)}, u32[]{:S(2)}, u32[]{:S(2)}) collective-permute-start(bf16[4,192,96]{2,1,0:T(8,128)(2,1)S(1)} %get-tuple-element.202), channel_id=1, source_target_pairs={{0,6},{1,7},{2,0},{3,1},{4,2},{5,3},{6,4},{7,5},{8,14},{9,15},{10,... | collective-permute-start | bytes 442376 | tf_op jit(solution)/shard_map/ppermute | solution.py:1027
  213.0 23.1 %collective-permute-start.56 = (bf16[4,192,384]{2,1,0:T(8,128)(2,1)S(1)}, bf16[4,192,384]{2,1,0:T(8,128)(2,1)}, u32[]{:S(2)}, u32[]{:S(2)}) collective-permute-start(bf16[4,192,384]{2,1,0:T(8,128)(2,1)S(1)} %fusion.2), channel_id=1, source_target_pairs={{0,16},{8,24},{16,0},{24,8},{1,17},{9,25},{17,1},{25,9},{2,18},{10... | collective-permute-start | bytes 1769480 | tf_op jit(solution)/shard_map/ppermute | solution.py:1023
  214.4 24.1 %collective-permute-start.57 = (bf16[4,192,384]{2,1,0:T(8,128)(2,1)S(1)}, bf16[4,192,384]{2,1,0:T(8,128)(2,1)S(1)}, u32[]{:S(2)}, u32[]{:S(2)}) collective-permute-start(bf16[4,192,384]{2,1,0:T(8,128)(2,1)S(1)} %fusion.3), channel_id=1, source_target_pairs={{0,8},{8,0},{16,24},{24,16},{1,9},{9,1},{17,25},{25,17},{2,10},{10... | collective-permute-start | bytes 1769480 | tf_op jit(solution)/shard_map/ppermute | solution.py:1023
  232.1 27.8 %collective-permute-start.47 = (bf16[4,192,288]{2,1,0:T(8,128)(2,1)}, bf16[4,192,288]{2,1,0:T(8,128)(2,1)S(1)}, u32[]{:S(2)}, u32[]{:S(2)}) collective-permute-start(bf16[4,192,288]{2,1,0:T(8,128)(2,1)} %get-tuple-element.187), channel_id=1, source_target_pairs={{0,1},{1,0},{2,3},{3,2},{4,5},{5,4},{6,7},{7,6},{8,9},{9,8},{10,11... | collective-permute-start | bytes 1327112 | tf_op jit(solution)/shard_map/ppermute | solution.py:1020
  233.2 12.3 %collective-permute-start.44 = (bf16[256,768]{1,0:T(8,128)(2,1)S(1)}, bf16[256,768]{1,0:T(8,128)(2,1)}, u32[]{:S(2)}, u32[]{:S(2)}) collective-permute-start(bf16[256,768]{1,0:T(8,128)(2,1)S(1)} %pad_maximum_fusion.7), channel_id=1, source_target_pairs={{0,6},{1,7},{2,0},{3,1},{4,2},{5,3},{6,4},{7,5},{8,14},{9,15},{10,... | collective-permute-start | bytes 1179656 | tf_op jit(solution)/shard_map/ppermute | solution.py:1027
  236.1 19.6 %collective-permute-start.42 = (bf16[256,768]{1,0:T(8,128)(2,1)S(1)}, bf16[256,768]{1,0:T(8,128)(2,1)}, u32[]{:S(2)}, u32[]{:S(2)}) collective-permute-start(bf16[256,768]{1,0:T(8,128)(2,1)S(1)} %pad_maximum_fusion.6), channel_id=1, source_target_pairs={{0,2},{1,3},{2,4},{3,5},{4,6},{5,7},{6,0},{7,1},{8,10},{9,11},{10,... | collective-permute-start | bytes 1179656 | tf_op jit(solution)/shard_map/ppermute | solution.py:1027
  237.5 24.0 %collective-permute-start.58 = (bf16[192,384]{1,0:T(8,128)(2,1)S(1)}, bf16[192,384]{1,0:T(8,128)(2,1)S(1)}, u32[]{:S(2)}, u32[]{:S(2)}) collective-permute-start(bf16[192,384]{1,0:T(8,128)(2,1)S(1)} %get-tuple-element.210), channel_id=1, source_target_pairs={{0,2},{1,3},{2,4},{3,5},{4,6},{5,7},{6,0},{7,1},{8,10},{9,11},{10,... | collective-permute-start | bytes 442376 | tf_op jit(solution)/shard_map/ppermute | solution.py:1027
  238.8 24.0 %collective-permute-start.60 = (bf16[192,384]{1,0:T(8,128)(2,1)S(1)}, bf16[192,384]{1,0:T(8,128)(2,1)S(1)}, u32[]{:S(2)}, u32[]{:S(2)}) collective-permute-start(bf16[192,384]{1,0:T(8,128)(2,1)S(1)} %get-tuple-element.213), channel_id=1, source_target_pairs={{0,6},{1,7},{2,0},{3,1},{4,2},{5,3},{6,4},{7,5},{8,14},{9,15},{10,... | collective-permute-start | bytes 442376 | tf_op jit(solution)/shard_map/ppermute | solution.py:1027
  262.9 15.2 %collective-permute-start.61 = (bf16[2,192,384]{2,1,0:T(8,128)(2,1)S(1)}, bf16[2,192,384]{2,1,0:T(8,128)(2,1)S(1)}, u32[]{:S(2)}, u32[]{:S(2)}) collective-permute-start(bf16[2,192,384]{2,1,0:T(8,128)(2,1)S(1)} %pad_maximum_fusion.15), channel_id=1, source_target_pairs={{0,6},{1,7},{2,0},{3,1},{4,2},{5,3},{6,4},{7,5},{8,14},{9,15},{10,... | collective-permute-start | bytes 884744 | tf_op jit(solution)/shard_map/ppermute | solution.py:1027
  278.2 12.9 %collective-permute-start.62 = (f32[96,384]{1,0:T(8,128)S(1)}, f32[96,384]{1,0:T(8,128)S(1)}, u32[]{:S(2)}, u32[]{:S(2)}) collective-permute-start(f32[96,384]{1,0:T(8,128)S(1)} %select_bitcast_fusion), channel_id=1, source_target_pairs={{0,1},{1,0},{2,3},{3,2},{4,5},{5,4},{6,7},{7,6},{8,9},{9,8},{10,11... | collective-permute-start | bytes 442376 | tf_op jit(solution)/shard_map/ppermute | solution.py:1020
  (77 other events, 525.8 us)

commit v2 on v1

--- a/solution.py
+++ b/solution.py
@@ -19,8 +19,10 @@
 VMEM_LIMIT = 56 * 1024 * 1024
 
 
-def cost(flops, nbytes):
-    return pl.CostEstimate(flops=int(flops * 1e-3), bytes_accessed=int(nbytes * 1e-3), transcendentals=0)
+def cost(flops, nbytes, scale=1e-3):
+    return pl.CostEstimate(
+        flops=int(flops * scale), bytes_accessed=int(nbytes * scale), transcendentals=0
+    )
 
 
 def params(*semantics):
@@ -1133,11 +1135,11 @@
         )
         wq_own = jnp.stack([wq_own, links.flip(wq_own, 1)])
         wq_own = jnp.stack([wq_own, links.flip(wq_own, 2)]).reshape(4, 192, 384)
+        wq_own, qkv_order = lax.optimization_barrier((wq_own, qkv_order))
         wq = (wq_own, links.core(wq_own))
         wo_own = jnp.concatenate([wq_own[j, :, 288:] for j in range(4)], axis=1)
 
-        x_ext_late, _ = lax.optimization_barrier((arrays[0], (w1, w2, wo_own)))
-        arrays[0] = x_ext_late
+        arrays, w1, w2, wo_own = lax.optimization_barrier((arrays, w1, w2, wo_own))
         w1_in = links.flip(w1, 2)
         w2_in = links.flip(w2, 1)
         wo_all = [wo_own] + [links.shift(wo_own, -k) for k in range(1, 4)]
@@ -1163,7 +1165,7 @@
         bias = lax.dynamic_slice_in_dim(bias_all, c * (FF // 2), FF // 2, 0).reshape(4, 384)
         bias = jnp.pad(bias, ((0, 4), (0, 0)))
         ff_place = jnp.stack([0 * d, 0 * z, c]).astype(jnp.int32)
-    cot_in = links.core(after(cot, x_ext))
+    cot_in = links.core(after(cot, arrays))
 
     far = sorted(range(1, nz), key=lambda k: -min(k, nz - k))
     first = far[: nz // 2]
@@ -1208,16 +1210,27 @@
     pulled = [gmixed[0]] + [links.shift(gmixed[k], k) for k in range(1, nz)]
     pulled = [pulled[(nz - k) % nz] for k in range(nz)]
     part = attention_backward(pulled, by, saved, heads, chunk, [0], None, None)
+    if fast:
+        part, pulled, gproj = lax.optimization_barrier((part, pulled, gproj))
     out_rows = (residual + out_own + out_in.astype(F32) + gains[2:3]).astype(BF)
     rows_in = links.core(out_rows[local:])
     if fast:
         wo_keep, wo_send = out_weight(place, mixed, gproj, out_order)
         wo_came = links.core(wo_send)
+        dw1_in, dw2_in, _ = lax.optimization_barrier((dw1_in, dw2_in, wo_keep))
+        dw1_sum = add_low(dw1a[1], dw1_in[1])
+        dw2_sum = add_low(dw2a[1], dw2_in[1])
         dwo = [
             add_low(wo_keep[..., 96 * k : 96 * k + 96], wo_came[..., 96 * k : 96 * k + 96])
             for k in range(4)
         ]
-        part, _ = lax.optimization_barrier((part, (dwo, out_rows)))
+        dw1 = dw1a[0].astype(F32) + dw1_in[0].astype(F32)
+        dw2 = dw2a[0].astype(F32) + dw2_in[0].astype(F32)
+        part, dwo, dw1_sum, dw2_sum, dw1, dw2, _ = lax.optimization_barrier(
+            (part, dwo, dw1_sum, dw2_sum, dw1, dw2, out_rows)
+        )
+        dw1_in = links.flip(dw1_sum, 2)
+        dw2_in = links.flip(dw2_sum, 1)
         dwo = [dwo[0]] + [links.shift(dwo[k], k) for k in range(1, 4)]
     made = attention_backward(
         pulled, by, saved, heads, chunk, list(range(1, nz)), part, (sums, out_order)
@@ -1230,32 +1243,44 @@
     if nz == 4:
         low_in = links.shift(gh1[2], 1)
         high_in = links.shift(gh1[4], -1)
+        if fast:
+            wq_keep, wq_send = qkv_weight(place, h1_t, gqkv, qkv_order)
+            low_in, high_in, wq_keep, wq_send = lax.optimization_barrier(
+                (low_in, high_in, wq_keep, wq_send)
+            )
         up = jnp.concatenate([add_low(gh1[1][:local], low_in), gh1[1][local:]], axis=0)
         down = jnp.concatenate([gh1[3][:local], add_low(gh1[3][local:], high_in)], axis=0)
         terms = [gh1[0], links.shift(up, 1), links.shift(down, -1)]
     else:
         terms = [gh1[0]] + [links.shift(gh1[k], k) for k in range(1, nz)]
-    grad_rows = input_backward(terms, x_ext, gains, gres)
-    grad_in = links.core(grad_rows[local:])
-
-    def by_micro(own, other):
-        return jnp.where(c == 0, jnp.stack([own, other]), jnp.stack([other, own]))[:, None]
-
-    outputs = by_micro(out_rows[:local], rows_in)
-    input_grad = by_micro(grad_rows[:local], grad_in)
-    vec = vec_keep + links.core(vec_send)
-
     if fast:
-        dw1_in = links.flip(add_low(dw1a[1], dw1_in[1]), 2), dw1_in[0]
-        dw2_in = links.flip(add_low(dw2a[1], dw2_in[1]), 1), dw2_in[0]
-        wq_keep, wq_send = qkv_weight(place, h1_t, after(gqkv, low_in, high_in), qkv_order)
+        dw1_in, dw2_in, dwo, wq_send = lax.optimization_barrier((dw1_in, dw2_in, dwo, wq_send))
+        dw1 = dw1 + dw1_in.astype(F32)
+        dw2 = dw2 + dw2_in.astype(F32)
+        dw = after(jnp.stack([dw1, dw2], axis=1).astype(BF), up, down)
+        dw_came = (
+            links.shift(dw[1], 1),
+            links.shift(dw[3], -1),
+            links.shift(dw[2], 2),
+        )
         dwo = sum(t.astype(F32) for t in dwo)
         joint = jnp.concatenate(
             [add_low(wq_keep, links.core(wq_send)), dwo.astype(BF)], axis=2
         )
         joint = joint.reshape(2, 384, 384)
+        vec = vec_keep + links.core(vec_send)
         vec = jnp.concatenate([vec[:3], db1[:, 0], jnp.zeros((9, 384), F32)], axis=0)
         came = links.flip(jnp.concatenate([joint[1], vec.astype(BF)], axis=0), 2)
+        terms, came = lax.optimization_barrier((terms, came))
+    grad_rows = input_backward(terms, x_ext, gains, gres)
+    grad_in = links.core(grad_rows[local:])
+
+    def by_micro(own, other):
+        return jnp.where(c == 0, jnp.stack([own, other]), jnp.stack([other, own]))[:, None]
+
+    outputs = by_micro(*after((out_rows[:local], rows_in), terms))
+    input_grad = by_micro(grad_rows[:local], grad_in)
+    if fast:
         joint = add_low(joint[0], came[:384]).reshape(2, 192, 384)
         vec = vec + came[384:].astype(F32)
         came = links.flip(jnp.concatenate([joint[1], vec.astype(BF)], axis=0), 1)
@@ -1283,15 +1308,9 @@
             ],
             axis=1,
         )
-        dw1 = dw1a[0].astype(F32) + dw1_in[0].astype(F32) + dw1_in[1].astype(F32)
-        dw2 = dw2a[0].astype(F32) + dw2_in[0].astype(F32) + dw2_in[1].astype(F32)
-        low_in = links.shift(dw1[2].astype(BF), 1)
-        high_in = links.shift(dw2[2].astype(BF), -1)
-        up = jnp.stack([dw1[1] + low_in.astype(F32), dw2[1]]).astype(BF)
-        down = jnp.stack([dw1[3], dw2[3] + high_in.astype(F32)]).astype(BF)
-        up_in = links.shift(up, 1).astype(F32)
-        down_in = links.shift(down, -1).astype(F32)
-        dw = jnp.stack([dw1[0], dw2[0]]) + up_in + down_in
+        dw_came, _ = lax.optimization_barrier((dw_came, (vecs, g_qkv, grad_rows)))
+        dw_came = [v.astype(F32) for v in dw_came]
+        dw = jnp.stack([dw1[0], dw2[0]]) + dw_came[0] + dw_came[1] + dw_came[2]
         g_fc1 = dw[0]
         keep, send = to_both((dw[1, :96], dw[1, 96:]))
         g_fc2 = jnp.concatenate(to_both((keep, links.core(send))), axis=1).T
@@ -1328,6 +1347,7 @@
         bias_full = lax.psum(
             lax.psum_scatter(bias_full, "seq", scatter_dimension=0, tiled=True), "dp"
         )
+        vec = vec_keep + links.core(vec_send)
         vec = vec[:3].reshape(3, nz, n_w)
         vec = sum([vec[:, 0]] + [links.shift(vec[:, k], k) for k in range(1, nz)])
         vec = lax.psum(vec, "dp")

time: 297 us -> 286 us (0.963)
  waiting for transfers between devices: 81.1 us -> 62.7 us
  starting transfers between devices: 76.1 us -> 82.6 us
  local copies, waits for them, and re-layouts: 13.2 us -> 17 us
    ppermute x31 -> x30, waiting for transfers between devices: 69.8 us -> 55.2 us  [shift(): lax.ppermute(v, 'seq', [(s, 2 * ((s // 2 + k) % n) + s % 2) for s in rang...]
    ppermute x3, starting transfers between devices: 5.03 us -> 9.73 us  [per_device(): lax.ppermute(pick(third, lax.rem(2 * (i - s + 9), 3)), 'seq', [((3 * q +...]
    ppermute x12, waiting for transfers between devices: 4.08 us -> 0.03 us  [flip(): return lax.ppermute(v, 'dp', [(i, i ^ bit) for i in range(self.n_dp)])]
    unnamed x93 -> x91, local copies, waits for them, and re-layouts: 4.41 us -> 6.82 us
    ppermute x31 -> x30, starting transfers between devices: 46.2 us -> 47.8 us  [shift(): lax.ppermute(v, 'seq', [(s, 2 * ((s // 2 + k) % n) + s % 2) for s in rang...]
  transfers between devices with their start and end apart: 63 -> 62, of which waited for: 19 -> 14; matrix products, arithmetic and copies ran while one was open for 8% -> 7% of each run, Pallas kernels for 27% -> 28%
where the time goes in v2:
time: 286 us; the launch traced here: 285 us
  Pallas kernels  107 us (37%)
  starting transfers between devices  82.6 us (29%)
  waiting for transfers between devices  62.7 us (22%)
  local copies, waits for them, and re-layouts  17 us (6%)
  other arithmetic  14.6 us (5%)
    ppermute x30, waiting for transfers between devices, shift(): lax.ppermute(v, 'seq', [(s, 2 * ((s // 2 + k) % n) + s % 2) for s in rang...  55.2 us
    ppermute x30, starting transfers between devices, shift(): lax.ppermute(v, 'seq', [(s, 2 * ((s // 2 + k) % n) + s % 2) for s in rang...  47.8 us
    pallas_call x2, Pallas kernels, attention_backward(): pl.pallas_call(kernel, name='attention_backward_last' if last else 'atten...  26.9 us
    pallas_call x1, Pallas kernels, feed_forward(): pl.pallas_call(kernel, name='feed_forward', grid_spec=pltpu.PrefetchScala...  21 us
    pallas_call x1, Pallas kernels, attention_first(): pl.pallas_call(kernel, name='attention_first', grid_spec=pltpu.PrefetchSc...  16.6 us
    ppermute x12, starting transfers between devices, flip(): return lax.ppermute(v, 'dp', [(i, i ^ bit) for i in range(self.n_dp)])  14.2 us
    ppermute x3, starting transfers between devices, per_device(): lax.ppermute(pick(third, lax.rem(2 * (i - s + 9), 3)), 'seq', [((3 * q +...  9.73 us
    ppermute x3, starting transfers between devices, per_device(): lax.ppermute(wq_parts[:, 96 * i:96 * i + 96], 'seq', [(q, (3 * q + i) % 8...  9.29 us
  transfers between devices with their start and end apart: 62, of which 14 were waited for; matrix products, arithmetic and copies ran while one was open for 7% of the time, Pallas kernels for 28%

profile of v2, /device:TPU:0, one launch (start us, length us, event | category | flops | bytes accessed | tf_op | source)
XLA Modules:
  0.0 285.1 jit_solution(1561912587291195818)
XLA Ops:
  2.5 2.6 message_rows.1
  8.9 2.6 own_rows.1.refs_0_.refs_5_.refs_3_
  12.3 4.1 %collective-permute-start.11 = (bf16[192,96]{1,0:T(8,128)(2,1)S(1)}, bf16[192,96]{1,0:T(8,128)(2,1)S(1)}, u32[]{:S(2)}, u32[]{:S(2)}) collective-permute-start(bf16[192,96]{1,0:T(8,128)(2,1)S(1)} %get-tuple-element.337), channel_id=1, source_target_pairs={{0,1},{1,4},{2,7},{3,2},{4,5},{5,0},{6,3},{7,6},{8,9},{9,12},{10,1... | collective-permute-start | bytes 110600 | tf_op jit(solution)/shard_map/ppermute | solution.py:1126
  16.4 4.5 %collective-permute-start.12 = (bf16[192,96]{1,0:T(8,128)(2,1)S(1)}, bf16[192,96]{1,0:T(8,128)(2,1)S(1)}, u32[]{:S(2)}, u32[]{:S(2)}) collective-permute-start(bf16[192,96]{1,0:T(8,128)(2,1)S(1)} %get-tuple-element.336), channel_id=1, source_target_pairs={{0,2},{1,5},{2,0},{3,3},{4,6},{5,1},{6,4},{7,7},{8,10},{9,13},{10,... | collective-permute-start | bytes 110600 | tf_op jit(solution)/shard_map/ppermute | solution.py:1126
  23.1 3.8 %collective-permute-start.1 = (bf16[272,768]{1,0:T(8,128)(2,1)}, bf16[272,768]{1,0:T(8,128)(2,1)S(1)}, u32[]{:S(2)}, u32[]{:S(2)}) collective-permute-start(bf16[272,768]{1,0:T(8,128)(2,1)} %own_rows.1.refs_0_.refs_5_.refs_3_), channel_id=1, source_target_pairs={{0,6},{1,7},{2,0},{3,1},{4,2},{5,3},{6,4},{7,5},{8,14},{9,15},{10,... | collective-permute-start | bytes 1253384 | tf_op jit(solution)/shard_map/ppermute | solution.py:1029
  28.8 17.0 %collective-permute-done.6 = bf16[2,192,384]{2,1,0:T(8,128)(2,1)S(1)} collective-permute-done((bf16[2,192,384]{2,1,0:T(8,128)(2,1)S(1)}, bf16[2,192,384]{2,1,0:T(8,128)(2,1)S(1)}, u32[]{:S(2)}, u32[]{:S(2)}) %collective-permute-start.6) | collective-permute-done | bytes 294944 | tf_op jit(solution)/shard_map/ppermute | solution.py:1029
  51.3 6.7 %collective-permute-done.9 = bf16[192,384]{1,0:T(8,128)(2,1)S(1)} collective-permute-done((bf16[192,384]{1,0:T(8,128)(2,1)S(1)}, bf16[192,384]{1,0:T(8,128)(2,1)S(1)}, u32[]{:S(2)}, u32[]{:S(2)}) %collective-permute-start.9) | collective-permute-done | bytes 147488 | tf_op jit(solution)/shard_map/ppermute | solution.py:1029
  58.1 2.5 collective-permute-done.8
  61.7 3.0 %collective-permute-start.4 = (bf16[128,768]{1,0:T(8,128)(2,1)S(1)}, bf16[128,768]{1,0:T(8,128)(2,1)S(1)}, u32[]{:S(2)}, u32[]{:S(2)}) collective-permute-start(bf16[128,768]{1,0:T(8,128)(2,1)S(1)} %slice.299), channel_id=1, source_target_pairs={{0,6},{1,7},{2,0},{3,1},{4,2},{5,3},{6,4},{7,5},{8,14},{9,15},{10,... | collective-permute-start | bytes 589832 | tf_op jit(solution)/shard_map/ppermute | solution.py:1029
  65.1 6.6 %collective-permute-done.4.refs_3_ = bf16[128,768]{1,0:T(8,128)(2,1)S(1)} collective-permute-done((bf16[128,768]{1,0:T(8,128)(2,1)S(1)}, bf16[128,768]{1,0:T(8,128)(2,1)S(1)}, u32[]{:S(2)}, u32[]{:S(2)}) %collective-permute-start.4) | collective-permute-done | bytes 196640 | tf_op jit(solution)/shard_map/ppermute | solution.py:1029
  74.8 2.1 collective-permute-start.18
  80.4 16.6 %attention_first.1 = (bf16[1024,768]{1,0:T(8,128)(2,1)}, bf16[1024,256]{1,0:T(8,128)(2,1)}, bf16[1024,256]{1,0:T(8,128)(2,1)}, bf16[1024,256]{1,0:T(8,128)(2,1)}...) custom-call(s32[3]{0:T(128)} %pad_add_fusion.place_ref, ...), custom_call_target="tpu_custom_call" | custom-call | flops 8000000 | bytes 8000 | tf_op jit(solution)/shard_map/attention_first/pallas_call | solution.py:424
  103.4 8.1 %attention_rest.1 = (bf16[256,192]{1,0:T(8,128)(2,1)}, f32[256,256]{1,0:T(8,128)}, f32[8,256]{1,0:T(8,128)}, bf16[256,192]{1,0:T(8,128)(2,1)}, f32[256,256]{1,0:T(8,128)}, /*index=5*/f32[8,256]{1,0:T(8,128)}) custom-call(bf16[1024,256]{1,0:T(8,128)(2,1)} %get-tuple-element.171.q_ref.refs_3_.refs_9_, ...), custom_call_target="tpu_custom_call" | custom-call | flops 5000000 | bytes 4000 | tf_op jit(solution)/shard_map/attention_rest/pallas_call | solution.py:460
  114.3 5.7 %reorder_out.1.refs_4_.w_ref = bf16[4,192,768]{2,1,0:T(8,128)(2,1)} custom-call(s32[3]{0:T(128)} %pad_add_fusion.place_ref, bf16[4,192,384]{2,1,0:T(8,128)(2,1)} %copy-done.4, bf16[4,192,384]{2,1,0:T(8,128)(2,1)} %copy-done.17, bf16[768,768]{1,0:T(8,128)(2,1)} %select_convert_fusion.refs_6_.order_ref.refs_5_.refs_23_), custom_call_target="tpu_custom_call" | custom-call | flops 1000000 | bytes 3000 | tf_op jit(solution)/shard_map/reorder_out/pallas_call | solution.py:665
  120.7 3.9 %output_projection.1 = (f32[256,768]{1,0:T(8,128)}, bf16[256,768]{1,0:T(8,128)(2,1)}) custom-call(s32[3]{0:T(128)} %pad_add_fusion.place_ref, bf16[256,192]{1,0:T(8,128)(2,1)} %get-tuple-element.176.refs_0_, bf16[256,192]{1,0:T(8,128)(2,1)} %copy-done.18, bf16[256,192]{1,0:T(8,128)(2,1)} %collective-permute-done.22.refs_2_, ...), custom_call_target="tpu_custom_call" | custom-call | flops 1000000 | bytes 3000 | tf_op jit(solution)/shard_map/output_projection/pallas_call | solution.py:755
  127.3 21.0 %feed_forward.1 = (f32[256,768]{1,0:T(8,128)}, bf16[256,768]{1,0:T(8,128)(2,1)}, f32[256,768]{1,0:T(8,128)}, bf16[256,768]{1,0:T(8,128)(2,1)}, bf16[2,4,192,384]...) custom-call(s32[3]{0:T(128)} %pad_add_fusion.place_ref, ...), custom_call_target="tpu_custom_call" | custom-call | flops 7200000 | bytes 15000 | tf_op jit(solution)/shard_map/feed_forward/pallas_call | solution.py:886
  152.2 4.8 %residual_backward.1 = (f32[256,768]{1,0:T(8,128)}, bf16[256,768]{1,0:T(8,128)(2,1)}, f32[16,768]{1,0:T(8,128)}, bf16[256,192]{1,0:T(8,128)(2,1)}, bf16[256,192]...) custom-call(s32[3]{0:T(128)} %pad_add_fusion.place_ref, f32[256,768]{1,0:T(8,128)} %get-tuple-element.190.gh_ref, ...), custom_call_target="tpu_custom_call" | custom-call | flops 1000000 | bytes 4000 | tf_op jit(solution)/shard_map/residual_backward/pallas_call | solution.py:956
  160.7 2.4 collective-permute-done.31.refs_0_
  163.8 7.6 %attention_backward_own.1 = (bf16[256,256]{1,0:T(8,128)(2,1)}, f32[1024,256]{1,0:T(8,128)}, f32[1024,256]{1,0:T(8,128)}) custom-call(bf16[256,192]{1,0:T(8,128)(2,1)} %get-tuple-element.192.refs_0_, f32[256,256]{1,0:T(8,128)} %get-tuple-element.193.refs_1_, f32[8,256]{1,0:T(8,128)} %get-tuple-element.194.refs_2_, ...), custom_call_target="tpu_custom_call" | custom-call | flops 3000000 | bytes 10000 | tf_op jit(solution)/shard_map/attention_backward_own/pallas_call | solution.py:625
  171.9 4.7 %out_weight.1 = (bf16[4,192,384]{2,1,0:T(8,128)(2,1)}, bf16[4,192,384]{2,1,0:T(8,128)(2,1)}) custom-call(s32[3]{0:T(128)} %pad_add_fusion.place_ref, bf16[256,192]{1,0:T(8,128)(2,1)} %get-tuple-element.176.refs_0_, bf16[256,192]{1,0:T(8,128)(2,1)} %copy-done.18, bf16[256,192]{1,0:T(8,128)(2,1)} %collective-permute-done.22.refs_2_, ...), custom_call_target="tpu_custom_call" | custom-call | flops 1000000 | bytes 4000 | tf_op jit(solution)/shard_map/out_weight/pallas_call | solution.py:723
  183.5 7.2 %collective-permute-start.37 = (bf16[4,192,96]{2,1,0:T(8,128)(2,1)}, bf16[4,192,96]{2,1,0:T(8,128)(2,1)S(1)}, u32[]{:S(2)}, u32[]{:S(2)}) collective-permute-start(bf16[4,192,96]{2,1,0:T(8,128)(2,1)} %get-tuple-element.240), channel_id=1, source_target_pairs={{0,2},{1,3},{2,4},{3,5},{4,6},{5,7},{6,0},{7,1},{8,10},{9,11},{10,... | collective-permute-start | bytes 442376 | tf_op jit(solution)/shard_map/ppermute | solution.py:1029
  190.6 2.4 collective-permute-start.39
  193.1 19.4 %attention_backward_last.1 = (bf16[1024,768]{1,0:T(8,128)(2,1)}, f32[16,384]{1,0:T(8,128)}, f32[16,384]{1,0:T(8,128)}, f32[256,768]{1,0:T(8,128)}, bf16[256,768]...) custom-call(bf16[256,192]{1,0:T(8,128)(2,1)} %copy-done.38, ...), custom_call_target="tpu_custom_call" | custom-call | flops 9000000 | bytes 10000 | tf_op jit(solution)/shard_map/attention_backward_last/pallas_call | solution.py:625
  213.7 3.8 %collective-permute-start.44 = (bf16[128,768]{1,0:T(8,128)(2,1)}, bf16[128,768]{1,0:T(8,128)(2,1)S(1)}, u32[]{:S(2)}, u32[]{:S(2)}) collective-permute-start(bf16[128,768]{1,0:T(8,128)(2,1)} %get-tuple-element.249), channel_id=1, source_target_pairs={{0,6},{1,7},{2,0},{3,1},{4,2},{5,3},{6,4},{7,5},{8,14},{9,15},{10,... | collective-permute-start | bytes 589832 | tf_op jit(solution)/shard_map/ppermute | solution.py:1029
  219.4 6.6 %qkv_weight.1 = (bf16[4,192,288]{2,1,0:T(8,128)(2,1)}, bf16[4,192,288]{2,1,0:T(8,128)(2,1)}) custom-call(s32[3]{0:T(128)} %pad_add_fusion.place_ref, bf16[768,1024]{1,0:T(8,128)(2,1)} %bitcast.122, bf16[1024,768]{1,0:T(8,128)(2,1)} %get-tuple-element.250.g_ref, bf16[768,768]{1,0:T(8,128)(2,1)} %select_convert_fusion.1.order_ref), custom_call_target="tpu_custom_call" | custom-call | flops 2000000 | bytes 5000 | tf_op jit(solution)/shard_map/qkv_weight/pallas_call | solution.py:692
  233.1 3.0 %collective-permute-start.59 = (bf16[2,192,384]{2,1,0:T(8,128)(2,1)S(1)}, bf16[2,192,384]{2,1,0:T(8,128)(2,1)S(1)}, u32[]{:S(2)}, u32[]{:S(2)}) collective-permute-start(bf16[2,192,384]{2,1,0:T(8,128)(2,1)S(1)} %get-tuple-element.299), channel_id=1, source_target_pairs={{0,6},{1,7},{2,0},{3,1},{4,2},{5,3},{6,4},{7,5},{8,14},{9,15},{10,... | collective-permute-start | bytes 884744 | tf_op jit(solution)/shard_map/ppermute | solution.py:1029
  236.1 17.4 %collective-permute-done.46.refs_2_ = bf16[256,768]{1,0:T(8,128)(2,1)S(1)} collective-permute-done((bf16[256,768]{1,0:T(8,128)(2,1)S(1)}, bf16[256,768]{1,0:T(8,128)(2,1)S(1)}, u32[]{:S(2)}, u32[]{:S(2)}) %collective-permute-start.46) | collective-permute-done | bytes 393248 | tf_op jit(solution)/shard_map/ppermute | solution.py:1029
  254.6 3.1 %input_backward.1 = bf16[256,768]{1,0:T(8,128)(2,1)} custom-call(f32[256,768]{1,0:T(8,128)} %get-tuple-element.273.refs_0_, bf16[256,768]{1,0:T(8,128)(2,1)} %copy-done.20, bf16[256,768]{1,0:T(8,128)(2,1)} %copy-done.19, bf16[272,768]{1,0:T(8,128)(2,1)} %own_rows.1.refs_0_.refs_5_.refs_3_, f32[16,768]{1,0:T(8,128)} %get-tuple-element.183.refs_6_.gain_ref.refs_21_.refs_4_, ...), custom_call_target="tpu_custom_call" | custom-call | flops 100000 | bytes 3000 | tf_op jit(solution)/shard_map/input_backward/pallas_call | solution.py:993
  260.7 3.9 %collective-permute-start.54 = (f32[4,384]{1,0:T(4,128)S(1)}, f32[4,384]{1,0:T(4,128)S(1)}, u32[]{:S(2)}, u32[]{:S(2)}) collective-permute-start(f32[4,384]{1,0:T(4,128)S(1)} %select_maximum_fusion), channel_id=1, source_target_pairs={{0,6},{1,7},{2,0},{3,1},{4,2},{5,3},{6,4},{7,5},{8,14},{9,15},{10,... | collective-permute-start | bytes 18440 | tf_op jit(solution)/shard_map/ppermute | solution.py:1029
  269.1 3.4 %collective-permute-start.56 = (f32[192,96]{1,0:T(8,128)S(1)}, f32[192,96]{1,0:T(8,128)S(1)}, u32[]{:S(2)}, u32[]{:S(2)}) collective-permute-start(f32[192,96]{1,0:T(8,128)S(1)} %get-tuple-element.323), channel_id=1, source_target_pairs={{1,0},{4,1},{7,2},{2,3},{5,4},{0,5},{3,6},{6,7},{9,8},{12,9},{15,1... | collective-permute-start | bytes 221192 | tf_op jit(solution)/shard_map/ppermute | solution.py:1302
  272.5 5.7 %collective-permute-start.57 = (f32[192,96]{1,0:T(8,128)S(1)}, f32[192,96]{1,0:T(8,128)S(1)}, u32[]{:S(2)}, u32[]{:S(2)}) collective-permute-start(f32[192,96]{1,0:T(8,128)S(1)} %get-tuple-element.322), channel_id=1, source_target_pairs={{2,0},{5,1},{0,2},{3,3},{6,4},{1,5},{4,6},{7,7},{10,8},{13,9},{8,1... | collective-permute-start | bytes 221192 | tf_op jit(solution)/shard_map/ppermute | solution.py:1302
  279.0 2.8 collective-permute-done.57
  (285 shorter events, 74.5 us)
Async XLA Ops:
  21.0 24.8 %collective-permute-start.6 = (bf16[2,192,384]{2,1,0:T(8,128)(2,1)S(1)}, bf16[2,192,384]{2,1,0:T(8,128)(2,1)S(1)}, u32[]{:S(2)}, u32[]{:S(2)}) collective-permute-start(bf16[2,192,384]{2,1,0:T(8,128)(2,1)S(1)} %pad_maximum_fusion.11), channel_id=1, source_target_pairs={{0,6},{1,7},{2,0},{3,1},{4,2},{5,3},{6,4},{7,5},{8,14},{9,15},{10,... | collective-permute-start | bytes 884744 | tf_op jit(solution)/shard_map/ppermute | solution.py:1029
  22.5 23.5 %collective-permute-start.7 = (bf16[2,192,384]{2,1,0:T(8,128)(2,1)S(1)}, bf16[2,192,384]{2,1,0:T(8,128)(2,1)S(1)}, u32[]{:S(2)}, u32[]{:S(2)}) collective-permute-start(bf16[2,192,384]{2,1,0:T(8,128)(2,1)S(1)} %pad_maximum_fusion.11), channel_id=1, source_target_pairs={{0,2},{1,3},{2,4},{3,5},{4,6},{5,7},{6,0},{7,1},{8,10},{9,11},{10,... | collective-permute-start | bytes 884744 | tf_op jit(solution)/shard_map/ppermute | solution.py:1029
  23.1 37.6 %collective-permute-start.2 = (bf16[272,768]{1,0:T(8,128)(2,1)}, bf16[272,768]{1,0:T(8,128)(2,1)S(1)}, u32[]{:S(2)}, u32[]{:S(2)}) collective-permute-start(bf16[272,768]{1,0:T(8,128)(2,1)} %own_rows.1.refs_0_.refs_5_.refs_3_), channel_id=1, source_target_pairs={{0,2},{1,3},{2,4},{3,5},{4,6},{5,7},{6,0},{7,1},{8,10},{9,11},{10,... | collective-permute-start | bytes 1253384 | tf_op jit(solution)/shard_map/ppermute | solution.py:1029
  23.1 38.5 %collective-permute-start.1 = (bf16[272,768]{1,0:T(8,128)(2,1)}, bf16[272,768]{1,0:T(8,128)(2,1)S(1)}, u32[]{:S(2)}, u32[]{:S(2)}) collective-permute-start(bf16[272,768]{1,0:T(8,128)(2,1)} %own_rows.1.refs_0_.refs_5_.refs_3_), channel_id=1, source_target_pairs={{0,6},{1,7},{2,0},{3,1},{4,2},{5,3},{6,4},{7,5},{8,14},{9,15},{10,... | collective-permute-start | bytes 1253384 | tf_op jit(solution)/shard_map/ppermute | solution.py:1029
  27.2 20.9 %collective-permute-start.13 = (bf16[192,384]{1,0:T(8,128)(2,1)S(1)}, bf16[192,384]{1,0:T(8,128)(2,1)S(1)}, u32[]{:S(2)}, u32[]{:S(2)}) collective-permute-start(bf16[192,384]{1,0:T(8,128)(2,1)S(1)} %pad_maximum_fusion.17), channel_id=1, source_target_pairs={{0,8},{8,0},{16,24},{24,16},{1,9},{9,1},{17,25},{25,17},{2,10},{10... | collective-permute-start | bytes 442376 | tf_op jit(solution)/shard_map/ppermute | solution.py:1025
  46.0 14.5 %collective-permute-start.8 = (bf16[192,384]{1,0:T(8,128)(2,1)S(1)}, bf16[192,384]{1,0:T(8,128)(2,1)S(1)}, u32[]{:S(2)}, u32[]{:S(2)}) collective-permute-start(bf16[192,384]{1,0:T(8,128)(2,1)S(1)} %get-tuple-element.330), channel_id=1, source_target_pairs={{0,2},{1,3},{2,4},{3,5},{4,6},{5,7},{6,0},{7,1},{8,10},{9,11},{10,... | collective-permute-start | bytes 442376 | tf_op jit(solution)/shard_map/ppermute | solution.py:1029
  48.1 16.5 %collective-permute-start.14 = (bf16[2,192,384]{2,1,0:T(8,128)(2,1)S(1)}, bf16[2,192,384]{2,1,0:T(8,128)(2,1)S(1)}, u32[]{:S(2)}, u32[]{:S(2)}) collective-permute-start(bf16[2,192,384]{2,1,0:T(8,128)(2,1)S(1)} %get-tuple-element.325), channel_id=1, source_target_pairs={{0,16},{8,24},{16,0},{24,8},{1,17},{9,25},{17,1},{25,9},{2,18},{10... | collective-permute-start | bytes 884744 | tf_op jit(solution)/shard_map/ppermute | solution.py:1025
  64.8 13.3 %collective-permute-start.15 = (bf16[4,192,384]{2,1,0:T(8,128)(2,1)S(1)}, bf16[4,192,384]{2,1,0:T(8,128)(2,1)S(1)}, u32[]{:S(2)}, u32[]{:S(2)}) collective-permute-start(bf16[4,192,384]{2,1,0:T(8,128)(2,1)S(1)} %bitcast.123), channel_id=1, source_target_pairs={{0,1},{1,0},{2,3},{3,2},{4,5},{5,4},{6,7},{7,6},{8,9},{9,8},{10,11... | collective-permute-start | bytes 1769480 | tf_op jit(solution)/shard_map/ppermute | solution.py:1022
  71.7 25.3 %collective-permute-start.16 = (bf16[4,192,384]{2,1,0:T(8,128)(2,1)S(1)}, bf16[4,192,384]{2,1,0:T(8,128)(2,1)S(1)}, u32[]{:S(2)}, u32[]{:S(2)}) collective-permute-start(bf16[4,192,384]{2,1,0:T(8,128)(2,1)S(1)} %pad_maximum_fusion.3), channel_id=1, source_target_pairs={{0,16},{8,24},{16,0},{24,8},{1,17},{9,25},{17,1},{25,9},{2,18},{10... | collective-permute-start | bytes 1769480 | tf_op jit(solution)/shard_map/ppermute | solution.py:1025
  73.3 23.8 %collective-permute-start.17 = (bf16[4,192,384]{2,1,0:T(8,128)(2,1)S(1)}, bf16[4,192,384]{2,1,0:T(8,128)(2,1)S(1)}, u32[]{:S(2)}, u32[]{:S(2)}) collective-permute-start(bf16[4,192,384]{2,1,0:T(8,128)(2,1)S(1)} %pad_maximum_fusion.4), channel_id=1, source_target_pairs={{0,8},{8,0},{16,24},{24,16},{1,9},{9,1},{17,25},{25,17},{2,10},{10... | collective-permute-start | bytes 1769480 | tf_op jit(solution)/shard_map/ppermute | solution.py:1025
  74.8 22.2 %collective-permute-start.18 = (bf16[192,384]{1,0:T(8,128)(2,1)S(1)}, bf16[192,384]{1,0:T(8,128)(2,1)S(1)}, u32[]{:S(2)}, u32[]{:S(2)}) collective-permute-start(bf16[192,384]{1,0:T(8,128)(2,1)S(1)} %pad_maximum_fusion.18), channel_id=1, source_target_pairs={{0,6},{1,7},{2,0},{3,1},{4,2},{5,3},{6,4},{7,5},{8,14},{9,15},{10,... | collective-permute-start | bytes 442376 | tf_op jit(solution)/shard_map/ppermute | solution.py:1029
  76.9 20.0 %collective-permute-start.19 = (bf16[192,384]{1,0:T(8,128)(2,1)S(1)}, bf16[192,384]{1,0:T(8,128)(2,1)S(1)}, u32[]{:S(2)}, u32[]{:S(2)}) collective-permute-start(bf16[192,384]{1,0:T(8,128)(2,1)S(1)} %pad_maximum_fusion.18), channel_id=1, source_target_pairs={{0,4},{1,5},{2,6},{3,7},{4,0},{5,1},{6,2},{7,3},{8,12},{9,13},{10,... | collective-permute-start | bytes 442376 | tf_op jit(solution)/shard_map/ppermute | solution.py:1029
  78.1 18.9 %collective-permute-start.20 = (bf16[192,384]{1,0:T(8,128)(2,1)S(1)}, bf16[192,384]{1,0:T(8,128)(2,1)S(1)}, u32[]{:S(2)}, u32[]{:S(2)}) collective-permute-start(bf16[192,384]{1,0:T(8,128)(2,1)S(1)} %pad_maximum_fusion.18), channel_id=1, source_target_pairs={{0,2},{1,3},{2,4},{3,5},{4,6},{5,7},{6,0},{7,1},{8,10},{9,11},{10,... | collective-permute-start | bytes 442376 | tf_op jit(solution)/shard_map/ppermute | solution.py:1029
  97.2 29.4 %collective-permute-start.28 = (bf16[2,4,192,384]{3,2,1,0:T(8,128)(2,1)S(1)}, bf16[2,4,192,384]{3,2,1,0:T(8,128)(2,1)}, u32[]{:S(2)}, u32[]{:S(2)}) collective-permute-start(bf16[2,4,192,384]{3,2,1,0:T(8,128)(2,1)S(1)} %pad_maximum_fusion.1.w2a_ref), channel_id=1, source_target_pairs={{0,16},{8,24},{16,0},{24,8},{1,17},{9,25},{17,1},{25,9},{2,18},{10... | collective-permute-start | bytes 3538952 | tf_op jit(solution)/shard_map/ppermute | solution.py:1025
  98.9 27.6 %collective-permute-start.27 = (bf16[2,4,192,384]{3,2,1,0:T(8,128)(2,1)}, bf16[2,4,192,384]{3,2,1,0:T(8,128)(2,1)}, u32[]{:S(2)}, u32[]{:S(2)}) collective-permute-start(bf16[2,4,192,384]{3,2,1,0:T(8,128)(2,1)} %pad_maximum_fusion.w1a_ref), channel_id=1, source_target_pairs={{0,8},{8,0},{16,24},{24,16},{1,9},{9,1},{17,25},{25,17},{2,10},{10... | collective-permute-start | bytes 3538952 | tf_op jit(solution)/shard_map/ppermute | solution.py:1025
  99.6 20.4 %collective-permute-start.21 = (bf16[256,192]{1,0:T(8,128)(2,1)}, bf16[256,192]{1,0:T(8,128)(2,1)S(1)}, u32[]{:S(2)}, u32[]{:S(2)}) collective-permute-start(bf16[256,192]{1,0:T(8,128)(2,1)} %get-tuple-element.177), channel_id=1, source_target_pairs={{0,2},{1,3},{2,4},{3,5},{4,6},{5,7},{6,0},{7,1},{8,10},{9,11},{10,... | collective-permute-start | bytes 294920 | tf_op jit(solution)/shard_map/ppermute | solution.py:1029
  101.4 18.8 %collective-permute-start.22 = (bf16[256,192]{1,0:T(8,128)(2,1)}, bf16[256,192]{1,0:T(8,128)(2,1)}, u32[]{:S(2)}, u32[]{:S(2)}) collective-permute-start(bf16[256,192]{1,0:T(8,128)(2,1)} %get-tuple-element.178), channel_id=1, source_target_pairs={{0,4},{1,5},{2,6},{3,7},{4,0},{5,1},{6,2},{7,3},{8,12},{9,13},{10,... | collective-permute-start | bytes 294920 | tf_op jit(solution)/shard_map/ppermute | solution.py:1029
  148.4 31.6 %collective-permute-start.35 = (bf16[2,4,192,384]{3,2,1,0:T(8,128)(2,1)}, bf16[2,4,192,384]{3,2,1,0:T(8,128)(2,1)S(1)}, u32[]{:S(2)}, u32[]{:S(2)}) collective-permute-start(bf16[2,4,192,384]{3,2,1,0:T(8,128)(2,1)} %get-tuple-element.221), channel_id=1, source_target_pairs={{0,8},{8,0},{16,24},{24,16},{1,9},{9,1},{17,25},{25,17},{2,10},{10... | collective-permute-start | bytes 3538952 | tf_op jit(solution)/shard_map/ppermute | solution.py:1025
  149.9 30.0 %collective-permute-start.36 = (bf16[2,4,192,384]{3,2,1,0:T(8,128)(2,1)}, bf16[2,4,192,384]{3,2,1,0:T(8,128)(2,1)S(1)}, u32[]{:S(2)}, u32[]{:S(2)}) collective-permute-start(bf16[2,4,192,384]{3,2,1,0:T(8,128)(2,1)} %get-tuple-element.222), channel_id=1, source_target_pairs={{0,16},{8,24},{16,0},{24,8},{1,17},{9,25},{17,1},{25,9},{2,18},{10... | collective-permute-start | bytes 3538952 | tf_op jit(solution)/shard_map/ppermute | solution.py:1025
  163.8 13.8 %collective-permute-start.29 = (bf16[256,768]{1,0:T(8,128)(2,1)S(1)}, bf16[256,768]{1,0:T(8,128)(2,1)S(1)}, u32[]{:S(2)}, u32[]{:S(2)}) collective-permute-start(bf16[256,768]{1,0:T(8,128)(2,1)S(1)} %copy-done.44), channel_id=1, source_target_pairs={{0,1},{1,0},{2,3},{3,2},{4,5},{5,4},{6,7},{7,6},{8,9},{9,8},{10,11... | collective-permute-start | bytes 1179656 | tf_op jit(solution)/shard_map/ppermute | solution.py:1022
  181.2 31.4 %collective-permute-start.40 = (bf16[4,192,384]{2,1,0:T(8,128)(2,1)S(1)}, bf16[4,192,384]{2,1,0:T(8,128)(2,1)S(1)}, u32[]{:S(2)}, u32[]{:S(2)}) collective-permute-start(bf16[4,192,384]{2,1,0:T(8,128)(2,1)S(1)} %get-tuple-element.243), channel_id=1, source_target_pairs={{0,16},{8,24},{16,0},{24,8},{1,17},{9,25},{17,1},{25,9},{2,18},{10... | collective-permute-start | bytes 1769480 | tf_op jit(solution)/shard_map/ppermute | solution.py:1025
  181.8 30.7 %collective-permute-start.41 = (bf16[4,192,384]{2,1,0:T(8,128)(2,1)S(1)}, bf16[4,192,384]{2,1,0:T(8,128)(2,1)S(1)}, u32[]{:S(2)}, u32[]{:S(2)}) collective-permute-start(bf16[4,192,384]{2,1,0:T(8,128)(2,1)S(1)} %get-tuple-element.244), channel_id=1, source_target_pairs={{0,8},{8,0},{16,24},{24,16},{1,9},{9,1},{17,25},{25,17},{2,10},{10... | collective-permute-start | bytes 1769480 | tf_op jit(solution)/shard_map/ppermute | solution.py:1025
  183.5 29.0 %collective-permute-start.37 = (bf16[4,192,96]{2,1,0:T(8,128)(2,1)}, bf16[4,192,96]{2,1,0:T(8,128)(2,1)S(1)}, u32[]{:S(2)}, u32[]{:S(2)}) collective-permute-start(bf16[4,192,96]{2,1,0:T(8,128)(2,1)} %get-tuple-element.240), channel_id=1, source_target_pairs={{0,2},{1,3},{2,4},{3,5},{4,6},{5,7},{6,0},{7,1},{8,10},{9,11},{10,... | collective-permute-start | bytes 442376 | tf_op jit(solution)/shard_map/ppermute | solution.py:1029
  190.6 21.8 %collective-permute-start.38 = (bf16[4,192,96]{2,1,0:T(8,128)(2,1)S(1)}, bf16[4,192,96]{2,1,0:T(8,128)(2,1)S(1)}, u32[]{:S(2)}, u32[]{:S(2)}) collective-permute-start(bf16[4,192,96]{2,1,0:T(8,128)(2,1)S(1)} %get-tuple-element.241), channel_id=1, source_target_pairs={{0,4},{1,5},{2,6},{3,7},{4,0},{5,1},{6,2},{7,3},{8,12},{9,13},{10,... | collective-permute-start | bytes 442376 | tf_op jit(solution)/shard_map/ppermute | solution.py:1029
  190.6 21.9 %collective-permute-start.39 = (bf16[4,192,96]{2,1,0:T(8,128)(2,1)S(1)}, bf16[4,192,96]{2,1,0:T(8,128)(2,1)S(1)}, u32[]{:S(2)}, u32[]{:S(2)}) collective-permute-start(bf16[4,192,96]{2,1,0:T(8,128)(2,1)S(1)} %get-tuple-element.242), channel_id=1, source_target_pairs={{0,6},{1,7},{2,0},{3,1},{4,2},{5,3},{6,4},{7,5},{8,14},{9,15},{10,... | collective-permute-start | bytes 442376 | tf_op jit(solution)/shard_map/ppermute | solution.py:1029
  213.7 13.2 %collective-permute-start.43 = (bf16[128,768]{1,0:T(8,128)(2,1)}, bf16[128,768]{1,0:T(8,128)(2,1)S(1)}, u32[]{:S(2)}, u32[]{:S(2)}) collective-permute-start(bf16[128,768]{1,0:T(8,128)(2,1)} %get-tuple-element.248), channel_id=1, source_target_pairs={{0,2},{1,3},{2,4},{3,5},{4,6},{5,7},{6,0},{7,1},{8,10},{9,11},{10,... | collective-permute-start | bytes 589832 | tf_op jit(solution)/shard_map/ppermute | solution.py:1029
  227.1 26.4 %collective-permute-start.46 = (bf16[256,768]{1,0:T(8,128)(2,1)S(1)}, bf16[256,768]{1,0:T(8,128)(2,1)S(1)}, u32[]{:S(2)}, u32[]{:S(2)}) collective-permute-start(bf16[256,768]{1,0:T(8,128)(2,1)S(1)} %pad_maximum_fusion.8), channel_id=1, source_target_pairs={{0,6},{1,7},{2,0},{3,1},{4,2},{5,3},{6,4},{7,5},{8,14},{9,15},{10,... | collective-permute-start | bytes 1179656 | tf_op jit(solution)/shard_map/ppermute | solution.py:1029
  227.8 25.7 %collective-permute-start.45 = (bf16[256,768]{1,0:T(8,128)(2,1)S(1)}, bf16[256,768]{1,0:T(8,128)(2,1)S(1)}, u32[]{:S(2)}, u32[]{:S(2)}) collective-permute-start(bf16[256,768]{1,0:T(8,128)(2,1)S(1)} %pad_maximum_fusion.7), channel_id=1, source_target_pairs={{0,2},{1,3},{2,4},{3,5},{4,6},{5,7},{6,0},{7,1},{8,10},{9,11},{10,... | collective-permute-start | bytes 1179656 | tf_op jit(solution)/shard_map/ppermute | solution.py:1029
  231.1 22.5 %collective-permute-start.49 = (bf16[400,384]{1,0:T(8,128)(2,1)S(1)}, bf16[400,384]{1,0:T(8,128)(2,1)S(1)}, u32[]{:S(2)}, u32[]{:S(2)}) collective-permute-start(bf16[400,384]{1,0:T(8,128)(2,1)S(1)} %pad_maximum_fusion.9), channel_id=1, source_target_pairs={{0,16},{8,24},{16,0},{24,8},{1,17},{9,25},{17,1},{25,9},{2,18},{10... | collective-permute-start | bytes 921608 | tf_op jit(solution)/shard_map/ppermute | solution.py:1025
  232.2 50.5 %collective-permute-start.58 = (bf16[2,192,384]{2,1,0:T(8,128)(2,1)S(1)}, bf16[2,192,384]{2,1,0:T(8,128)(2,1)S(1)}, u32[]{:S(2)}, u32[]{:S(2)}) collective-permute-start(bf16[2,192,384]{2,1,0:T(8,128)(2,1)S(1)} %get-tuple-element.300), channel_id=1, source_target_pairs={{0,2},{1,3},{2,4},{3,5},{4,6},{5,7},{6,0},{7,1},{8,10},{9,11},{10,... | collective-permute-start | bytes 884744 | tf_op jit(solution)/shard_map/ppermute | solution.py:1029
  233.1 49.7 %collective-permute-start.59 = (bf16[2,192,384]{2,1,0:T(8,128)(2,1)S(1)}, bf16[2,192,384]{2,1,0:T(8,128)(2,1)S(1)}, u32[]{:S(2)}, u32[]{:S(2)}) collective-permute-start(bf16[2,192,384]{2,1,0:T(8,128)(2,1)S(1)} %get-tuple-element.299), channel_id=1, source_target_pairs={{0,6},{1,7},{2,0},{3,1},{4,2},{5,3},{6,4},{7,5},{8,14},{9,15},{10,... | collective-permute-start | bytes 884744 | tf_op jit(solution)/shard_map/ppermute | solution.py:1029
  266.1 16.6 %collective-permute-start.60 = (bf16[2,192,384]{2,1,0:T(8,128)(2,1)S(1)}, bf16[2,192,384]{2,1,0:T(8,128)(2,1)S(1)}, u32[]{:S(2)}, u32[]{:S(2)}) collective-permute-start(bf16[2,192,384]{2,1,0:T(8,128)(2,1)S(1)} %get-tuple-element.298), channel_id=1, source_target_pairs={{0,4},{1,5},{2,6},{3,7},{4,0},{5,1},{6,2},{7,3},{8,12},{9,13},{10,... | collective-permute-start | bytes 884744 | tf_op jit(solution)/shard_map/ppermute | solution.py:1029
  (75 other events, 444.6 us)

commit v3 on v2

--- a/solution.py
+++ b/solution.py
@@ -1129,13 +1129,13 @@
                     [(q, (3 * q + i) % 8) for q in range(8)],
                 )
             )
-        parts = jnp.stack(parts)
+        parts = after(jnp.stack(parts), x_before, x_after)
         wq_own = jnp.concatenate(
             [pick(parts, (2 * t + s) % 3) for t in range(3)] + [w_out.astype(BF)], axis=1
         )
         wq_own = jnp.stack([wq_own, links.flip(wq_own, 1)])
         wq_own = jnp.stack([wq_own, links.flip(wq_own, 2)]).reshape(4, 192, 384)
-        wq_own, qkv_order = lax.optimization_barrier((wq_own, qkv_order))
+        wq_own, qkv_order, out_order = lax.optimization_barrier((wq_own, qkv_order, out_order))
         wq = (wq_own, links.core(wq_own))
         wo_own = jnp.concatenate([wq_own[j, :, 288:] for j in range(4)], axis=1)
 

time: 286 us -> 282 us (0.986)
  starting transfers between devices: 82.6 us -> 78 us
    ppermute x3, waiting for transfers between devices: 0.01 us -> 16.7 us  [per_device(): lax.ppermute(wq_parts[:, 96 * i:96 * i + 96], 'seq', [(q, (3 * q + i) % 8...]
    ppermute x30, waiting for transfers between devices: 55.2 us -> 39 us  [shift(): lax.ppermute(v, 'seq', [(s, 2 * ((s // 2 + k) % n) + s % 2) for s in rang...]
    ppermute x3, starting transfers between devices: 9.29 us -> 5.8 us  [per_device(): lax.ppermute(wq_parts[:, 96 * i:96 * i + 96], 'seq', [(q, (3 * q + i) % 8...]
    unnamed x91 -> x93, local copies, waits for them, and re-layouts: 6.82 us -> 7.78 us
  transfers between devices with their start and end apart: 62 -> 62, of which waited for: 14 -> 14; matrix products, arithmetic and copies ran while one was open for 7% -> 8% of each run, Pallas kernels for 28% -> 30%
where the time goes in v3:
time: 282 us; the launch traced here: 281 us
  Pallas kernels  107 us (38%)
  starting transfers between devices  78 us (28%)
  waiting for transfers between devices  61.7 us (22%)
  local copies, waits for them, and re-layouts  17.9 us (6%)
  other arithmetic  14.6 us (5%)
    ppermute x30, starting transfers between devices, shift(): lax.ppermute(v, 'seq', [(s, 2 * ((s // 2 + k) % n) + s % 2) for s in rang...  46.5 us
    ppermute x30, waiting for transfers between devices, shift(): lax.ppermute(v, 'seq', [(s, 2 * ((s // 2 + k) % n) + s % 2) for s in rang...  39 us
    pallas_call x2, Pallas kernels, attention_backward(): pl.pallas_call(kernel, name='attention_backward_last' if last else 'atten...  26.9 us
    pallas_call x1, Pallas kernels, feed_forward(): pl.pallas_call(kernel, name='feed_forward', grid_spec=pltpu.PrefetchScala...  21 us
    ppermute x3, waiting for transfers between devices, per_device(): lax.ppermute(wq_parts[:, 96 * i:96 * i + 96], 'seq', [(q, (3 * q + i) % 8...  16.7 us
    pallas_call x1, Pallas kernels, attention_first(): pl.pallas_call(kernel, name='attention_first', grid_spec=pltpu.PrefetchSc...  16.6 us
    ppermute x12, starting transfers between devices, flip(): return lax.ppermute(v, 'dp', [(i, i ^ bit) for i in range(self.n_dp)])  13.2 us
    ppermute x3, starting transfers between devices, per_device(): lax.ppermute(pick(third, lax.rem(2 * (i - s + 9), 3)), 'seq', [((3 * q +...  9.53 us
  transfers between devices with their start and end apart: 62, of which 14 were waited for; matrix products, arithmetic and copies ran while one was open for 8% of the time, Pallas kernels for 30%

profile of v3, /device:TPU:0, one launch (start us, length us, event | category | flops | bytes accessed | tf_op | source)
XLA Modules:
  0.0 280.8 jit_solution(6023070883247019293)
XLA Ops:
  8.2 4.8 %collective-permute-start.6 = (bf16[2,192,384]{2,1,0:T(8,128)(2,1)S(1)}, bf16[2,192,384]{2,1,0:T(8,128)(2,1)S(1)}, u32[]{:S(2)}, u32[]{:S(2)}) collective-permute-start(bf16[2,192,384]{2,1,0:T(8,128)(2,1)S(1)} %pad_maximum_fusion.11), channel_id=1, source_target_pairs={{0,6},{1,7},{2,0},{3,1},{4,2},{5,3},{6,4},{7,5},{8,14},{9,15},{10,... | collective-permute-start | bytes 884744 | tf_op jit(solution)/shard_map/ppermute | solution.py:1029
  13.7 2.7 own_rows.1.refs_0_.refs_5_.refs_3_
  21.7 4.5 %collective-permute-start.12 = (bf16[192,96]{1,0:T(8,128)(2,1)S(1)}, bf16[192,96]{1,0:T(8,128)(2,1)S(1)}, u32[]{:S(2)}, u32[]{:S(2)}) collective-permute-start(bf16[192,96]{1,0:T(8,128)(2,1)S(1)} %get-tuple-element.340), channel_id=1, source_target_pairs={{0,2},{1,5},{2,0},{3,3},{4,6},{5,1},{6,4},{7,7},{8,10},{9,13},{10,... | collective-permute-start | bytes 110600 | tf_op jit(solution)/shard_map/ppermute | solution.py:1126
  26.3 16.7 %collective-permute-done.11 = bf16[192,96]{1,0:T(8,128)(2,1)S(1)} collective-permute-done((bf16[192,96]{1,0:T(8,128)(2,1)S(1)}, bf16[192,96]{1,0:T(8,128)(2,1)S(1)}, u32[]{:S(2)}, u32[]{:S(2)}) %collective-permute-start.11) | collective-permute-done | bytes 36896 | tf_op jit(solution)/shard_map/ppermute | solution.py:1126
  43.0 3.9 %collective-permute-start.9 = (bf16[192,384]{1,0:T(8,128)(2,1)S(1)}, bf16[192,384]{1,0:T(8,128)(2,1)S(1)}, u32[]{:S(2)}, u32[]{:S(2)}) collective-permute-start(bf16[192,384]{1,0:T(8,128)(2,1)S(1)} %get-tuple-element.331), channel_id=1, source_target_pairs={{0,6},{1,7},{2,0},{3,1},{4,2},{5,3},{6,4},{7,5},{8,14},{9,15},{10,... | collective-permute-start | bytes 442376 | tf_op jit(solution)/shard_map/ppermute | solution.py:1029
  48.7 4.6 %collective-permute-done.7 = bf16[2,192,384]{2,1,0:T(8,128)(2,1)S(1)} collective-permute-done((bf16[2,192,384]{2,1,0:T(8,128)(2,1)S(1)}, bf16[2,192,384]{2,1,0:T(8,128)(2,1)S(1)}, u32[]{:S(2)}, u32[]{:S(2)}) %collective-permute-start.7) | collective-permute-done | bytes 294944 | tf_op jit(solution)/shard_map/ppermute | solution.py:1029
  56.9 3.5 %collective-permute-done.8 = bf16[192,384]{1,0:T(8,128)(2,1)S(1)} collective-permute-done((bf16[192,384]{1,0:T(8,128)(2,1)S(1)}, bf16[192,384]{1,0:T(8,128)(2,1)S(1)}, u32[]{:S(2)}, u32[]{:S(2)}) %collective-permute-start.8) | collective-permute-done | bytes 147488 | tf_op jit(solution)/shard_map/ppermute | solution.py:1029
  60.6 3.9 %collective-permute-start.4 = (bf16[128,768]{1,0:T(8,128)(2,1)S(1)}, bf16[128,768]{1,0:T(8,128)(2,1)S(1)}, u32[]{:S(2)}, u32[]{:S(2)}) collective-permute-start(bf16[128,768]{1,0:T(8,128)(2,1)S(1)} %slice.299), channel_id=1, source_target_pairs={{0,6},{1,7},{2,0},{3,1},{4,2},{5,3},{6,4},{7,5},{8,14},{9,15},{10,... | collective-permute-start | bytes 589832 | tf_op jit(solution)/shard_map/ppermute | solution.py:1029
  64.9 4.4 %collective-permute-done.4.refs_3_ = bf16[128,768]{1,0:T(8,128)(2,1)S(1)} collective-permute-done((bf16[128,768]{1,0:T(8,128)(2,1)S(1)}, bf16[128,768]{1,0:T(8,128)(2,1)S(1)}, u32[]{:S(2)}, u32[]{:S(2)}) %collective-permute-start.4) | collective-permute-done | bytes 196640 | tf_op jit(solution)/shard_map/ppermute | solution.py:1029
  72.4 2.7 collective-permute-start.18
  76.2 16.6 %attention_first.1 = (bf16[1024,768]{1,0:T(8,128)(2,1)}, bf16[1024,256]{1,0:T(8,128)(2,1)}, bf16[1024,256]{1,0:T(8,128)(2,1)}, bf16[1024,256]{1,0:T(8,128)(2,1)}...) custom-call(s32[3]{0:T(128)} %pad_add_fusion.place_ref, ...), custom_call_target="tpu_custom_call" | custom-call | flops 8000000 | bytes 8000 | tf_op jit(solution)/shard_map/attention_first/pallas_call | solution.py:424
  95.9 8.3 %attention_rest.1 = (bf16[256,192]{1,0:T(8,128)(2,1)}, f32[256,256]{1,0:T(8,128)}, f32[8,256]{1,0:T(8,128)}, bf16[256,192]{1,0:T(8,128)(2,1)}, f32[256,256]{1,0:T(8,128)}, /*index=5*/f32[8,256]{1,0:T(8,128)}) custom-call(bf16[1024,256]{1,0:T(8,128)(2,1)} %get-tuple-element.175.q_ref.refs_3_.refs_9_, ...), custom_call_target="tpu_custom_call" | custom-call | flops 5000000 | bytes 4000 | tf_op jit(solution)/shard_map/attention_rest/pallas_call | solution.py:460
  104.2 3.1 %collective-permute-start.23 = (bf16[256,192]{1,0:T(8,128)(2,1)}, bf16[256,192]{1,0:T(8,128)(2,1)S(1)}, u32[]{:S(2)}, u32[]{:S(2)}) collective-permute-start(bf16[256,192]{1,0:T(8,128)(2,1)} %get-tuple-element.183), channel_id=1, source_target_pairs={{0,6},{1,7},{2,0},{3,1},{4,2},{5,3},{6,4},{7,5},{8,14},{9,15},{10,... | collective-permute-start | bytes 294920 | tf_op jit(solution)/shard_map/ppermute | solution.py:1029
  111.2 5.7 %reorder_out.1.refs_4_.w_ref = bf16[4,192,768]{2,1,0:T(8,128)(2,1)} custom-call(s32[3]{0:T(128)} %pad_add_fusion.place_ref, bf16[4,192,384]{2,1,0:T(8,128)(2,1)} %copy-done.5, bf16[4,192,384]{2,1,0:T(8,128)(2,1)} %copy-done.18, bf16[768,768]{1,0:T(8,128)(2,1)} %select_convert_fusion.refs_6_.order_ref.refs_5_.refs_23_), custom_call_target="tpu_custom_call" | custom-call | flops 1000000 | bytes 3000 | tf_op jit(solution)/shard_map/reorder_out/pallas_call | solution.py:665
  117.0 3.3 %collective-permute-done.22.refs_2_ = bf16[256,192]{1,0:T(8,128)(2,1)} collective-permute-done((bf16[256,192]{1,0:T(8,128)(2,1)}, bf16[256,192]{1,0:T(8,128)(2,1)}, u32[]{:S(2)}, u32[]{:S(2)}) %collective-permute-start.22) | collective-permute-done | bytes 98336 | tf_op jit(solution)/shard_map/ppermute | solution.py:1029
  120.3 3.9 %output_projection.1 = (f32[256,768]{1,0:T(8,128)}, bf16[256,768]{1,0:T(8,128)(2,1)}) custom-call(s32[3]{0:T(128)} %pad_add_fusion.place_ref, bf16[256,192]{1,0:T(8,128)(2,1)} %get-tuple-element.180.refs_0_, bf16[256,192]{1,0:T(8,128)(2,1)} %collective-permute-done.21.refs_1_, bf16[256,192]{1,0:T(8,128)(2,1)} %collective-permute-done.22.refs_2_, ...), custom_call_target="tpu_custom_call" | custom-call | flops 1000000 | bytes 3000 | tf_op jit(solution)/shard_map/output_projection/pallas_call | solution.py:755
  126.8 21.0 %feed_forward.1 = (f32[256,768]{1,0:T(8,128)}, bf16[256,768]{1,0:T(8,128)(2,1)}, f32[256,768]{1,0:T(8,128)}, bf16[256,768]{1,0:T(8,128)(2,1)}, bf16[2,4,192,384]...) custom-call(s32[3]{0:T(128)} %pad_add_fusion.place_ref, ...), custom_call_target="tpu_custom_call" | custom-call | flops 7200000 | bytes 15000 | tf_op jit(solution)/shard_map/feed_forward/pallas_call | solution.py:886
  151.4 4.8 %residual_backward.1 = (f32[256,768]{1,0:T(8,128)}, bf16[256,768]{1,0:T(8,128)(2,1)}, f32[16,768]{1,0:T(8,128)}, bf16[256,192]{1,0:T(8,128)(2,1)}, bf16[256,192]...) custom-call(s32[3]{0:T(128)} %pad_add_fusion.place_ref, f32[256,768]{1,0:T(8,128)} %get-tuple-element.194.gh_ref, ...), custom_call_target="tpu_custom_call" | custom-call | flops 1000000 | bytes 4000 | tf_op jit(solution)/shard_map/residual_backward/pallas_call | solution.py:956
  156.2 2.6 collective-permute-start.31
  159.4 3.6 %collective-permute-done.31.refs_0_ = bf16[256,192]{1,0:T(8,128)(2,1)S(1)} collective-permute-done((bf16[256,192]{1,0:T(8,128)(2,1)}, bf16[256,192]{1,0:T(8,128)(2,1)S(1)}, u32[]{:S(2)}, u32[]{:S(2)}) %collective-permute-start.31) | collective-permute-done | bytes 98336 | tf_op jit(solution)/shard_map/ppermute | solution.py:1029
  163.7 7.6 %attention_backward_own.1 = (bf16[256,256]{1,0:T(8,128)(2,1)}, f32[1024,256]{1,0:T(8,128)}, f32[1024,256]{1,0:T(8,128)}) custom-call(bf16[256,192]{1,0:T(8,128)(2,1)} %get-tuple-element.196.refs_0_, f32[256,256]{1,0:T(8,128)} %get-tuple-element.197.refs_1_, f32[8,256]{1,0:T(8,128)} %get-tuple-element.198.refs_2_, ...), custom_call_target="tpu_custom_call" | custom-call | flops 3000000 | bytes 10000 | tf_op jit(solution)/shard_map/attention_backward_own/pallas_call | solution.py:625
  171.3 4.9 %out_weight.1 = (bf16[4,192,384]{2,1,0:T(8,128)(2,1)}, bf16[4,192,384]{2,1,0:T(8,128)(2,1)}) custom-call(s32[3]{0:T(128)} %pad_add_fusion.place_ref, bf16[256,192]{1,0:T(8,128)(2,1)} %get-tuple-element.180.refs_0_, bf16[256,192]{1,0:T(8,128)(2,1)} %collective-permute-done.21.refs_1_, bf16[256,192]{1,0:T(8,128)(2,1)} %collective-permute-done.22.refs_2_, ...), custom_call_target="tpu_custom_call" | custom-call | flops 1000000 | bytes 4000 | tf_op jit(solution)/shard_map/out_weight/pallas_call | solution.py:723
  183.5 4.8 %collective-permute-start.38 = (bf16[4,192,96]{2,1,0:T(8,128)(2,1)S(1)}, bf16[4,192,96]{2,1,0:T(8,128)(2,1)S(1)}, u32[]{:S(2)}, u32[]{:S(2)}) collective-permute-start(bf16[4,192,96]{2,1,0:T(8,128)(2,1)S(1)} %get-tuple-element.245), channel_id=1, source_target_pairs={{0,4},{1,5},{2,6},{3,7},{4,0},{5,1},{6,2},{7,3},{8,12},{9,13},{10,... | collective-permute-start | bytes 442376 | tf_op jit(solution)/shard_map/ppermute | solution.py:1029
  189.1 19.3 %attention_backward_last.1 = (bf16[1024,768]{1,0:T(8,128)(2,1)}, f32[16,384]{1,0:T(8,128)}, f32[16,384]{1,0:T(8,128)}, f32[256,768]{1,0:T(8,128)}, bf16[256,768]...) custom-call(bf16[256,192]{1,0:T(8,128)(2,1)} %copy-done.39, ...), custom_call_target="tpu_custom_call" | custom-call | flops 9000000 | bytes 10000 | tf_op jit(solution)/shard_map/attention_backward_last/pallas_call | solution.py:625
  210.9 2.6 collective-permute-start.44
  215.5 6.5 %qkv_weight.1 = (bf16[4,192,288]{2,1,0:T(8,128)(2,1)}, bf16[4,192,288]{2,1,0:T(8,128)(2,1)}) custom-call(s32[3]{0:T(128)} %pad_add_fusion.place_ref, bf16[768,1024]{1,0:T(8,128)(2,1)} %bitcast.122, bf16[1024,768]{1,0:T(8,128)(2,1)} %get-tuple-element.254.g_ref, bf16[768,768]{1,0:T(8,128)(2,1)} %select_convert_fusion.1.order_ref), custom_call_target="tpu_custom_call" | custom-call | flops 2000000 | bytes 5000 | tf_op jit(solution)/shard_map/qkv_weight/pallas_call | solution.py:692
  228.9 3.3 %collective-permute-start.59 = (bf16[2,192,384]{2,1,0:T(8,128)(2,1)S(1)}, bf16[2,192,384]{2,1,0:T(8,128)(2,1)S(1)}, u32[]{:S(2)}, u32[]{:S(2)}) collective-permute-start(bf16[2,192,384]{2,1,0:T(8,128)(2,1)S(1)} %get-tuple-element.303), channel_id=1, source_target_pairs={{0,6},{1,7},{2,0},{3,1},{4,2},{5,3},{6,4},{7,5},{8,14},{9,15},{10,... | collective-permute-start | bytes 884744 | tf_op jit(solution)/shard_map/ppermute | solution.py:1029
  232.3 17.2 %collective-permute-done.46.refs_2_ = bf16[256,768]{1,0:T(8,128)(2,1)S(1)} collective-permute-done((bf16[256,768]{1,0:T(8,128)(2,1)S(1)}, bf16[256,768]{1,0:T(8,128)(2,1)S(1)}, u32[]{:S(2)}, u32[]{:S(2)}) %collective-permute-start.46) | collective-permute-done | bytes 393248 | tf_op jit(solution)/shard_map/ppermute | solution.py:1029
  250.4 3.1 %input_backward.1 = bf16[256,768]{1,0:T(8,128)(2,1)} custom-call(f32[256,768]{1,0:T(8,128)} %get-tuple-element.277.refs_0_, bf16[256,768]{1,0:T(8,128)(2,1)} %copy-done.21, bf16[256,768]{1,0:T(8,128)(2,1)} %copy-done.20, bf16[272,768]{1,0:T(8,128)(2,1)} %own_rows.1.refs_0_.refs_5_.refs_3_, f32[16,768]{1,0:T(8,128)} %get-tuple-element.187.refs_6_.gain_ref.refs_21_.refs_4_, ...), custom_call_target="tpu_custom_call" | custom-call | flops 100000 | bytes 3000 | tf_op jit(solution)/shard_map/input_backward/pallas_call | solution.py:993
  256.5 3.9 %collective-permute-start.54 = (f32[4,384]{1,0:T(4,128)S(1)}, f32[4,384]{1,0:T(4,128)S(1)}, u32[]{:S(2)}, u32[]{:S(2)}) collective-permute-start(f32[4,384]{1,0:T(4,128)S(1)} %select_maximum_fusion), channel_id=1, source_target_pairs={{0,6},{1,7},{2,0},{3,1},{4,2},{5,3},{6,4},{7,5},{8,14},{9,15},{10,... | collective-permute-start | bytes 18440 | tf_op jit(solution)/shard_map/ppermute | solution.py:1029
  265.1 3.2 %collective-permute-start.56 = (f32[192,96]{1,0:T(8,128)S(1)}, f32[192,96]{1,0:T(8,128)S(1)}, u32[]{:S(2)}, u32[]{:S(2)}) collective-permute-start(f32[192,96]{1,0:T(8,128)S(1)} %get-tuple-element.327), channel_id=1, source_target_pairs={{1,0},{4,1},{7,2},{2,3},{5,4},{0,5},{3,6},{6,7},{9,8},{12,9},{15,1... | collective-permute-start | bytes 221192 | tf_op jit(solution)/shard_map/ppermute | solution.py:1302
  268.3 5.7 %collective-permute-start.57 = (f32[192,96]{1,0:T(8,128)S(1)}, f32[192,96]{1,0:T(8,128)S(1)}, u32[]{:S(2)}, u32[]{:S(2)}) collective-permute-start(f32[192,96]{1,0:T(8,128)S(1)} %get-tuple-element.326), channel_id=1, source_target_pairs={{2,0},{5,1},{0,2},{3,3},{6,4},{1,5},{4,6},{7,7},{10,8},{13,9},{8,1... | collective-permute-start | bytes 221192 | tf_op jit(solution)/shard_map/ppermute | solution.py:1302
  (287 shorter events, 72.5 us)
Async XLA Ops:
  8.2 34.8 %collective-permute-start.6 = (bf16[2,192,384]{2,1,0:T(8,128)(2,1)S(1)}, bf16[2,192,384]{2,1,0:T(8,128)(2,1)S(1)}, u32[]{:S(2)}, u32[]{:S(2)}) collective-permute-start(bf16[2,192,384]{2,1,0:T(8,128)(2,1)S(1)} %pad_maximum_fusion.11), channel_id=1, source_target_pairs={{0,6},{1,7},{2,0},{3,1},{4,2},{5,3},{6,4},{7,5},{8,14},{9,15},{10,... | collective-permute-start | bytes 884744 | tf_op jit(solution)/shard_map/ppermute | solution.py:1029
  18.9 28.0 %collective-permute-start.1 = (bf16[272,768]{1,0:T(8,128)(2,1)S(1)}, bf16[272,768]{1,0:T(8,128)(2,1)S(1)}, u32[]{:S(2)}, u32[]{:S(2)}) collective-permute-start(bf16[272,768]{1,0:T(8,128)(2,1)S(1)} %copy-done), channel_id=1, source_target_pairs={{0,6},{1,7},{2,0},{3,1},{4,2},{5,3},{6,4},{7,5},{8,14},{9,15},{10,... | collective-permute-start | bytes 1253384 | tf_op jit(solution)/shard_map/ppermute | solution.py:1029
  20.6 26.3 %collective-permute-start.2 = (bf16[272,768]{1,0:T(8,128)(2,1)S(1)}, bf16[272,768]{1,0:T(8,128)(2,1)S(1)}, u32[]{:S(2)}, u32[]{:S(2)}) collective-permute-start(bf16[272,768]{1,0:T(8,128)(2,1)S(1)} %copy-done), channel_id=1, source_target_pairs={{0,2},{1,3},{2,4},{3,5},{4,6},{5,7},{6,0},{7,1},{8,10},{9,11},{10,... | collective-permute-start | bytes 1253384 | tf_op jit(solution)/shard_map/ppermute | solution.py:1029
  21.1 21.8 %collective-permute-start.11 = (bf16[192,96]{1,0:T(8,128)(2,1)S(1)}, bf16[192,96]{1,0:T(8,128)(2,1)S(1)}, u32[]{:S(2)}, u32[]{:S(2)}) collective-permute-start(bf16[192,96]{1,0:T(8,128)(2,1)S(1)} %get-tuple-element.341), channel_id=1, source_target_pairs={{0,1},{1,4},{2,7},{3,2},{4,5},{5,0},{6,3},{7,6},{8,9},{9,12},{10,1... | collective-permute-start | bytes 110600 | tf_op jit(solution)/shard_map/ppermute | solution.py:1126
  21.7 21.3 %collective-permute-start.12 = (bf16[192,96]{1,0:T(8,128)(2,1)S(1)}, bf16[192,96]{1,0:T(8,128)(2,1)S(1)}, u32[]{:S(2)}, u32[]{:S(2)}) collective-permute-start(bf16[192,96]{1,0:T(8,128)(2,1)S(1)} %get-tuple-element.340), channel_id=1, source_target_pairs={{0,2},{1,5},{2,0},{3,3},{4,6},{5,1},{6,4},{7,7},{8,10},{9,13},{10,... | collective-permute-start | bytes 110600 | tf_op jit(solution)/shard_map/ppermute | solution.py:1126
  43.0 13.7 %collective-permute-start.9 = (bf16[192,384]{1,0:T(8,128)(2,1)S(1)}, bf16[192,384]{1,0:T(8,128)(2,1)S(1)}, u32[]{:S(2)}, u32[]{:S(2)}) collective-permute-start(bf16[192,384]{1,0:T(8,128)(2,1)S(1)} %get-tuple-element.331), channel_id=1, source_target_pairs={{0,6},{1,7},{2,0},{3,1},{4,2},{5,3},{6,4},{7,5},{8,14},{9,15},{10,... | collective-permute-start | bytes 442376 | tf_op jit(solution)/shard_map/ppermute | solution.py:1029
  69.3 23.5 %collective-permute-start.16 = (bf16[4,192,384]{2,1,0:T(8,128)(2,1)S(1)}, bf16[4,192,384]{2,1,0:T(8,128)(2,1)S(1)}, u32[]{:S(2)}, u32[]{:S(2)}) collective-permute-start(bf16[4,192,384]{2,1,0:T(8,128)(2,1)S(1)} %pad_maximum_fusion.3), channel_id=1, source_target_pairs={{0,16},{8,24},{16,0},{24,8},{1,17},{9,25},{17,1},{25,9},{2,18},{10... | collective-permute-start | bytes 1769480 | tf_op jit(solution)/shard_map/ppermute | solution.py:1025
  70.9 21.9 %collective-permute-start.17 = (bf16[4,192,384]{2,1,0:T(8,128)(2,1)S(1)}, bf16[4,192,384]{2,1,0:T(8,128)(2,1)S(1)}, u32[]{:S(2)}, u32[]{:S(2)}) collective-permute-start(bf16[4,192,384]{2,1,0:T(8,128)(2,1)S(1)} %pad_maximum_fusion.4), channel_id=1, source_target_pairs={{0,8},{8,0},{16,24},{24,16},{1,9},{9,1},{17,25},{25,17},{2,10},{10... | collective-permute-start | bytes 1769480 | tf_op jit(solution)/shard_map/ppermute | solution.py:1025
  72.4 20.4 %collective-permute-start.18 = (bf16[192,384]{1,0:T(8,128)(2,1)S(1)}, bf16[192,384]{1,0:T(8,128)(2,1)S(1)}, u32[]{:S(2)}, u32[]{:S(2)}) collective-permute-start(bf16[192,384]{1,0:T(8,128)(2,1)S(1)} %pad_maximum_fusion.18), channel_id=1, source_target_pairs={{0,6},{1,7},{2,0},{3,1},{4,2},{5,3},{6,4},{7,5},{8,14},{9,15},{10,... | collective-permute-start | bytes 442376 | tf_op jit(solution)/shard_map/ppermute | solution.py:1029
  75.1 17.7 %collective-permute-start.19 = (bf16[192,384]{1,0:T(8,128)(2,1)S(1)}, bf16[192,384]{1,0:T(8,128)(2,1)S(1)}, u32[]{:S(2)}, u32[]{:S(2)}) collective-permute-start(bf16[192,384]{1,0:T(8,128)(2,1)S(1)} %pad_maximum_fusion.18), channel_id=1, source_target_pairs={{0,4},{1,5},{2,6},{3,7},{4,0},{5,1},{6,2},{7,3},{8,12},{9,13},{10,... | collective-permute-start | bytes 442376 | tf_op jit(solution)/shard_map/ppermute | solution.py:1029
  75.1 17.7 %collective-permute-start.20 = (bf16[192,384]{1,0:T(8,128)(2,1)S(1)}, bf16[192,384]{1,0:T(8,128)(2,1)S(1)}, u32[]{:S(2)}, u32[]{:S(2)}) collective-permute-start(bf16[192,384]{1,0:T(8,128)(2,1)S(1)} %pad_maximum_fusion.18), channel_id=1, source_target_pairs={{0,2},{1,3},{2,4},{3,5},{4,6},{5,7},{6,0},{7,1},{8,10},{9,11},{10,... | collective-permute-start | bytes 442376 | tf_op jit(solution)/shard_map/ppermute | solution.py:1029
  93.0 33.1 %collective-permute-start.28 = (bf16[2,4,192,384]{3,2,1,0:T(8,128)(2,1)S(1)}, bf16[2,4,192,384]{3,2,1,0:T(8,128)(2,1)}, u32[]{:S(2)}, u32[]{:S(2)}) collective-permute-start(bf16[2,4,192,384]{3,2,1,0:T(8,128)(2,1)S(1)} %pad_maximum_fusion.1.w2a_ref), channel_id=1, source_target_pairs={{0,16},{8,24},{16,0},{24,8},{1,17},{9,25},{17,1},{25,9},{2,18},{10... | collective-permute-start | bytes 3538952 | tf_op jit(solution)/shard_map/ppermute | solution.py:1025
  94.7 31.4 %collective-permute-start.27 = (bf16[2,4,192,384]{3,2,1,0:T(8,128)(2,1)}, bf16[2,4,192,384]{3,2,1,0:T(8,128)(2,1)}, u32[]{:S(2)}, u32[]{:S(2)}) collective-permute-start(bf16[2,4,192,384]{3,2,1,0:T(8,128)(2,1)} %pad_maximum_fusion.w1a_ref), channel_id=1, source_target_pairs={{0,8},{8,0},{16,24},{24,16},{1,9},{9,1},{17,25},{25,17},{2,10},{10... | collective-permute-start | bytes 3538952 | tf_op jit(solution)/shard_map/ppermute | solution.py:1025
  104.2 12.7 %collective-permute-start.23 = (bf16[256,192]{1,0:T(8,128)(2,1)}, bf16[256,192]{1,0:T(8,128)(2,1)S(1)}, u32[]{:S(2)}, u32[]{:S(2)}) collective-permute-start(bf16[256,192]{1,0:T(8,128)(2,1)} %get-tuple-element.183), channel_id=1, source_target_pairs={{0,6},{1,7},{2,0},{3,1},{4,2},{5,3},{6,4},{7,5},{8,14},{9,15},{10,... | collective-permute-start | bytes 294920 | tf_op jit(solution)/shard_map/ppermute | solution.py:1029
  148.0 31.7 %collective-permute-start.35 = (bf16[2,4,192,384]{3,2,1,0:T(8,128)(2,1)}, bf16[2,4,192,384]{3,2,1,0:T(8,128)(2,1)S(1)}, u32[]{:S(2)}, u32[]{:S(2)}) collective-permute-start(bf16[2,4,192,384]{3,2,1,0:T(8,128)(2,1)} %get-tuple-element.225), channel_id=1, source_target_pairs={{0,8},{8,0},{16,24},{24,16},{1,9},{9,1},{17,25},{25,17},{2,10},{10... | collective-permute-start | bytes 3538952 | tf_op jit(solution)/shard_map/ppermute | solution.py:1025
  149.2 30.5 %collective-permute-start.36 = (bf16[2,4,192,384]{3,2,1,0:T(8,128)(2,1)}, bf16[2,4,192,384]{3,2,1,0:T(8,128)(2,1)S(1)}, u32[]{:S(2)}, u32[]{:S(2)}) collective-permute-start(bf16[2,4,192,384]{3,2,1,0:T(8,128)(2,1)} %get-tuple-element.226), channel_id=1, source_target_pairs={{0,16},{8,24},{16,0},{24,8},{1,17},{9,25},{17,1},{25,9},{2,18},{10... | collective-permute-start | bytes 3538952 | tf_op jit(solution)/shard_map/ppermute | solution.py:1025
  158.9 12.4 %collective-permute-start.32 = (bf16[256,192]{1,0:T(8,128)(2,1)}, bf16[256,192]{1,0:T(8,128)(2,1)S(1)}, u32[]{:S(2)}, u32[]{:S(2)}) collective-permute-start(bf16[256,192]{1,0:T(8,128)(2,1)} %get-tuple-element.206), channel_id=1, source_target_pairs={{0,4},{1,5},{2,6},{3,7},{4,0},{5,1},{6,2},{7,3},{8,12},{9,13},{10,... | collective-permute-start | bytes 294920 | tf_op jit(solution)/shard_map/ppermute | solution.py:1029
  158.9 12.5 %collective-permute-start.33 = (bf16[256,192]{1,0:T(8,128)(2,1)}, bf16[256,192]{1,0:T(8,128)(2,1)S(1)}, u32[]{:S(2)}, u32[]{:S(2)}) collective-permute-start(bf16[256,192]{1,0:T(8,128)(2,1)} %get-tuple-element.207), channel_id=1, source_target_pairs={{0,2},{1,3},{2,4},{3,5},{4,6},{5,7},{6,0},{7,1},{8,10},{9,11},{10,... | collective-permute-start | bytes 294920 | tf_op jit(solution)/shard_map/ppermute | solution.py:1029
  163.7 13.8 %collective-permute-start.29 = (bf16[256,768]{1,0:T(8,128)(2,1)S(1)}, bf16[256,768]{1,0:T(8,128)(2,1)S(1)}, u32[]{:S(2)}, u32[]{:S(2)}) collective-permute-start(bf16[256,768]{1,0:T(8,128)(2,1)S(1)} %copy-done.45), channel_id=1, source_target_pairs={{0,1},{1,0},{2,3},{3,2},{4,5},{5,4},{6,7},{7,6},{8,9},{9,8},{10,11... | collective-permute-start | bytes 1179656 | tf_op jit(solution)/shard_map/ppermute | solution.py:1022
  181.4 27.1 %collective-permute-start.40 = (bf16[4,192,384]{2,1,0:T(8,128)(2,1)S(1)}, bf16[4,192,384]{2,1,0:T(8,128)(2,1)S(1)}, u32[]{:S(2)}, u32[]{:S(2)}) collective-permute-start(bf16[4,192,384]{2,1,0:T(8,128)(2,1)S(1)} %get-tuple-element.247), channel_id=1, source_target_pairs={{0,16},{8,24},{16,0},{24,8},{1,17},{9,25},{17,1},{25,9},{2,18},{10... | collective-permute-start | bytes 1769480 | tf_op jit(solution)/shard_map/ppermute | solution.py:1025
  182.0 26.6 %collective-permute-start.41 = (bf16[4,192,384]{2,1,0:T(8,128)(2,1)S(1)}, bf16[4,192,384]{2,1,0:T(8,128)(2,1)S(1)}, u32[]{:S(2)}, u32[]{:S(2)}) collective-permute-start(bf16[4,192,384]{2,1,0:T(8,128)(2,1)S(1)} %get-tuple-element.248), channel_id=1, source_target_pairs={{0,8},{8,0},{16,24},{24,16},{1,9},{9,1},{17,25},{25,17},{2,10},{10... | collective-permute-start | bytes 1769480 | tf_op jit(solution)/shard_map/ppermute | solution.py:1025
  183.5 25.0 %collective-permute-start.37 = (bf16[4,192,96]{2,1,0:T(8,128)(2,1)}, bf16[4,192,96]{2,1,0:T(8,128)(2,1)S(1)}, u32[]{:S(2)}, u32[]{:S(2)}) collective-permute-start(bf16[4,192,96]{2,1,0:T(8,128)(2,1)} %get-tuple-element.244), channel_id=1, source_target_pairs={{0,2},{1,3},{2,4},{3,5},{4,6},{5,7},{6,0},{7,1},{8,10},{9,11},{10,... | collective-permute-start | bytes 442376 | tf_op jit(solution)/shard_map/ppermute | solution.py:1029
  183.5 25.0 %collective-permute-start.38 = (bf16[4,192,96]{2,1,0:T(8,128)(2,1)S(1)}, bf16[4,192,96]{2,1,0:T(8,128)(2,1)S(1)}, u32[]{:S(2)}, u32[]{:S(2)}) collective-permute-start(bf16[4,192,96]{2,1,0:T(8,128)(2,1)S(1)} %get-tuple-element.245), channel_id=1, source_target_pairs={{0,4},{1,5},{2,6},{3,7},{4,0},{5,1},{6,2},{7,3},{8,12},{9,13},{10,... | collective-permute-start | bytes 442376 | tf_op jit(solution)/shard_map/ppermute | solution.py:1029
  188.3 20.2 %collective-permute-start.39 = (bf16[4,192,96]{2,1,0:T(8,128)(2,1)S(1)}, bf16[4,192,96]{2,1,0:T(8,128)(2,1)S(1)}, u32[]{:S(2)}, u32[]{:S(2)}) collective-permute-start(bf16[4,192,96]{2,1,0:T(8,128)(2,1)S(1)} %get-tuple-element.246), channel_id=1, source_target_pairs={{0,6},{1,7},{2,0},{3,1},{4,2},{5,3},{6,4},{7,5},{8,14},{9,15},{10,... | collective-permute-start | bytes 442376 | tf_op jit(solution)/shard_map/ppermute | solution.py:1029
  209.5 12.5 %collective-permute-start.48 = (f32[16,384]{1,0:T(8,128)}, f32[16,384]{1,0:T(8,128)S(1)}, u32[]{:S(2)}, u32[]{:S(2)}) collective-permute-start(f32[16,384]{1,0:T(8,128)} %get-tuple-element.275), channel_id=1, source_target_pairs={{0,1},{1,0},{2,3},{3,2},{4,5},{5,4},{6,7},{7,6},{8,9},{9,8},{10,11... | collective-permute-start | bytes 73736 | tf_op jit(solution)/shard_map/ppermute | solution.py:1022
  209.7 13.2 %collective-permute-start.43 = (bf16[128,768]{1,0:T(8,128)(2,1)}, bf16[128,768]{1,0:T(8,128)(2,1)S(1)}, u32[]{:S(2)}, u32[]{:S(2)}) collective-permute-start(bf16[128,768]{1,0:T(8,128)(2,1)} %get-tuple-element.252), channel_id=1, source_target_pairs={{0,2},{1,3},{2,4},{3,5},{4,6},{5,7},{6,0},{7,1},{8,10},{9,11},{10,... | collective-permute-start | bytes 589832 | tf_op jit(solution)/shard_map/ppermute | solution.py:1029
  223.1 26.4 %collective-permute-start.46 = (bf16[256,768]{1,0:T(8,128)(2,1)S(1)}, bf16[256,768]{1,0:T(8,128)(2,1)S(1)}, u32[]{:S(2)}, u32[]{:S(2)}) collective-permute-start(bf16[256,768]{1,0:T(8,128)(2,1)S(1)} %pad_maximum_fusion.8), channel_id=1, source_target_pairs={{0,6},{1,7},{2,0},{3,1},{4,2},{5,3},{6,4},{7,5},{8,14},{9,15},{10,... | collective-permute-start | bytes 1179656 | tf_op jit(solution)/shard_map/ppermute | solution.py:1029
  224.8 24.7 %collective-permute-start.45 = (bf16[256,768]{1,0:T(8,128)(2,1)S(1)}, bf16[256,768]{1,0:T(8,128)(2,1)S(1)}, u32[]{:S(2)}, u32[]{:S(2)}) collective-permute-start(bf16[256,768]{1,0:T(8,128)(2,1)S(1)} %pad_maximum_fusion.7), channel_id=1, source_target_pairs={{0,2},{1,3},{2,4},{3,5},{4,6},{5,7},{6,0},{7,1},{8,10},{9,11},{10,... | collective-permute-start | bytes 1179656 | tf_op jit(solution)/shard_map/ppermute | solution.py:1029
  227.4 22.1 %collective-permute-start.49 = (bf16[400,384]{1,0:T(8,128)(2,1)S(1)}, bf16[400,384]{1,0:T(8,128)(2,1)S(1)}, u32[]{:S(2)}, u32[]{:S(2)}) collective-permute-start(bf16[400,384]{1,0:T(8,128)(2,1)S(1)} %pad_maximum_fusion.9), channel_id=1, source_target_pairs={{0,16},{8,24},{16,0},{24,8},{1,17},{9,25},{17,1},{25,9},{2,18},{10... | collective-permute-start | bytes 921608 | tf_op jit(solution)/shard_map/ppermute | solution.py:1025
  228.4 49.1 %collective-permute-start.58 = (bf16[2,192,384]{2,1,0:T(8,128)(2,1)S(1)}, bf16[2,192,384]{2,1,0:T(8,128)(2,1)S(1)}, u32[]{:S(2)}, u32[]{:S(2)}) collective-permute-start(bf16[2,192,384]{2,1,0:T(8,128)(2,1)S(1)} %get-tuple-element.304), channel_id=1, source_target_pairs={{0,2},{1,3},{2,4},{3,5},{4,6},{5,7},{6,0},{7,1},{8,10},{9,11},{10,... | collective-permute-start | bytes 884744 | tf_op jit(solution)/shard_map/ppermute | solution.py:1029
  228.9 48.6 %collective-permute-start.59 = (bf16[2,192,384]{2,1,0:T(8,128)(2,1)S(1)}, bf16[2,192,384]{2,1,0:T(8,128)(2,1)S(1)}, u32[]{:S(2)}, u32[]{:S(2)}) collective-permute-start(bf16[2,192,384]{2,1,0:T(8,128)(2,1)S(1)} %get-tuple-element.303), channel_id=1, source_target_pairs={{0,6},{1,7},{2,0},{3,1},{4,2},{5,3},{6,4},{7,5},{8,14},{9,15},{10,... | collective-permute-start | bytes 884744 | tf_op jit(solution)/shard_map/ppermute | solution.py:1029
  261.9 15.5 %collective-permute-start.60 = (bf16[2,192,384]{2,1,0:T(8,128)(2,1)S(1)}, bf16[2,192,384]{2,1,0:T(8,128)(2,1)S(1)}, u32[]{:S(2)}, u32[]{:S(2)}) collective-permute-start(bf16[2,192,384]{2,1,0:T(8,128)(2,1)S(1)} %get-tuple-element.302), channel_id=1, source_target_pairs={{0,4},{1,5},{2,6},{3,7},{4,0},{5,1},{6,2},{7,3},{8,12},{9,13},{10,... | collective-permute-start | bytes 884744 | tf_op jit(solution)/shard_map/ppermute | solution.py:1029
  (76 other events, 444.5 us)

commit v4 on v3

--- a/solution.py
+++ b/solution.py
@@ -1296,7 +1296,7 @@
         vec = sum([vec[0]] + [links.shift(vec[k], k) for k in range(1, 4)])
         vecs = (vec[0, :96], vec[1, :96], vec[3], vec[2, :96])
         g_out = joint[:, 288:]
-        third = jnp.stack([joint[:, 96 * t : 96 * t + 96] for t in range(3)])
+        third = jnp.stack([joint[:, 96 * t : 96 * t + 96] for t in range(3)]).astype(BF)
         g_qkv = jnp.concatenate(
             [
                 lax.ppermute(
@@ -1307,7 +1307,7 @@
                 for i in range(3)
             ],
             axis=1,
-        )
+        ).astype(F32)
         dw_came, _ = lax.optimization_barrier((dw_came, (vecs, g_qkv, grad_rows)))
         dw_came = [v.astype(F32) for v in dw_came]
         dw = jnp.stack([dw1[0], dw2[0]]) + dw_came[0] + dw_came[1] + dw_came[2]

time: 282 us -> 281 us (level)
  transfers between devices with their start and end apart: 62 -> 62, of which waited for: 14 -> 13; matrix products, arithmetic and copies ran while one was open for 8% -> 8% of each run, Pallas kernels for 30% -> 30%
where the time goes in v4:
time: 281 us; the launch traced here: 280 us
  Pallas kernels  107 us (38%)
  starting transfers between devices  78.8 us (28%)
  waiting for transfers between devices  60.2 us (21%)
  local copies, waits for them, and re-layouts  17.4 us (6%)
  other arithmetic  14.5 us (5%)
    ppermute x30, starting transfers between devices, shift(): lax.ppermute(v, 'seq', [(s, 2 * ((s // 2 + k) % n) + s % 2) for s in rang...  47.1 us
    ppermute x30, waiting for transfers between devices, shift(): lax.ppermute(v, 'seq', [(s, 2 * ((s // 2 + k) % n) + s % 2) for s in rang...  38.1 us
    pallas_call x2, Pallas kernels, attention_backward(): pl.pallas_call(kernel, name='attention_backward_last' if last else 'atten...  27 us
    pallas_call x1, Pallas kernels, feed_forward(): pl.pallas_call(kernel, name='feed_forward', grid_spec=pltpu.PrefetchScala...  21 us
    ppermute x3, waiting for transfers between devices, per_device(): lax.ppermute(wq_parts[:, 96 * i:96 * i + 96], 'seq', [(q, (3 * q + i) % 8...  16.7 us
    pallas_call x1, Pallas kernels, attention_first(): pl.pallas_call(kernel, name='attention_first', grid_spec=pltpu.PrefetchSc...  16.6 us
    ppermute x12, starting transfers between devices, flip(): return lax.ppermute(v, 'dp', [(i, i ^ bit) for i in range(self.n_dp)])  13.9 us
    ppermute x3, starting transfers between devices, per_device(): lax.ppermute(pick(third, lax.rem(2 * (i - s + 9), 3)), 'seq', [((3 * q +...  10.3 us
  transfers between devices with their start and end apart: 62, of which 13 were waited for; matrix products, arithmetic and copies ran while one was open for 8% of the time, Pallas kernels for 30%

profile of v4, /device:TPU:0, one launch (start us, length us, event | category | flops | bytes accessed | tf_op | source)
XLA Modules:
  0.0 279.7 jit_solution(9257525586288107154)
XLA Ops:
  2.5 2.4 message_rows.1
  8.2 4.8 %collective-permute-start.6 = (bf16[2,192,384]{2,1,0:T(8,128)(2,1)S(1)}, bf16[2,192,384]{2,1,0:T(8,128)(2,1)S(1)}, u32[]{:S(2)}, u32[]{:S(2)}) collective-permute-start(bf16[2,192,384]{2,1,0:T(8,128)(2,1)S(1)} %pad_maximum_fusion.11), channel_id=1, source_target_pairs={{0,6},{1,7},{2,0},{3,1},{4,2},{5,3},{6,4},{7,5},{8,14},{9,15},{10,... | collective-permute-start | bytes 884744 | tf_op jit(solution)/shard_map/ppermute | solution.py:1029
  13.7 2.6 own_rows.1.refs_0_.refs_5_.refs_3_
  21.7 4.5 %collective-permute-start.12 = (bf16[192,96]{1,0:T(8,128)(2,1)S(1)}, bf16[192,96]{1,0:T(8,128)(2,1)S(1)}, u32[]{:S(2)}, u32[]{:S(2)}) collective-permute-start(bf16[192,96]{1,0:T(8,128)(2,1)S(1)} %get-tuple-element.341), channel_id=1, source_target_pairs={{0,2},{1,5},{2,0},{3,3},{4,6},{5,1},{6,4},{7,7},{8,10},{9,13},{10,... | collective-permute-start | bytes 110600 | tf_op jit(solution)/shard_map/ppermute | solution.py:1126
  26.3 16.7 %collective-permute-done.11 = bf16[192,96]{1,0:T(8,128)(2,1)S(1)} collective-permute-done((bf16[192,96]{1,0:T(8,128)(2,1)S(1)}, bf16[192,96]{1,0:T(8,128)(2,1)S(1)}, u32[]{:S(2)}, u32[]{:S(2)}) %collective-permute-start.11) | collective-permute-done | bytes 36896 | tf_op jit(solution)/shard_map/ppermute | solution.py:1126
  43.0 3.9 %collective-permute-start.9 = (bf16[192,384]{1,0:T(8,128)(2,1)S(1)}, bf16[192,384]{1,0:T(8,128)(2,1)S(1)}, u32[]{:S(2)}, u32[]{:S(2)}) collective-permute-start(bf16[192,384]{1,0:T(8,128)(2,1)S(1)} %get-tuple-element.326), channel_id=1, source_target_pairs={{0,6},{1,7},{2,0},{3,1},{4,2},{5,3},{6,4},{7,5},{8,14},{9,15},{10,... | collective-permute-start | bytes 442376 | tf_op jit(solution)/shard_map/ppermute | solution.py:1029
  48.6 4.6 %collective-permute-done.7 = bf16[2,192,384]{2,1,0:T(8,128)(2,1)S(1)} collective-permute-done((bf16[2,192,384]{2,1,0:T(8,128)(2,1)S(1)}, bf16[2,192,384]{2,1,0:T(8,128)(2,1)S(1)}, u32[]{:S(2)}, u32[]{:S(2)}) %collective-permute-start.7) | collective-permute-done | bytes 294944 | tf_op jit(solution)/shard_map/ppermute | solution.py:1029
  56.9 3.5 %collective-permute-done.8 = bf16[192,384]{1,0:T(8,128)(2,1)S(1)} collective-permute-done((bf16[192,384]{1,0:T(8,128)(2,1)S(1)}, bf16[192,384]{1,0:T(8,128)(2,1)S(1)}, u32[]{:S(2)}, u32[]{:S(2)}) %collective-permute-start.8) | collective-permute-done | bytes 147488 | tf_op jit(solution)/shard_map/ppermute | solution.py:1029
  60.6 3.9 %collective-permute-start.4 = (bf16[128,768]{1,0:T(8,128)(2,1)S(1)}, bf16[128,768]{1,0:T(8,128)(2,1)S(1)}, u32[]{:S(2)}, u32[]{:S(2)}) collective-permute-start(bf16[128,768]{1,0:T(8,128)(2,1)S(1)} %slice.302), channel_id=1, source_target_pairs={{0,6},{1,7},{2,0},{3,1},{4,2},{5,3},{6,4},{7,5},{8,14},{9,15},{10,... | collective-permute-start | bytes 589832 | tf_op jit(solution)/shard_map/ppermute | solution.py:1029
  64.9 4.4 %collective-permute-done.4.refs_3_ = bf16[128,768]{1,0:T(8,128)(2,1)S(1)} collective-permute-done((bf16[128,768]{1,0:T(8,128)(2,1)S(1)}, bf16[128,768]{1,0:T(8,128)(2,1)S(1)}, u32[]{:S(2)}, u32[]{:S(2)}) %collective-permute-start.4) | collective-permute-done | bytes 196640 | tf_op jit(solution)/shard_map/ppermute | solution.py:1029
  72.4 2.7 collective-permute-start.18
  76.2 16.6 %attention_first.1 = (bf16[1024,768]{1,0:T(8,128)(2,1)}, bf16[1024,256]{1,0:T(8,128)(2,1)}, bf16[1024,256]{1,0:T(8,128)(2,1)}, bf16[1024,256]{1,0:T(8,128)(2,1)}...) custom-call(s32[3]{0:T(128)} %pad_add_fusion.place_ref, ...), custom_call_target="tpu_custom_call" | custom-call | flops 8000000 | bytes 8000 | tf_op jit(solution)/shard_map/attention_first/pallas_call | solution.py:424
  95.9 8.4 %attention_rest.1 = (bf16[256,192]{1,0:T(8,128)(2,1)}, f32[256,256]{1,0:T(8,128)}, f32[8,256]{1,0:T(8,128)}, bf16[256,192]{1,0:T(8,128)(2,1)}, f32[256,256]{1,0:T(8,128)}, /*index=5*/f32[8,256]{1,0:T(8,128)}) custom-call(bf16[1024,256]{1,0:T(8,128)(2,1)} %get-tuple-element.175.q_ref.refs_3_.refs_9_, ...), custom_call_target="tpu_custom_call" | custom-call | flops 5000000 | bytes 4000 | tf_op jit(solution)/shard_map/attention_rest/pallas_call | solution.py:460
  104.2 3.0 %collective-permute-start.23 = (bf16[256,192]{1,0:T(8,128)(2,1)}, bf16[256,192]{1,0:T(8,128)(2,1)S(1)}, u32[]{:S(2)}, u32[]{:S(2)}) collective-permute-start(bf16[256,192]{1,0:T(8,128)(2,1)} %get-tuple-element.183), channel_id=1, source_target_pairs={{0,6},{1,7},{2,0},{3,1},{4,2},{5,3},{6,4},{7,5},{8,14},{9,15},{10,... | collective-permute-start | bytes 294920 | tf_op jit(solution)/shard_map/ppermute | solution.py:1029
  111.2 5.8 %reorder_out.1.refs_4_.w_ref = bf16[4,192,768]{2,1,0:T(8,128)(2,1)} custom-call(s32[3]{0:T(128)} %pad_add_fusion.place_ref, bf16[4,192,384]{2,1,0:T(8,128)(2,1)} %copy-done.5, bf16[4,192,384]{2,1,0:T(8,128)(2,1)} %copy-done.18, bf16[768,768]{1,0:T(8,128)(2,1)} %select_convert_fusion.refs_6_.order_ref.refs_5_.refs_23_), custom_call_target="tpu_custom_call" | custom-call | flops 1000000 | bytes 3000 | tf_op jit(solution)/shard_map/reorder_out/pallas_call | solution.py:665
  117.0 3.2 %collective-permute-done.22.refs_2_ = bf16[256,192]{1,0:T(8,128)(2,1)} collective-permute-done((bf16[256,192]{1,0:T(8,128)(2,1)}, bf16[256,192]{1,0:T(8,128)(2,1)}, u32[]{:S(2)}, u32[]{:S(2)}) %collective-permute-start.22) | collective-permute-done | bytes 98336 | tf_op jit(solution)/shard_map/ppermute | solution.py:1029
  120.3 3.9 %output_projection.1 = (f32[256,768]{1,0:T(8,128)}, bf16[256,768]{1,0:T(8,128)(2,1)}) custom-call(s32[3]{0:T(128)} %pad_add_fusion.place_ref, bf16[256,192]{1,0:T(8,128)(2,1)} %get-tuple-element.180.refs_0_, bf16[256,192]{1,0:T(8,128)(2,1)} %collective-permute-done.21.refs_1_, bf16[256,192]{1,0:T(8,128)(2,1)} %collective-permute-done.22.refs_2_, ...), custom_call_target="tpu_custom_call" | custom-call | flops 1000000 | bytes 3000 | tf_op jit(solution)/shard_map/output_projection/pallas_call | solution.py:755
  126.8 21.0 %feed_forward.1 = (f32[256,768]{1,0:T(8,128)}, bf16[256,768]{1,0:T(8,128)(2,1)}, f32[256,768]{1,0:T(8,128)}, bf16[256,768]{1,0:T(8,128)(2,1)}, bf16[2,4,192,384]...) custom-call(s32[3]{0:T(128)} %pad_add_fusion.place_ref, ...), custom_call_target="tpu_custom_call" | custom-call | flops 7200000 | bytes 15000 | tf_op jit(solution)/shard_map/feed_forward/pallas_call | solution.py:886
  151.4 4.8 %residual_backward.1 = (f32[256,768]{1,0:T(8,128)}, bf16[256,768]{1,0:T(8,128)(2,1)}, f32[16,768]{1,0:T(8,128)}, bf16[256,192]{1,0:T(8,128)(2,1)}, bf16[256,192]...) custom-call(s32[3]{0:T(128)} %pad_add_fusion.place_ref, f32[256,768]{1,0:T(8,128)} %get-tuple-element.194.gh_ref, ...), custom_call_target="tpu_custom_call" | custom-call | flops 1000000 | bytes 4000 | tf_op jit(solution)/shard_map/residual_backward/pallas_call | solution.py:956
  156.2 2.6 collective-permute-start.31
  159.4 3.6 %collective-permute-done.31.refs_0_ = bf16[256,192]{1,0:T(8,128)(2,1)S(1)} collective-permute-done((bf16[256,192]{1,0:T(8,128)(2,1)}, bf16[256,192]{1,0:T(8,128)(2,1)S(1)}, u32[]{:S(2)}, u32[]{:S(2)}) %collective-permute-start.31) | collective-permute-done | bytes 98336 | tf_op jit(solution)/shard_map/ppermute | solution.py:1029
  163.7 7.6 %attention_backward_own.1 = (bf16[256,256]{1,0:T(8,128)(2,1)}, f32[1024,256]{1,0:T(8,128)}, f32[1024,256]{1,0:T(8,128)}) custom-call(bf16[256,192]{1,0:T(8,128)(2,1)} %get-tuple-element.196.refs_0_, f32[256,256]{1,0:T(8,128)} %get-tuple-element.197.refs_1_, f32[8,256]{1,0:T(8,128)} %get-tuple-element.198.refs_2_, ...), custom_call_target="tpu_custom_call" | custom-call | flops 3000000 | bytes 10000 | tf_op jit(solution)/shard_map/attention_backward_own/pallas_call | solution.py:625
  171.4 4.9 %out_weight.1 = (bf16[4,192,384]{2,1,0:T(8,128)(2,1)}, bf16[4,192,384]{2,1,0:T(8,128)(2,1)}) custom-call(s32[3]{0:T(128)} %pad_add_fusion.place_ref, bf16[256,192]{1,0:T(8,128)(2,1)} %get-tuple-element.180.refs_0_, bf16[256,192]{1,0:T(8,128)(2,1)} %collective-permute-done.21.refs_1_, bf16[256,192]{1,0:T(8,128)(2,1)} %collective-permute-done.22.refs_2_, ...), custom_call_target="tpu_custom_call" | custom-call | flops 1000000 | bytes 4000 | tf_op jit(solution)/shard_map/out_weight/pallas_call | solution.py:723
  183.6 4.8 %collective-permute-start.38 = (bf16[4,192,96]{2,1,0:T(8,128)(2,1)S(1)}, bf16[4,192,96]{2,1,0:T(8,128)(2,1)S(1)}, u32[]{:S(2)}, u32[]{:S(2)}) collective-permute-start(bf16[4,192,96]{2,1,0:T(8,128)(2,1)S(1)} %get-tuple-element.245), channel_id=1, source_target_pairs={{0,4},{1,5},{2,6},{3,7},{4,0},{5,1},{6,2},{7,3},{8,12},{9,13},{10,... | collective-permute-start | bytes 442376 | tf_op jit(solution)/shard_map/ppermute | solution.py:1029
  189.2 19.4 %attention_backward_last.1 = (bf16[1024,768]{1,0:T(8,128)(2,1)}, f32[16,384]{1,0:T(8,128)}, f32[16,384]{1,0:T(8,128)}, f32[256,768]{1,0:T(8,128)}, bf16[256,768]...) custom-call(bf16[256,192]{1,0:T(8,128)(2,1)} %copy-done.39, ...), custom_call_target="tpu_custom_call" | custom-call | flops 9000000 | bytes 10000 | tf_op jit(solution)/shard_map/attention_backward_last/pallas_call | solution.py:625
  211.0 2.6 collective-permute-start.44
  215.6 6.5 %qkv_weight.1 = (bf16[4,192,288]{2,1,0:T(8,128)(2,1)}, bf16[4,192,288]{2,1,0:T(8,128)(2,1)}) custom-call(s32[3]{0:T(128)} %pad_add_fusion.place_ref, bf16[768,1024]{1,0:T(8,128)(2,1)} %bitcast.122, bf16[1024,768]{1,0:T(8,128)(2,1)} %get-tuple-element.254.g_ref, bf16[768,768]{1,0:T(8,128)(2,1)} %select_convert_fusion.1.order_ref), custom_call_target="tpu_custom_call" | custom-call | flops 2000000 | bytes 5000 | tf_op jit(solution)/shard_map/qkv_weight/pallas_call | solution.py:692
  229.0 3.4 %collective-permute-start.59 = (bf16[2,192,384]{2,1,0:T(8,128)(2,1)S(1)}, bf16[2,192,384]{2,1,0:T(8,128)(2,1)S(1)}, u32[]{:S(2)}, u32[]{:S(2)}) collective-permute-start(bf16[2,192,384]{2,1,0:T(8,128)(2,1)S(1)} %get-tuple-element.303), channel_id=1, source_target_pairs={{0,6},{1,7},{2,0},{3,1},{4,2},{5,3},{6,4},{7,5},{8,14},{9,15},{10,... | collective-permute-start | bytes 884744 | tf_op jit(solution)/shard_map/ppermute | solution.py:1029
  232.4 17.2 %collective-permute-done.46.refs_2_ = bf16[256,768]{1,0:T(8,128)(2,1)S(1)} collective-permute-done((bf16[256,768]{1,0:T(8,128)(2,1)S(1)}, bf16[256,768]{1,0:T(8,128)(2,1)S(1)}, u32[]{:S(2)}, u32[]{:S(2)}) %collective-permute-start.46) | collective-permute-done | bytes 393248 | tf_op jit(solution)/shard_map/ppermute | solution.py:1029
  250.6 3.1 %input_backward.1 = bf16[256,768]{1,0:T(8,128)(2,1)} custom-call(f32[256,768]{1,0:T(8,128)} %get-tuple-element.277.refs_0_, bf16[256,768]{1,0:T(8,128)(2,1)} %copy-done.21, bf16[256,768]{1,0:T(8,128)(2,1)} %copy-done.20, bf16[272,768]{1,0:T(8,128)(2,1)} %own_rows.1.refs_0_.refs_5_.refs_3_, f32[16,768]{1,0:T(8,128)} %get-tuple-element.187.refs_6_.gain_ref.refs_21_.refs_4_, ...), custom_call_target="tpu_custom_call" | custom-call | flops 100000 | bytes 3000 | tf_op jit(solution)/shard_map/input_backward/pallas_call | solution.py:993
  256.1 3.9 %collective-permute-start.54 = (f32[4,384]{1,0:T(4,128)S(1)}, f32[4,384]{1,0:T(4,128)S(1)}, u32[]{:S(2)}, u32[]{:S(2)}) collective-permute-start(f32[4,384]{1,0:T(4,128)S(1)} %select_maximum_fusion), channel_id=1, source_target_pairs={{0,6},{1,7},{2,0},{3,1},{4,2},{5,3},{6,4},{7,5},{8,14},{9,15},{10,... | collective-permute-start | bytes 18440 | tf_op jit(solution)/shard_map/ppermute | solution.py:1029
  264.7 9.6 %collective-permute-start.57 = (bf16[192,96]{1,0:T(8,128)(2,1)S(1)}, bf16[192,96]{1,0:T(8,128)(2,1)S(1)}, u32[]{:S(2)}, u32[]{:S(2)}) collective-permute-start(bf16[192,96]{1,0:T(8,128)(2,1)S(1)} %get-tuple-element.332), channel_id=1, source_target_pairs={{2,0},{5,1},{0,2},{3,3},{6,4},{1,5},{4,6},{7,7},{10,8},{13,9},{8,1... | collective-permute-start | bytes 110600 | tf_op jit(solution)/shard_map/ppermute | solution.py:1302
  (288 shorter events, 68.1 us)
Async XLA Ops:
  8.2 34.8 %collective-permute-start.6 = (bf16[2,192,384]{2,1,0:T(8,128)(2,1)S(1)}, bf16[2,192,384]{2,1,0:T(8,128)(2,1)S(1)}, u32[]{:S(2)}, u32[]{:S(2)}) collective-permute-start(bf16[2,192,384]{2,1,0:T(8,128)(2,1)S(1)} %pad_maximum_fusion.11), channel_id=1, source_target_pairs={{0,6},{1,7},{2,0},{3,1},{4,2},{5,3},{6,4},{7,5},{8,14},{9,15},{10,... | collective-permute-start | bytes 884744 | tf_op jit(solution)/shard_map/ppermute | solution.py:1029
  18.9 28.0 %collective-permute-start.1 = (bf16[272,768]{1,0:T(8,128)(2,1)S(1)}, bf16[272,768]{1,0:T(8,128)(2,1)S(1)}, u32[]{:S(2)}, u32[]{:S(2)}) collective-permute-start(bf16[272,768]{1,0:T(8,128)(2,1)S(1)} %copy-done), channel_id=1, source_target_pairs={{0,6},{1,7},{2,0},{3,1},{4,2},{5,3},{6,4},{7,5},{8,14},{9,15},{10,... | collective-permute-start | bytes 1253384 | tf_op jit(solution)/shard_map/ppermute | solution.py:1029
  20.6 26.3 %collective-permute-start.2 = (bf16[272,768]{1,0:T(8,128)(2,1)S(1)}, bf16[272,768]{1,0:T(8,128)(2,1)S(1)}, u32[]{:S(2)}, u32[]{:S(2)}) collective-permute-start(bf16[272,768]{1,0:T(8,128)(2,1)S(1)} %copy-done), channel_id=1, source_target_pairs={{0,2},{1,3},{2,4},{3,5},{4,6},{5,7},{6,0},{7,1},{8,10},{9,11},{10,... | collective-permute-start | bytes 1253384 | tf_op jit(solution)/shard_map/ppermute | solution.py:1029
  21.1 21.8 %collective-permute-start.11 = (bf16[192,96]{1,0:T(8,128)(2,1)S(1)}, bf16[192,96]{1,0:T(8,128)(2,1)S(1)}, u32[]{:S(2)}, u32[]{:S(2)}) collective-permute-start(bf16[192,96]{1,0:T(8,128)(2,1)S(1)} %get-tuple-element.342), channel_id=1, source_target_pairs={{0,1},{1,4},{2,7},{3,2},{4,5},{5,0},{6,3},{7,6},{8,9},{9,12},{10,1... | collective-permute-start | bytes 110600 | tf_op jit(solution)/shard_map/ppermute | solution.py:1126
  21.7 21.3 %collective-permute-start.12 = (bf16[192,96]{1,0:T(8,128)(2,1)S(1)}, bf16[192,96]{1,0:T(8,128)(2,1)S(1)}, u32[]{:S(2)}, u32[]{:S(2)}) collective-permute-start(bf16[192,96]{1,0:T(8,128)(2,1)S(1)} %get-tuple-element.341), channel_id=1, source_target_pairs={{0,2},{1,5},{2,0},{3,3},{4,6},{5,1},{6,4},{7,7},{8,10},{9,13},{10,... | collective-permute-start | bytes 110600 | tf_op jit(solution)/shard_map/ppermute | solution.py:1126
  43.0 13.8 %collective-permute-start.9 = (bf16[192,384]{1,0:T(8,128)(2,1)S(1)}, bf16[192,384]{1,0:T(8,128)(2,1)S(1)}, u32[]{:S(2)}, u32[]{:S(2)}) collective-permute-start(bf16[192,384]{1,0:T(8,128)(2,1)S(1)} %get-tuple-element.326), channel_id=1, source_target_pairs={{0,6},{1,7},{2,0},{3,1},{4,2},{5,3},{6,4},{7,5},{8,14},{9,15},{10,... | collective-permute-start | bytes 442376 | tf_op jit(solution)/shard_map/ppermute | solution.py:1029
  69.3 23.5 %collective-permute-start.16 = (bf16[4,192,384]{2,1,0:T(8,128)(2,1)S(1)}, bf16[4,192,384]{2,1,0:T(8,128)(2,1)S(1)}, u32[]{:S(2)}, u32[]{:S(2)}) collective-permute-start(bf16[4,192,384]{2,1,0:T(8,128)(2,1)S(1)} %pad_maximum_fusion.3), channel_id=1, source_target_pairs={{0,16},{8,24},{16,0},{24,8},{1,17},{9,25},{17,1},{25,9},{2,18},{10... | collective-permute-start | bytes 1769480 | tf_op jit(solution)/shard_map/ppermute | solution.py:1025
  70.9 21.9 %collective-permute-start.17 = (bf16[4,192,384]{2,1,0:T(8,128)(2,1)S(1)}, bf16[4,192,384]{2,1,0:T(8,128)(2,1)S(1)}, u32[]{:S(2)}, u32[]{:S(2)}) collective-permute-start(bf16[4,192,384]{2,1,0:T(8,128)(2,1)S(1)} %pad_maximum_fusion.4), channel_id=1, source_target_pairs={{0,8},{8,0},{16,24},{24,16},{1,9},{9,1},{17,25},{25,17},{2,10},{10... | collective-permute-start | bytes 1769480 | tf_op jit(solution)/shard_map/ppermute | solution.py:1025
  72.4 20.4 %collective-permute-start.18 = (bf16[192,384]{1,0:T(8,128)(2,1)S(1)}, bf16[192,384]{1,0:T(8,128)(2,1)S(1)}, u32[]{:S(2)}, u32[]{:S(2)}) collective-permute-start(bf16[192,384]{1,0:T(8,128)(2,1)S(1)} %pad_maximum_fusion.16), channel_id=1, source_target_pairs={{0,6},{1,7},{2,0},{3,1},{4,2},{5,3},{6,4},{7,5},{8,14},{9,15},{10,... | collective-permute-start | bytes 442376 | tf_op jit(solution)/shard_map/ppermute | solution.py:1029
  75.1 17.7 %collective-permute-start.19 = (bf16[192,384]{1,0:T(8,128)(2,1)S(1)}, bf16[192,384]{1,0:T(8,128)(2,1)S(1)}, u32[]{:S(2)}, u32[]{:S(2)}) collective-permute-start(bf16[192,384]{1,0:T(8,128)(2,1)S(1)} %pad_maximum_fusion.16), channel_id=1, source_target_pairs={{0,4},{1,5},{2,6},{3,7},{4,0},{5,1},{6,2},{7,3},{8,12},{9,13},{10,... | collective-permute-start | bytes 442376 | tf_op jit(solution)/shard_map/ppermute | solution.py:1029
  75.1 17.7 %collective-permute-start.20 = (bf16[192,384]{1,0:T(8,128)(2,1)S(1)}, bf16[192,384]{1,0:T(8,128)(2,1)S(1)}, u32[]{:S(2)}, u32[]{:S(2)}) collective-permute-start(bf16[192,384]{1,0:T(8,128)(2,1)S(1)} %pad_maximum_fusion.16), channel_id=1, source_target_pairs={{0,2},{1,3},{2,4},{3,5},{4,6},{5,7},{6,0},{7,1},{8,10},{9,11},{10,... | collective-permute-start | bytes 442376 | tf_op jit(solution)/shard_map/ppermute | solution.py:1029
  93.0 33.1 %collective-permute-start.28 = (bf16[2,4,192,384]{3,2,1,0:T(8,128)(2,1)S(1)}, bf16[2,4,192,384]{3,2,1,0:T(8,128)(2,1)}, u32[]{:S(2)}, u32[]{:S(2)}) collective-permute-start(bf16[2,4,192,384]{3,2,1,0:T(8,128)(2,1)S(1)} %pad_maximum_fusion.1.w2a_ref), channel_id=1, source_target_pairs={{0,16},{8,24},{16,0},{24,8},{1,17},{9,25},{17,1},{25,9},{2,18},{10... | collective-permute-start | bytes 3538952 | tf_op jit(solution)/shard_map/ppermute | solution.py:1025
  94.7 31.4 %collective-permute-start.27 = (bf16[2,4,192,384]{3,2,1,0:T(8,128)(2,1)}, bf16[2,4,192,384]{3,2,1,0:T(8,128)(2,1)}, u32[]{:S(2)}, u32[]{:S(2)}) collective-permute-start(bf16[2,4,192,384]{3,2,1,0:T(8,128)(2,1)} %pad_maximum_fusion.w1a_ref), channel_id=1, source_target_pairs={{0,8},{8,0},{16,24},{24,16},{1,9},{9,1},{17,25},{25,17},{2,10},{10... | collective-permute-start | bytes 3538952 | tf_op jit(solution)/shard_map/ppermute | solution.py:1025
  104.2 12.7 %collective-permute-start.23 = (bf16[256,192]{1,0:T(8,128)(2,1)}, bf16[256,192]{1,0:T(8,128)(2,1)S(1)}, u32[]{:S(2)}, u32[]{:S(2)}) collective-permute-start(bf16[256,192]{1,0:T(8,128)(2,1)} %get-tuple-element.183), channel_id=1, source_target_pairs={{0,6},{1,7},{2,0},{3,1},{4,2},{5,3},{6,4},{7,5},{8,14},{9,15},{10,... | collective-permute-start | bytes 294920 | tf_op jit(solution)/shard_map/ppermute | solution.py:1029
  148.0 31.7 %collective-permute-start.35 = (bf16[2,4,192,384]{3,2,1,0:T(8,128)(2,1)}, bf16[2,4,192,384]{3,2,1,0:T(8,128)(2,1)S(1)}, u32[]{:S(2)}, u32[]{:S(2)}) collective-permute-start(bf16[2,4,192,384]{3,2,1,0:T(8,128)(2,1)} %get-tuple-element.225), channel_id=1, source_target_pairs={{0,8},{8,0},{16,24},{24,16},{1,9},{9,1},{17,25},{25,17},{2,10},{10... | collective-permute-start | bytes 3538952 | tf_op jit(solution)/shard_map/ppermute | solution.py:1025
  149.1 30.5 %collective-permute-start.36 = (bf16[2,4,192,384]{3,2,1,0:T(8,128)(2,1)}, bf16[2,4,192,384]{3,2,1,0:T(8,128)(2,1)S(1)}, u32[]{:S(2)}, u32[]{:S(2)}) collective-permute-start(bf16[2,4,192,384]{3,2,1,0:T(8,128)(2,1)} %get-tuple-element.226), channel_id=1, source_target_pairs={{0,16},{8,24},{16,0},{24,8},{1,17},{9,25},{17,1},{25,9},{2,18},{10... | collective-permute-start | bytes 3538952 | tf_op jit(solution)/shard_map/ppermute | solution.py:1025
  158.8 12.5 %collective-permute-start.32 = (bf16[256,192]{1,0:T(8,128)(2,1)}, bf16[256,192]{1,0:T(8,128)(2,1)S(1)}, u32[]{:S(2)}, u32[]{:S(2)}) collective-permute-start(bf16[256,192]{1,0:T(8,128)(2,1)} %get-tuple-element.206), channel_id=1, source_target_pairs={{0,4},{1,5},{2,6},{3,7},{4,0},{5,1},{6,2},{7,3},{8,12},{9,13},{10,... | collective-permute-start | bytes 294920 | tf_op jit(solution)/shard_map/ppermute | solution.py:1029
  158.8 12.5 %collective-permute-start.33 = (bf16[256,192]{1,0:T(8,128)(2,1)}, bf16[256,192]{1,0:T(8,128)(2,1)S(1)}, u32[]{:S(2)}, u32[]{:S(2)}) collective-permute-start(bf16[256,192]{1,0:T(8,128)(2,1)} %get-tuple-element.207), channel_id=1, source_target_pairs={{0,2},{1,3},{2,4},{3,5},{4,6},{5,7},{6,0},{7,1},{8,10},{9,11},{10,... | collective-permute-start | bytes 294920 | tf_op jit(solution)/shard_map/ppermute | solution.py:1029
  163.7 13.8 %collective-permute-start.29 = (bf16[256,768]{1,0:T(8,128)(2,1)S(1)}, bf16[256,768]{1,0:T(8,128)(2,1)S(1)}, u32[]{:S(2)}, u32[]{:S(2)}) collective-permute-start(bf16[256,768]{1,0:T(8,128)(2,1)S(1)} %copy-done.45), channel_id=1, source_target_pairs={{0,1},{1,0},{2,3},{3,2},{4,5},{5,4},{6,7},{7,6},{8,9},{9,8},{10,11... | collective-permute-start | bytes 1179656 | tf_op jit(solution)/shard_map/ppermute | solution.py:1022
  181.4 27.2 %collective-permute-start.40 = (bf16[4,192,384]{2,1,0:T(8,128)(2,1)S(1)}, bf16[4,192,384]{2,1,0:T(8,128)(2,1)S(1)}, u32[]{:S(2)}, u32[]{:S(2)}) collective-permute-start(bf16[4,192,384]{2,1,0:T(8,128)(2,1)S(1)} %get-tuple-element.247), channel_id=1, source_target_pairs={{0,16},{8,24},{16,0},{24,8},{1,17},{9,25},{17,1},{25,9},{2,18},{10... | collective-permute-start | bytes 1769480 | tf_op jit(solution)/shard_map/ppermute | solution.py:1025
  182.1 26.6 %collective-permute-start.41 = (bf16[4,192,384]{2,1,0:T(8,128)(2,1)S(1)}, bf16[4,192,384]{2,1,0:T(8,128)(2,1)S(1)}, u32[]{:S(2)}, u32[]{:S(2)}) collective-permute-start(bf16[4,192,384]{2,1,0:T(8,128)(2,1)S(1)} %get-tuple-element.248), channel_id=1, source_target_pairs={{0,8},{8,0},{16,24},{24,16},{1,9},{9,1},{17,25},{25,17},{2,10},{10... | collective-permute-start | bytes 1769480 | tf_op jit(solution)/shard_map/ppermute | solution.py:1025
  183.5 25.1 %collective-permute-start.37 = (bf16[4,192,96]{2,1,0:T(8,128)(2,1)}, bf16[4,192,96]{2,1,0:T(8,128)(2,1)S(1)}, u32[]{:S(2)}, u32[]{:S(2)}) collective-permute-start(bf16[4,192,96]{2,1,0:T(8,128)(2,1)} %get-tuple-element.244), channel_id=1, source_target_pairs={{0,2},{1,3},{2,4},{3,5},{4,6},{5,7},{6,0},{7,1},{8,10},{9,11},{10,... | collective-permute-start | bytes 442376 | tf_op jit(solution)/shard_map/ppermute | solution.py:1029
  183.6 25.0 %collective-permute-start.38 = (bf16[4,192,96]{2,1,0:T(8,128)(2,1)S(1)}, bf16[4,192,96]{2,1,0:T(8,128)(2,1)S(1)}, u32[]{:S(2)}, u32[]{:S(2)}) collective-permute-start(bf16[4,192,96]{2,1,0:T(8,128)(2,1)S(1)} %get-tuple-element.245), channel_id=1, source_target_pairs={{0,4},{1,5},{2,6},{3,7},{4,0},{5,1},{6,2},{7,3},{8,12},{9,13},{10,... | collective-permute-start | bytes 442376 | tf_op jit(solution)/shard_map/ppermute | solution.py:1029
  188.3 20.3 %collective-permute-start.39 = (bf16[4,192,96]{2,1,0:T(8,128)(2,1)S(1)}, bf16[4,192,96]{2,1,0:T(8,128)(2,1)S(1)}, u32[]{:S(2)}, u32[]{:S(2)}) collective-permute-start(bf16[4,192,96]{2,1,0:T(8,128)(2,1)S(1)} %get-tuple-element.246), channel_id=1, source_target_pairs={{0,6},{1,7},{2,0},{3,1},{4,2},{5,3},{6,4},{7,5},{8,14},{9,15},{10,... | collective-permute-start | bytes 442376 | tf_op jit(solution)/shard_map/ppermute | solution.py:1029
  209.6 12.5 %collective-permute-start.48 = (f32[16,384]{1,0:T(8,128)}, f32[16,384]{1,0:T(8,128)S(1)}, u32[]{:S(2)}, u32[]{:S(2)}) collective-permute-start(f32[16,384]{1,0:T(8,128)} %get-tuple-element.275), channel_id=1, source_target_pairs={{0,1},{1,0},{2,3},{3,2},{4,5},{5,4},{6,7},{7,6},{8,9},{9,8},{10,11... | collective-permute-start | bytes 73736 | tf_op jit(solution)/shard_map/ppermute | solution.py:1022
  209.8 13.2 %collective-permute-start.43 = (bf16[128,768]{1,0:T(8,128)(2,1)}, bf16[128,768]{1,0:T(8,128)(2,1)S(1)}, u32[]{:S(2)}, u32[]{:S(2)}) collective-permute-start(bf16[128,768]{1,0:T(8,128)(2,1)} %get-tuple-element.252), channel_id=1, source_target_pairs={{0,2},{1,3},{2,4},{3,5},{4,6},{5,7},{6,0},{7,1},{8,10},{9,11},{10,... | collective-permute-start | bytes 589832 | tf_op jit(solution)/shard_map/ppermute | solution.py:1029
  223.2 26.4 %collective-permute-start.46 = (bf16[256,768]{1,0:T(8,128)(2,1)S(1)}, bf16[256,768]{1,0:T(8,128)(2,1)S(1)}, u32[]{:S(2)}, u32[]{:S(2)}) collective-permute-start(bf16[256,768]{1,0:T(8,128)(2,1)S(1)} %pad_maximum_fusion.8), channel_id=1, source_target_pairs={{0,6},{1,7},{2,0},{3,1},{4,2},{5,3},{6,4},{7,5},{8,14},{9,15},{10,... | collective-permute-start | bytes 1179656 | tf_op jit(solution)/shard_map/ppermute | solution.py:1029
  224.9 24.7 %collective-permute-start.45 = (bf16[256,768]{1,0:T(8,128)(2,1)S(1)}, bf16[256,768]{1,0:T(8,128)(2,1)S(1)}, u32[]{:S(2)}, u32[]{:S(2)}) collective-permute-start(bf16[256,768]{1,0:T(8,128)(2,1)S(1)} %pad_maximum_fusion.7), channel_id=1, source_target_pairs={{0,2},{1,3},{2,4},{3,5},{4,6},{5,7},{6,0},{7,1},{8,10},{9,11},{10,... | collective-permute-start | bytes 1179656 | tf_op jit(solution)/shard_map/ppermute | solution.py:1029
  227.5 22.1 %collective-permute-start.49 = (bf16[400,384]{1,0:T(8,128)(2,1)S(1)}, bf16[400,384]{1,0:T(8,128)(2,1)S(1)}, u32[]{:S(2)}, u32[]{:S(2)}) collective-permute-start(bf16[400,384]{1,0:T(8,128)(2,1)S(1)} %pad_maximum_fusion.9), channel_id=1, source_target_pairs={{0,16},{8,24},{16,0},{24,8},{1,17},{9,25},{17,1},{25,9},{2,18},{10... | collective-permute-start | bytes 921608 | tf_op jit(solution)/shard_map/ppermute | solution.py:1025
  228.5 48.7 %collective-permute-start.58 = (bf16[2,192,384]{2,1,0:T(8,128)(2,1)S(1)}, bf16[2,192,384]{2,1,0:T(8,128)(2,1)S(1)}, u32[]{:S(2)}, u32[]{:S(2)}) collective-permute-start(bf16[2,192,384]{2,1,0:T(8,128)(2,1)S(1)} %get-tuple-element.304), channel_id=1, source_target_pairs={{0,2},{1,3},{2,4},{3,5},{4,6},{5,7},{6,0},{7,1},{8,10},{9,11},{10,... | collective-permute-start | bytes 884744 | tf_op jit(solution)/shard_map/ppermute | solution.py:1029
  229.0 48.1 %collective-permute-start.59 = (bf16[2,192,384]{2,1,0:T(8,128)(2,1)S(1)}, bf16[2,192,384]{2,1,0:T(8,128)(2,1)S(1)}, u32[]{:S(2)}, u32[]{:S(2)}) collective-permute-start(bf16[2,192,384]{2,1,0:T(8,128)(2,1)S(1)} %get-tuple-element.303), channel_id=1, source_target_pairs={{0,6},{1,7},{2,0},{3,1},{4,2},{5,3},{6,4},{7,5},{8,14},{9,15},{10,... | collective-permute-start | bytes 884744 | tf_op jit(solution)/shard_map/ppermute | solution.py:1029
  261.5 15.6 %collective-permute-start.60 = (bf16[2,192,384]{2,1,0:T(8,128)(2,1)S(1)}, bf16[2,192,384]{2,1,0:T(8,128)(2,1)S(1)}, u32[]{:S(2)}, u32[]{:S(2)}) collective-permute-start(bf16[2,192,384]{2,1,0:T(8,128)(2,1)S(1)} %get-tuple-element.302), channel_id=1, source_target_pairs={{0,4},{1,5},{2,6},{3,7},{4,0},{5,1},{6,2},{7,3},{8,12},{9,13},{10,... | collective-permute-start | bytes 884744 | tf_op jit(solution)/shard_map/ppermute | solution.py:1029
  (76 other events, 448.1 us)
